TPU v7x, 32 devices: a whole 2x2x4 slice. The times are simulated.
32 devices in a mesh: samp: 16 (over z, y, x), feat: 2 (over core).
Axes of the slice: x: 2, y: 2, z: 4, core: 2. Of those that a mesh axis runs over, the one named last changes fastest.
Arguments:
- design_matrix: bfloat16 [2048, 32768], P('samp', 'feat'), may hold values from -0.046875 to 0.046875
- labels: int32 [2048], P('samp'), may hold values from 0 to 1
- weights: float32 [16, 32768], P(None, ('feat', 'samp')), may hold values from -6 to 6
- lambdas: float32 [16], replicated, may hold values from 0.05 to 1
- sketch: bfloat16 [32768, 384], P(('feat', 'samp')), may hold values from -0.03125 to 0.03125
- sketch_values: float32 [384], replicated, may hold values from 0.05 to 2
Outputs:
- new_weights: float32 [16, 32768], P(None, ('feat', 'samp'))
All inputs are finite; a program needn't handle non-finite values.
Results may differ from a plain program's by a relative error of at most 0.004.
Values may be sent and summed in bfloat16 or wider, within the bound.
No kernel may reach another device: no remote copies, remote signals or barrier semaphores. Data moves between devices by JAX's collectives and lax.ppermute only.
A program may use at most 64 MiB of HBM per device.

v0:
```python
import math

import jax
import jax.numpy as jnp
from jax import lax
from jax.experimental import pallas as pl
from jax.experimental.pallas import tpu as pltpu
from jax.sharding import PartitionSpec as P


LANES = 128
SUBLANES = 8
LARGEST = 0.09375
HALF_RANGE = 60000.0


def split(values):
    high = values.astype(jnp.bfloat16)
    rest = values - high.astype(jnp.float32)
    middle = rest.astype(jnp.bfloat16)
    low = (rest - middle.astype(jnp.float32)).astype(jnp.bfloat16)
    return high, middle, low


def exact_dot(values, other, contract):
    rows = values.shape[0]
    product = lax.dot_general(
        jnp.concatenate(split(values), axis=0),
        other,
        (((1,), (contract,)), ((), ())),
        preferred_element_type=jnp.float32,
    )
    return product[:rows] + product[rows : 2 * rows] + product[2 * rows :]


def pack(*columns_in):
    rows = columns_in[0].shape[0]
    lane = lax.broadcasted_iota(jnp.int32, (rows, LANES), 1)
    tile = jnp.zeros((rows, LANES), jnp.float32)
    for place, column in enumerate(columns_in):
        for index, part in enumerate(split(column)):
            tile = jnp.where(lane == 3 * place + index, part.astype(jnp.float32), tile)
    return tile


def unpack(tile, place):
    return jnp.sum(tile[:, 3 * place : 3 * place + 3], axis=1, keepdims=True)


def repeat(out_ref, block):
    for part in range(out_ref.shape[0]):
        out_ref[part] = block


def load_body(offsets_ref, design_ref, out_ref, sems):
    parts = offsets_ref.shape[0]
    width = design_ref.shape[1] // parts
    copies = []
    for part in range(parts):
        offset = pl.multiple_of(offsets_ref[part], width)
        copies.append(
            pltpu.make_async_copy(
                design_ref.at[:, pl.ds(offset, width)],
                out_ref.at[:, pl.ds(part * width, width)],
                sems.at[part],
            )
        )
    for copy in copies:
        copy.start()
    for copy in copies:
        copy.wait()


def design_part(design_ref, place, width):
    return design_ref[:, place * width : (place + 1) * width]


def rows_body(places, again, *refs):
    *field_refs, design_ref, base_ref, out_ref = refs
    samples = design_ref.shape[0]
    blocks = []
    for field_ref in field_refs:
        if len(field_ref.shape) == 2:
            blocks.append(field_ref[...])
        else:
            blocks.extend(field_ref[row] for row in range(field_ref.shape[0]))
    strengths, width = blocks[0].shape
    total = jnp.zeros((strengths, samples), jnp.float32)
    squares = jnp.zeros((strengths, width), jnp.float32)
    products = jnp.zeros((strengths, width), jnp.float32)
    for index, place in enumerate(places):
        total += lax.dot_general(
            blocks[index],
            design_part(design_ref, place, width),
            (((1,), (1,)), ((), ())),
            preferred_element_type=jnp.float32,
        )
        values = blocks[index].astype(jnp.float32)
        squares += values * values
        if again:
            products += values * blocks[len(places) + index].astype(jnp.float32)
    square = jnp.sum(squares, axis=1, keepdims=True)
    sums = [square, jnp.sum(products, axis=1, keepdims=True)] if again else [square]
    base = base_ref[...]
    if base.shape[1] > LANES:
        out_ref[:, :samples] = base[:, :samples] + total
        out_ref[:, samples:] = base[:, samples:] + tile_of(*sums)
    else:
        out_ref[:, :samples] = total
        out_ref[:, samples:] = base + tile_of(*sums)


def columns(values, design_ref, places, out_refs, scale=None):
    targets = []
    for out_ref in out_refs:
        if len(out_ref.shape) == 2:
            targets.append((out_ref, ...))
        else:
            targets.extend((out_ref, row) for row in range(out_ref.shape[0]))
    for place, (out_ref, row) in zip(places, targets):
        block = lax.dot_general(
            values,
            design_part(design_ref, place, out_ref.shape[-1]),
            (((1,), (0,)), ((), ())),
            preferred_element_type=jnp.float32,
        )
        if scale is not None:
            block = block * scale
        out_ref[row] = block.astype(out_ref.dtype)


def miss_body(scale, places, both_ref, other_ref, labels_ref, design_ref, hessian_ref, miss_ref, *out_refs):
    samples = design_ref.shape[0]
    logits = both_ref[:, :samples] + other_ref[:, :samples]
    probability = 1.0 / (1.0 + jnp.exp(-logits))
    hessian_ref[...] = probability * (1.0 - probability)
    miss_rows = (probability - labels_ref[...].astype(jnp.float32)).astype(jnp.bfloat16)
    miss_ref[...] = miss_rows
    columns(miss_rows, design_ref, places, out_refs, scale)


def more_body(scale, places, values_ref, design_ref, *out_refs):
    columns(values_ref[...], design_ref, places, out_refs, scale)


def tile_of(*columns_in):
    rows = columns_in[0].shape[0]
    lane = lax.broadcasted_iota(jnp.int32, (rows, LANES), 1)
    tile = jnp.zeros((rows, LANES), jnp.float32)
    for place, column in enumerate(columns_in):
        tile = jnp.where(lane == place, column, tile)
    return tile


def dot_of(first, second):
    return jnp.sum(first * second, axis=1, keepdims=True)


def ratios_of(lam_ref, values_ref):
    lam = lam_ref[:, :1]
    values = values_ref[...]
    smallest = jnp.min(values, axis=1, keepdims=True)
    return (smallest + lam) / (values + lam) - 1.0


def gradient_body(summed_ref, weights_ref, lam_ref, sketch_ref, residual_ref, payload_ref):
    residual = -(summed_ref[...] + lam_ref[:, :1] * weights_ref[...])
    residual_ref[...] = residual
    repeat(payload_ref, exact_dot(residual, sketch_ref[...], 0).astype(jnp.bfloat16))


def first_body(
    summed_ref, other_ref, lam_ref, values_ref, sketch_ref, residual_ref,
    direction_ref, projected_ref, half_ref,
):
    projected = summed_ref[...] + other_ref[...]
    projected_ref[...] = projected
    scaled = ratios_of(lam_ref, values_ref) * projected
    direction = residual_ref[...] + exact_dot(scaled, sketch_ref[...], 1)
    direction_ref[...] = direction
    half_ref[...] = direction.astype(jnp.bfloat16)


def image_of(image_rows, hessian_ref):
    return (hessian_ref[...] * image_rows).astype(jnp.bfloat16)


def image_body(
    places, both_ref, other_ref, hessian_ref, design_ref, rows_ref, image_ref, scalars_ref, *out_refs
):
    samples = hessian_ref.shape[1]
    both = both_ref[...] + other_ref[...]
    image_rows = both[:, :samples]
    rows_ref[...] = image_rows
    image = image_of(image_rows, hessian_ref)
    image_ref[...] = image
    scalars_ref[...] = tile_of(
        both[:, samples : samples + 1], dot_of(image.astype(jnp.float32), image_rows)
    )
    columns(image, design_ref, places, out_refs)


def fold_body(own_ref, *refs):
    count = own_ref.shape[0]
    received_refs, target_refs = refs[:-count], refs[-count:]
    for row, target_ref in enumerate(target_refs):
        total = own_ref[row]
        for received_ref in received_refs:
            total += received_ref[row].astype(jnp.float32)
        target_ref[...] = total.astype(target_ref.dtype)


def image_project_body(count, own_ref, *refs):
    received_refs = refs[:count]
    scalars_ref, lam_ref, direction_ref, residual_ref, sketch_ref, applied_ref, payload_ref = refs[count:]
    rank = sketch_ref.shape[1]
    summed = own_ref[...]
    for received_ref in received_refs:
        summed += received_ref[...].astype(jnp.float32)
    applied = summed + lam_ref[:, :1] * direction_ref[...]
    applied_ref[...] = applied
    projected = exact_dot(applied, sketch_ref[...], 0).astype(jnp.bfloat16)
    residual = residual_ref[...]
    packed = pack(scalars_ref[:, 1:2], dot_of(residual, residual)).astype(jnp.bfloat16)
    for part in range(payload_ref.shape[0]):
        payload_ref[part, :, :rank] = projected
        payload_ref[part, :, rank:] = packed


def second_body(
    summed_ref, other_ref, lam_ref, values_ref, sketch_ref, scalars_ref, projected_ref,
    weights_ref, direction_ref, residual_ref, applied_ref,
    precond_ref, update_ref, known_ref, extra_ref, half_ref,
):
    rank = sketch_ref.shape[1]
    lam = lam_ref[:, :1]
    ratios = ratios_of(lam_ref, values_ref)
    projected = projected_ref[...]
    square = unpack(summed_ref[:, rank:] + other_ref[:, rank:], 1)
    energy = unpack(summed_ref[:, rank:], 0)
    res_dot = square + dot_of(ratios * projected, projected)
    step_size = res_dot / (energy + lam * scalars_ref[:, :1])
    residual = residual_ref[...] - step_size * applied_ref[...]
    projected = projected - step_size * (summed_ref[:, :rank] + other_ref[:, :rank])
    scaled = ratios * projected
    precond_res = residual + exact_dot(scaled, sketch_ref[...], 1)
    precond_ref[...] = precond_res
    half_ref[...] = precond_res.astype(jnp.bfloat16)
    update_ref[...] = weights_ref[...] + step_size * direction_ref[...]
    known_ref[...] = tile_of(res_dot, dot_of(scaled, projected), energy, scalars_ref[:, :1])
    zero = jnp.zeros_like(square)
    extra_ref[...] = tile_of(zero, zero, dot_of(residual, residual))


def energy_body(both_ref, other_ref, hessian_ref, rows_ref, squares_ref, payload_ref):
    samples = hessian_ref.shape[1]
    both = both_ref[...] + other_ref[...]
    squares_ref[...] = both[:, samples:]
    image_rows = both[:, :samples]
    image = image_of(image_rows, hessian_ref).astype(jnp.float32)
    sums = [dot_of(image, image_rows), dot_of(image, rows_ref[...]), both[:, samples + 2 : samples + 3]]
    lane = lax.broadcasted_iota(jnp.int32, (SUBLANES, LANES), 1)
    tile = jnp.zeros((SUBLANES, LANES), jnp.float32)
    for group in range(both.shape[0] // SUBLANES):
        for place, column in enumerate(sums):
            piece = column[group * SUBLANES : (group + 1) * SUBLANES]
            tile = jnp.where(lane == len(sums) * group + place, piece, tile)
    repeat(payload_ref, tile)


def finish_body(
    received_ref, squares_ref, known_ref, lam_ref, precond_ref, direction_ref, update_ref, out_ref
):
    tile = received_ref[0]
    for part in range(1, received_ref.shape[0]):
        tile += received_ref[part]
    groups = direction_ref.shape[0] // SUBLANES

    def total(place):
        lanes = [3 * group + place for group in range(groups)]
        return jnp.concatenate([tile[:, lane : lane + 1] for lane in lanes], axis=0)

    old_dot, part, old_energy, old_square = (known_ref[:, lane : lane + 1] for lane in range(4))
    res_dot = total(2) + part
    beta = res_dot / old_dot
    energy = total(0) + beta * (2.0 * total(1) + beta * old_energy)
    square = squares_ref[:, :1] + beta * (2.0 * squares_ref[:, 1:2] + beta * old_square)
    step_size = res_dot / (energy + lam_ref[:, :1] * square)
    direction = precond_ref[...] + beta * direction_ref[...]
    out_ref[...] = update_ref[...] + step_size * direction


VMEM = pl.BlockSpec(memory_space=pltpu.VMEM)


def call(body, shapes, *operands):
    return pl.pallas_call(
        body,
        out_shape=[jax.ShapeDtypeStruct(shape, dtype) for shape, dtype in shapes],
        in_specs=[VMEM] * len(operands),
        out_specs=[VMEM] * len(shapes),
        compiler_params=pltpu.CompilerParams(vmem_limit_bytes=8 << 20),
    )(*operands)


def load(design, offsets):
    return pl.pallas_call(
        load_body,
        out_shape=pltpu.VMEM(design.shape, design.dtype),
        in_specs=[pl.BlockSpec(memory_space=pltpu.SMEM), pl.BlockSpec(memory_space=pltpu.HBM)],
        out_specs=VMEM,
        scratch_shapes=[pltpu.SemaphoreType.DMA((offsets.shape[0],))],
        compiler_params=pltpu.CompilerParams(vmem_limit_bytes=1 << 20),
        name="load",
    )(offsets, design)


def make_shards(samp, feat):
    near = min(samp, 4)
    far = samp // near
    near_order = list(range(1, near))
    far_order = sorted(range(1, far), key=lambda distance: (distance * 2) % (far + 1))

    def swap(values, distance):
        return lax.ppermute(values, "samp", [(i, i ^ distance) for i in range(samp)])

    def swap_far(values):
        received = []
        for value, distance in zip(values, far_order):
            received.append(swap(value, near * distance))
        return received

    def swap_near(values):
        return [swap(value, distance) for value, distance in zip(values, near_order)]

    def gather(block):
        column = jnp.stack([block] + swap_far([block] * len(far_order)))
        return [column], swap_near([column] * len(near_order))

    def exchange(blocks):
        return lax.all_to_all(blocks, "samp", 0, 0)

    def feat_parts(values):
        if feat == 2:
            return values, lax.ppermute(values, "feat", [(0, 1), (1, 0)])
        return lax.psum(values, "feat"), jnp.zeros_like(values)

    def shards(design_matrix, labels, weights, lambdas, sketch, sketch_values):
        strengths, width = weights.shape
        samples = design_matrix.shape[0]
        rank = sketch.shape[1]
        single, half = jnp.float32, jnp.bfloat16
        field = ((strengths, width), single)
        scalars = ((strengths, LANES), single)
        spread = ((strengths, width), half)
        payload = ((samp, strengths, rank), half)
        wide_payload = ((samp, strengths, rank + LANES), half)
        scale = 2.0 ** math.floor(math.log2(HALF_RANGE / (samples * near * LARGEST)))
        lam = jnp.broadcast_to(lambdas[:, None], (strengths, LANES))
        labels = labels[None, :]
        values = sketch_values[None, :]
        places = [k * near + j for j in [0] + near_order for k in [0] + far_order]
        places = jnp.bitwise_xor(lax.axis_index("samp"), jnp.array(places, jnp.int32))
        if width % LANES == 0:
            design = load(design_matrix, places * width)
        else:
            design = design_matrix.reshape(samples, samp, width)
            design = jnp.take(design, places, axis=1).reshape(design_matrix.shape)

        column_places = list(range(far))
        plane_places = list(range(far, samp))

        def apply_rows(fields, earlier, base):
            both = base
            for places, blocks, old in zip((column_places, plane_places), fields, earlier):
                both = call(
                    lambda *refs: rows_body(places, len(old) > 0, *refs),
                    [((strengths, samples + LANES), single)], *blocks, *old, design, both,
                )[0]
            return feat_parts(both)

        def reduced(blocks):
            return feat_parts(jnp.sum(exchange(blocks).astype(single), axis=0))

        nothing = jnp.zeros((strengths, LANES), single)
        start = lax.optimization_barrier(weights.astype(half))
        sample_field = (strengths, samples)
        column = (far, strengths, width)
        hessian_diag, miss_rows, *outs = call(
            lambda *refs: miss_body(scale, plane_places, *refs),
            [(sample_field, single), (sample_field, half)] + [(column, single)] * (near - 1),
            *apply_rows(gather(start), ([], []), nothing), labels, design,
        )
        folded = call(
            lambda *refs: more_body(scale, column_places, *refs),
            [(column, single)], miss_rows, design,
        )[0]
        for received in swap_near([out.astype(jnp.float16) for out in outs]):
            folded = folded + received.astype(single)
        summed = folded[0]
        for received in swap_far([folded[k].astype(jnp.float16) for k in range(1, far)]):
            summed = summed + received.astype(single)
        residual, blocks = call(
            gradient_body, [field, payload], summed * (1.0 / scale), weights, lam, sketch
        )
        direction, projected, block = call(
            first_body, [field, ((strengths, rank), single), spread],
            *reduced(blocks), lam, values, sketch, residual,
        )
        whole = gather(block)
        image_rows, image, known, *outs = call(
            lambda *refs: image_body(plane_places, *refs),
            [(sample_field, single), (sample_field, half), scalars] + [(column, half)] * (near - 1),
            *apply_rows(whole, ([], []), nothing), hessian_diag, design,
        )
        own = call(
            lambda *refs: more_body(None, column_places, *refs),
            [(column, single)], image, design,
        )[0]
        kept, *sent = call(fold_body, [field] + [spread] * (far - 1), own, *swap_near(outs))
        applied, blocks = call(
            lambda *refs: image_project_body(far - 1, *refs), [field, wide_payload],
            kept, *swap_far(sent), known, lam, direction, residual, sketch,
        )
        precond_res, update, known, extra, block = call(
            second_body, [field, field, scalars, scalars, spread],
            *reduced(blocks), lam, values, sketch, known, projected,
            weights, direction, residual, applied,
        )
        squares, blocks = call(
            energy_body, [scalars, ((samp, SUBLANES, LANES), single)],
            *apply_rows(gather(block), whole, extra), hessian_diag, image_rows,
        )
        return call(
            finish_body, [field],
            exchange(blocks), squares, known, lam, precond_res, direction, update,
        )[0]

    return shards


def solution(mesh):
    return jax.shard_map(
        make_shards(mesh.shape["samp"], mesh.shape["feat"]),
        mesh=mesh,
        in_specs=(
            P("samp", "feat"),
            P("samp"),
            P(None, ("feat", "samp")),
            P(),
            P(("feat", "samp"), None),
            P(),
        ),
        out_specs=P(None, ("feat", "samp")),
        check_vma=False,
    )
```

profile of v0, /device:TPU:0, one launch (start us, length us, event | category | flops | bytes accessed | tf_op | source)
XLA Modules:
  0.0 134.1 jit_solution(4909945394909832901)
XLA Ops:
  0.8 4.1 %collective-permute-start.2 = (bf16[16,1024]{1,0:T(8,128)(2,1)S(1)}, bf16[16,1024]{1,0:T(8,128)(2,1)S(1)}, u32[]{:S(2)}, u32[]{:S(2)}) collective-permute-start(bf16[16,1024]{1,0:T(8,128)(2,1)S(1)} %convert_element_type.48), channel_id=1, source_target_pairs={{0,16},{2,18},{4,20},{6,22},{8,24},{10,26},{12,28},{14,30},{16,0},... | collective-permute-start | bytes 98312 | tf_op jit(solution)/shard_map/ppermute | solution.py:325
  4.9 1.6 %collective-permute-start.1 = (bf16[16,1024]{1,0:T(8,128)(2,1)S(1)}, bf16[16,1024]{1,0:T(8,128)(2,1)S(1)}, u32[]{:S(2)}, u32[]{:S(2)}) collective-permute-start(bf16[16,1024]{1,0:T(8,128)(2,1)S(1)} %convert_element_type.48), channel_id=1, source_target_pairs={{0,8},{2,10},{4,12},{6,14},{8,0},{10,2},{12,4},{14,6},{16,24},{18,... | collective-permute-start | bytes 98312 | tf_op jit(solution)/shard_map/ppermute | solution.py:325
  7.3 1.6 %collective-permute-done.1 = bf16[16,1024]{1,0:T(8,128)(2,1)S(1)} collective-permute-done((bf16[16,1024]{1,0:T(8,128)(2,1)S(1)}, bf16[16,1024]{1,0:T(8,128)(2,1)S(1)}, u32[]{:S(2)}, u32[]{:S(2)}) %collective-permute-start.1) | collective-permute-done | bytes 32800 | tf_op jit(solution)/shard_map/ppermute | solution.py:325
  8.8 3.4 %collective-permute-done = bf16[16,1024]{1,0:T(8,128)(2,1)S(1)} collective-permute-done((bf16[16,1024]{1,0:T(8,128)(2,1)S(1)}, bf16[16,1024]{1,0:T(8,128)(2,1)S(1)}, u32[]{:S(2)}, u32[]{:S(2)}) %collective-permute-start) | collective-permute-done | bytes 32800 | tf_op jit(solution)/shard_map/ppermute | solution.py:325
  12.2 2.5 %collective-permute-start.5 = (bf16[4,16,1024]{2,1,0:T(8,128)(2,1)S(1)}, bf16[4,16,1024]{2,1,0:T(8,128)(2,1)S(1)}, u32[]{:S(2)}, u32[]{:S(2)}) collective-permute-start(bf16[4,16,1024]{2,1,0:T(8,128)(2,1)S(1)} %pad_maximum_fusion.refs_0_), channel_id=1, source_target_pairs={{0,6},{2,4},{4,2},{6,0},{8,14},{10,12},{12,10},{14,8},{16,22},{18,... | collective-permute-start | bytes 393224 | tf_op jit(solution)/shard_map/ppermute | solution.py:325
  16.4 2.2 %copy-done.1 = bf16[128,16384]{1,0:T(8,128)(2,1)S(1)} copy-done((bf16[128,16384]{1,0:T(8,128)(2,1)S(1)}, bf16[128,16384]{1,0:T(8,128)(2,1)}, u32[]{:S(2)}) %copy-start.1) | copy-done | bytes 4194328
  18.6 1.0 load.1.refs_1_.refs_3_.refs_2_.refs_6_
  20.3 0.9 shard_map.74.refs_0_
  21.3 1.2 collective-permute-done.6.refs_1_
  23.1 2.3 %collective-permute-start.9 = (f16[4,16,1024]{2,1,0:T(8,128)(2,1)S(1)}, f16[4,16,1024]{2,1,0:T(8,128)(2,1)S(1)}, u32[]{:S(2)}, u32[]{:S(2)}) collective-permute-start(f16[4,16,1024]{2,1,0:T(8,128)(2,1)S(1)} %convert_element_type.53), channel_id=1, source_target_pairs={{0,6},{2,4},{4,2},{6,0},{8,14},{10,12},{12,10},{14,8},{16,22},{18,... | collective-permute-start | bytes 393224 | tf_op jit(solution)/shard_map/ppermute | solution.py:325
  26.9 3.3 %collective-permute-done.9 = f16[4,16,1024]{2,1,0:T(8,128)(2,1)S(1)} collective-permute-done((f16[4,16,1024]{2,1,0:T(8,128)(2,1)S(1)}, f16[4,16,1024]{2,1,0:T(8,128)(2,1)S(1)}, u32[]{:S(2)}, u32[]{:S(2)}) %collective-permute-start.9) | collective-permute-done | bytes 131104 | tf_op jit(solution)/shard_map/ppermute | solution.py:325
  30.2 2.2 %collective-permute-done.8 = f16[4,16,1024]{2,1,0:T(8,128)(2,1)S(1)} collective-permute-done((f16[4,16,1024]{2,1,0:T(8,128)(2,1)S(1)}, f16[4,16,1024]{2,1,0:T(8,128)(2,1)S(1)}, u32[]{:S(2)}, u32[]{:S(2)}) %collective-permute-start.8) | collective-permute-done | bytes 131104 | tf_op jit(solution)/shard_map/ppermute | solution.py:325
  33.1 4.0 %collective-permute-start.11 = (f16[16,1024]{1,0:T(8,128)(2,1)S(1)}, f16[16,1024]{1,0:T(8,128)(2,1)S(1)}, u32[]{:S(2)}, u32[]{:S(2)}) collective-permute-start(f16[16,1024]{1,0:T(8,128)(2,1)S(1)} %get-tuple-element.67), channel_id=1, source_target_pairs={{0,8},{2,10},{4,12},{6,14},{8,0},{10,2},{12,4},{14,6},{16,24},{18,... | collective-permute-start | bytes 98312 | tf_op jit(solution)/shard_map/ppermute | solution.py:325
  37.0 1.4 %collective-permute-done.10 = f16[16,1024]{1,0:T(8,128)(2,1)S(1)} collective-permute-done((f16[16,1024]{1,0:T(8,128)(2,1)S(1)}, f16[16,1024]{1,0:T(8,128)(2,1)S(1)}, u32[]{:S(2)}, u32[]{:S(2)}) %collective-permute-start.10) | collective-permute-done | bytes 32800 | tf_op jit(solution)/shard_map/ppermute | solution.py:325
  39.3 12.8 %all_to_all.15 = bf16[16,16,384]{2,1,0:T(8,128)(2,1)S(1)} all-to-all(bf16[16,16,384]{2,1,0:T(8,128)(2,1)S(1)} %get-tuple-element.38), channel_id=1, replica_groups=mesh['samp'=16,'feat'=2] {'samp'}, dimensions={0} | all-to-all | bytes 393216 | tf_op jit(solution)/shard_map/all_to_all | solution.py:341
  52.3 1.2 collective-permute-done.13.other_ref
  53.9 1.1 collective-permute-start.16
  55.0 1.1 collective-permute-start.15
  56.0 2.2 %collective-permute-start.14 = (bf16[16,1024]{1,0:T(8,128)(2,1)S(1)}, bf16[16,1024]{1,0:T(8,128)(2,1)S(1)}, u32[]{:S(2)}, u32[]{:S(2)}) collective-permute-start(bf16[16,1024]{1,0:T(8,128)(2,1)S(1)} %get-tuple-element.40), channel_id=1, source_target_pairs={{0,24},{2,26},{4,28},{6,30},{8,16},{10,18},{12,20},{14,22},{16,8},... | collective-permute-start | bytes 98312 | tf_op jit(solution)/shard_map/ppermute | solution.py:325
  59.1 2.6 %collective-permute-done.14 = bf16[16,1024]{1,0:T(8,128)(2,1)S(1)} collective-permute-done((bf16[16,1024]{1,0:T(8,128)(2,1)S(1)}, bf16[16,1024]{1,0:T(8,128)(2,1)S(1)}, u32[]{:S(2)}, u32[]{:S(2)}) %collective-permute-start.14) | collective-permute-done | bytes 32800 | tf_op jit(solution)/shard_map/ppermute | solution.py:325
  62.5 1.3 collective-permute-start.18
  63.9 1.5 %collective-permute-start.17 = (bf16[4,16,1024]{2,1,0:T(8,128)(2,1)S(1)}, bf16[4,16,1024]{2,1,0:T(8,128)(2,1)S(1)}, u32[]{:S(2)}, u32[]{:S(2)}) collective-permute-start(bf16[4,16,1024]{2,1,0:T(8,128)(2,1)S(1)} %pad_maximum_fusion.1.refs_0_.refs_1_), channel_id=1, source_target_pairs={{0,2},{2,0},{4,6},{6,4},{8,10},{10,8},{12,14},{14,12},{16,18},{18,... | collective-permute-start | bytes 393224 | tf_op jit(solution)/shard_map/ppermute | solution.py:325
  65.7 2.7 %collective-permute-done.19.refs_2_.refs_5_ = bf16[4,16,1024]{2,1,0:T(8,128)(2,1)S(1)} collective-permute-done((bf16[4,16,1024]{2,1,0:T(8,128)(2,1)S(1)}, bf16[4,16,1024]{2,1,0:T(8,128)(2,1)S(1)}, u32[]{:S(2)}, u32[]{:S(2)}) %collective-permute-start.19) | collective-permute-done | bytes 131104 | tf_op jit(solution)/shard_map/ppermute | solution.py:325
  68.4 0.9 collective-permute-done.18.refs_1_.refs_4_
  69.3 0.9 shard_map.80.refs_0_
  70.2 1.2 collective-permute-done.20.refs_1_
  71.9 1.1 collective-permute-start.21
  73.8 1.6 %collective-permute-start.23 = (bf16[4,16,1024]{2,1,0:T(8,128)(2,1)S(1)}, bf16[4,16,1024]{2,1,0:T(8,128)(2,1)S(1)}, u32[]{:S(2)}, u32[]{:S(2)}) collective-permute-start(bf16[4,16,1024]{2,1,0:T(8,128)(2,1)S(1)} %get-tuple-element.45), channel_id=1, source_target_pairs={{0,6},{2,4},{4,2},{6,0},{8,14},{10,12},{12,10},{14,8},{16,22},{18,... | collective-permute-start | bytes 393224 | tf_op jit(solution)/shard_map/ppermute | solution.py:325
  75.7 2.6 %collective-permute-done.21.refs_0_ = bf16[4,16,1024]{2,1,0:T(8,128)(2,1)S(1)} collective-permute-done((bf16[4,16,1024]{2,1,0:T(8,128)(2,1)S(1)}, bf16[4,16,1024]{2,1,0:T(8,128)(2,1)S(1)}, u32[]{:S(2)}, u32[]{:S(2)}) %collective-permute-start.21) | collective-permute-done | bytes 131104 | tf_op jit(solution)/shard_map/ppermute | solution.py:325
  78.3 2.8 %collective-permute-done.22.refs_1_ = bf16[4,16,1024]{2,1,0:T(8,128)(2,1)S(1)} collective-permute-done((bf16[4,16,1024]{2,1,0:T(8,128)(2,1)S(1)}, bf16[4,16,1024]{2,1,0:T(8,128)(2,1)S(1)}, u32[]{:S(2)}, u32[]{:S(2)}) %collective-permute-start.22) | collective-permute-done | bytes 131104 | tf_op jit(solution)/shard_map/ppermute | solution.py:325
  81.2 2.6 %collective-permute-start.24 = (bf16[16,1024]{1,0:T(8,128)(2,1)S(1)}, bf16[16,1024]{1,0:T(8,128)(2,1)S(1)}, u32[]{:S(2)}, u32[]{:S(2)}) collective-permute-start(bf16[16,1024]{1,0:T(8,128)(2,1)S(1)} %get-tuple-element.47), channel_id=1, source_target_pairs={{0,24},{2,26},{4,28},{6,30},{8,16},{10,18},{12,20},{14,22},{16,8},... | collective-permute-start | bytes 98312 | tf_op jit(solution)/shard_map/ppermute | solution.py:325
  83.8 1.9 %collective-permute-start.26 = (bf16[16,1024]{1,0:T(8,128)(2,1)S(1)}, bf16[16,1024]{1,0:T(8,128)(2,1)S(1)}, u32[]{:S(2)}, u32[]{:S(2)}) collective-permute-start(bf16[16,1024]{1,0:T(8,128)(2,1)S(1)} %get-tuple-element.49), channel_id=1, source_target_pairs={{0,16},{2,18},{4,20},{6,22},{8,24},{10,26},{12,28},{14,30},{16,0},... | collective-permute-start | bytes 98312 | tf_op jit(solution)/shard_map/ppermute | solution.py:325
  85.6 1.3 collective-permute-done.24.refs_1_
  87.7 0.9 collective-permute-done.26.refs_3_
  88.9 12.5 %all_to_all.16 = bf16[16,16,512]{2,1,0:T(8,128)(2,1)S(1)} all-to-all(bf16[16,16,512]{2,1,0:T(8,128)(2,1)S(1)} %get-tuple-element.52), channel_id=1, replica_groups=mesh['samp'=16,'feat'=2] {'samp'}, dimensions={0} | all-to-all | bytes 524288 | tf_op jit(solution)/shard_map/all_to_all | solution.py:341
  101.5 1.2 collective-permute-done.27.other_ref
  103.3 1.1 collective-permute-start.30
  104.4 1.3 collective-permute-start.29
  105.7 2.0 %collective-permute-start.28 = (bf16[16,1024]{1,0:T(8,128)(2,1)S(1)}, bf16[16,1024]{1,0:T(8,128)(2,1)S(1)}, u32[]{:S(2)}, u32[]{:S(2)}) collective-permute-start(bf16[16,1024]{1,0:T(8,128)(2,1)S(1)} %get-tuple-element.55), channel_id=1, source_target_pairs={{0,24},{2,26},{4,28},{6,30},{8,16},{10,18},{12,20},{14,22},{16,8},... | collective-permute-start | bytes 98312 | tf_op jit(solution)/shard_map/ppermute | solution.py:325
  107.7 1.0 collective-permute-done.30
  108.7 2.7 %collective-permute-done.28 = bf16[16,1024]{1,0:T(8,128)(2,1)S(1)} collective-permute-done((bf16[16,1024]{1,0:T(8,128)(2,1)S(1)}, bf16[16,1024]{1,0:T(8,128)(2,1)S(1)}, u32[]{:S(2)}, u32[]{:S(2)}) %collective-permute-start.28) | collective-permute-done | bytes 32800 | tf_op jit(solution)/shard_map/ppermute | solution.py:325
  112.2 1.3 collective-permute-start.32
  113.5 1.5 %collective-permute-start.31 = (bf16[4,16,1024]{2,1,0:T(8,128)(2,1)S(1)}, bf16[4,16,1024]{2,1,0:T(8,128)(2,1)S(1)}, u32[]{:S(2)}, u32[]{:S(2)}) collective-permute-start(bf16[4,16,1024]{2,1,0:T(8,128)(2,1)S(1)} %pad_maximum_fusion.2.refs_0_), channel_id=1, source_target_pairs={{0,2},{2,0},{4,6},{6,4},{8,10},{10,8},{12,14},{14,12},{16,18},{18,... | collective-permute-start | bytes 393224 | tf_op jit(solution)/shard_map/ppermute | solution.py:325
  115.3 2.5 %collective-permute-done.33.refs_2_ = bf16[4,16,1024]{2,1,0:T(8,128)(2,1)S(1)} collective-permute-done((bf16[4,16,1024]{2,1,0:T(8,128)(2,1)S(1)}, bf16[4,16,1024]{2,1,0:T(8,128)(2,1)S(1)}, u32[]{:S(2)}, u32[]{:S(2)}) %collective-permute-start.33) | collective-permute-done | bytes 131104 | tf_op jit(solution)/shard_map/ppermute | solution.py:325
  118.7 1.0 shard_map.87.both_ref
  119.7 1.2 collective-permute-done.34.other_ref
  121.0 12.0 %all_to_all.17.received_ref = f32[16,8,128]{2,1,0:T(8,128)S(1)} all-to-all(f32[16,8,128]{2,1,0:T(8,128)S(1)} %get-tuple-element.58), channel_id=1, replica_groups=mesh['samp'=16,'feat'=2] {'samp'}, dimensions={0} | all-to-all | bytes 131072 | tf_op jit(solution)/shard_map/all_to_all | solution.py:341
  133.0 1.1 shard_map.89
  (71 shorter events, 15.8 us)
Async XLA Ops:
  0.8 6.4 %collective-permute-start.2 = (bf16[16,1024]{1,0:T(8,128)(2,1)S(1)}, bf16[16,1024]{1,0:T(8,128)(2,1)S(1)}, u32[]{:S(2)}, u32[]{:S(2)}) collective-permute-start(bf16[16,1024]{1,0:T(8,128)(2,1)S(1)} %convert_element_type.48), channel_id=1, source_target_pairs={{0,16},{2,18},{4,20},{6,22},{8,24},{10,26},{12,28},{14,30},{16,0},... | collective-permute-start | bytes 98312 | tf_op jit(solution)/shard_map/ppermute | solution.py:325
  4.9 3.9 %collective-permute-start.1 = (bf16[16,1024]{1,0:T(8,128)(2,1)S(1)}, bf16[16,1024]{1,0:T(8,128)(2,1)S(1)}, u32[]{:S(2)}, u32[]{:S(2)}) collective-permute-start(bf16[16,1024]{1,0:T(8,128)(2,1)S(1)} %convert_element_type.48), channel_id=1, source_target_pairs={{0,8},{2,10},{4,12},{6,14},{8,0},{10,2},{12,4},{14,6},{16,24},{18,... | collective-permute-start | bytes 98312 | tf_op jit(solution)/shard_map/ppermute | solution.py:325
  6.5 5.7 %collective-permute-start = (bf16[16,1024]{1,0:T(8,128)(2,1)S(1)}, bf16[16,1024]{1,0:T(8,128)(2,1)S(1)}, u32[]{:S(2)}, u32[]{:S(2)}) collective-permute-start(bf16[16,1024]{1,0:T(8,128)(2,1)S(1)} %convert_element_type.48), channel_id=1, source_target_pairs={{0,24},{2,26},{4,28},{6,30},{8,16},{10,18},{12,20},{14,22},{16,8},... | collective-permute-start | bytes 98312 | tf_op jit(solution)/shard_map/ppermute | solution.py:325
  12.2 7.8 %collective-permute-start.5 = (bf16[4,16,1024]{2,1,0:T(8,128)(2,1)S(1)}, bf16[4,16,1024]{2,1,0:T(8,128)(2,1)S(1)}, u32[]{:S(2)}, u32[]{:S(2)}) collective-permute-start(bf16[4,16,1024]{2,1,0:T(8,128)(2,1)S(1)} %pad_maximum_fusion.refs_0_), channel_id=1, source_target_pairs={{0,6},{2,4},{4,2},{6,0},{8,14},{10,12},{12,10},{14,8},{16,22},{18,... | collective-permute-start | bytes 393224 | tf_op jit(solution)/shard_map/ppermute | solution.py:325
  14.7 5.6 %collective-permute-start.4 = (bf16[4,16,1024]{2,1,0:T(8,128)(2,1)S(1)}, bf16[4,16,1024]{2,1,0:T(8,128)(2,1)S(1)}, u32[]{:S(2)}, u32[]{:S(2)}) collective-permute-start(bf16[4,16,1024]{2,1,0:T(8,128)(2,1)S(1)} %pad_maximum_fusion.refs_0_), channel_id=1, source_target_pairs={{0,4},{2,6},{4,0},{6,2},{8,12},{10,14},{12,8},{14,10},{16,20},{18,... | collective-permute-start | bytes 393224 | tf_op jit(solution)/shard_map/ppermute | solution.py:325
  15.2 5.1 %collective-permute-start.3 = (bf16[4,16,1024]{2,1,0:T(8,128)(2,1)S(1)}, bf16[4,16,1024]{2,1,0:T(8,128)(2,1)S(1)}, u32[]{:S(2)}, u32[]{:S(2)}) collective-permute-start(bf16[4,16,1024]{2,1,0:T(8,128)(2,1)S(1)} %pad_maximum_fusion.refs_0_), channel_id=1, source_target_pairs={{0,2},{2,0},{4,6},{6,4},{8,10},{10,8},{12,14},{14,12},{16,18},{18,... | collective-permute-start | bytes 393224 | tf_op jit(solution)/shard_map/ppermute | solution.py:325
  16.4 2.2 %copy-start.1 = (bf16[128,16384]{1,0:T(8,128)(2,1)S(1)}, bf16[128,16384]{1,0:T(8,128)(2,1)}, u32[]{:S(2)}) copy-start(bf16[128,16384]{1,0:T(8,128)(2,1)} %design_ref.1) | copy-start | bytes 12582916
  19.7 2.8 %copy-start.3 = (s32[128]{0:T(128)S(1)}, s32[128]{0:T(128)}, u32[]{:S(2)}) copy-start(s32[128]{0:T(128)} %param.8) | copy-start | bytes 1540
  21.3 1.2 collective-permute-start.6
  23.0 15.9 %copy-start.5 = (f32[16]{0:T(128)S(1)}, f32[16]{0:T(128)}, u32[]{:S(2)}) copy-start(f32[16]{0:T(128)} %param.10) | copy-start | bytes 196
  23.0 16.0 %copy-start = (bf16[1024,384]{1,0:T(8,128)(2,1)S(1)}, bf16[1024,384]{1,0:T(8,128)(2,1)}, u32[]{:S(2)}) copy-start(bf16[1024,384]{1,0:T(8,128)(2,1)} %sketch_ref.5) | copy-start | bytes 2359300
  23.0 16.0 %copy-start.2 = (f32[16,1024]{1,0:T(8,128)S(1)}, f32[16,1024]{1,0:T(8,128)}, u32[]{:S(2)}) copy-start(f32[16,1024]{1,0:T(8,128)} %weights_ref.3) | copy-start | bytes 196612
  23.0 29.2 %copy-start.4 = (f32[384]{0:T(512)S(1)}, f32[384]{0:T(512)}, u32[]{:S(2)}) copy-start(f32[384]{0:T(512)} %param.12) | copy-start | bytes 4612
  23.1 7.1 %collective-permute-start.9 = (f16[4,16,1024]{2,1,0:T(8,128)(2,1)S(1)}, f16[4,16,1024]{2,1,0:T(8,128)(2,1)S(1)}, u32[]{:S(2)}, u32[]{:S(2)}) collective-permute-start(f16[4,16,1024]{2,1,0:T(8,128)(2,1)S(1)} %convert_element_type.53), channel_id=1, source_target_pairs={{0,6},{2,4},{4,2},{6,0},{8,14},{10,12},{12,10},{14,8},{16,22},{18,... | collective-permute-start | bytes 393224 | tf_op jit(solution)/shard_map/ppermute | solution.py:325
  25.4 7.1 %collective-permute-start.8 = (f16[4,16,1024]{2,1,0:T(8,128)(2,1)S(1)}, f16[4,16,1024]{2,1,0:T(8,128)(2,1)S(1)}, u32[]{:S(2)}, u32[]{:S(2)}) collective-permute-start(f16[4,16,1024]{2,1,0:T(8,128)(2,1)S(1)} %convert_element_type.51), channel_id=1, source_target_pairs={{0,4},{2,6},{4,0},{6,2},{8,12},{10,14},{12,8},{14,10},{16,20},{18,... | collective-permute-start | bytes 393224 | tf_op jit(solution)/shard_map/ppermute | solution.py:325
  25.9 6.6 %collective-permute-start.7 = (f16[4,16,1024]{2,1,0:T(8,128)(2,1)S(1)}, f16[4,16,1024]{2,1,0:T(8,128)(2,1)S(1)}, u32[]{:S(2)}, u32[]{:S(2)}) collective-permute-start(f16[4,16,1024]{2,1,0:T(8,128)(2,1)S(1)} %convert_element_type.49), channel_id=1, source_target_pairs={{0,2},{2,0},{4,6},{6,4},{8,10},{10,8},{12,14},{14,12},{16,18},{18,... | collective-permute-start | bytes 393224 | tf_op jit(solution)/shard_map/ppermute | solution.py:325
  32.6 5.9 %collective-permute-start.10 = (f16[16,1024]{1,0:T(8,128)(2,1)S(1)}, f16[16,1024]{1,0:T(8,128)(2,1)S(1)}, u32[]{:S(2)}, u32[]{:S(2)}) collective-permute-start(f16[16,1024]{1,0:T(8,128)(2,1)S(1)} %get-tuple-element.65), channel_id=1, source_target_pairs={{0,24},{2,26},{4,28},{6,30},{8,16},{10,18},{12,20},{14,22},{16,8},... | collective-permute-start | bytes 98312 | tf_op jit(solution)/shard_map/ppermute | solution.py:325
  32.9 5.5 %collective-permute-start.12 = (f16[16,1024]{1,0:T(8,128)(2,1)S(1)}, f16[16,1024]{1,0:T(8,128)(2,1)S(1)}, u32[]{:S(2)}, u32[]{:S(2)}) collective-permute-start(f16[16,1024]{1,0:T(8,128)(2,1)S(1)} %get-tuple-element.66), channel_id=1, source_target_pairs={{0,16},{2,18},{4,20},{6,22},{8,24},{10,26},{12,28},{14,30},{16,0},... | collective-permute-start | bytes 98312 | tf_op jit(solution)/shard_map/ppermute | solution.py:325
  33.1 5.8 %collective-permute-start.11 = (f16[16,1024]{1,0:T(8,128)(2,1)S(1)}, f16[16,1024]{1,0:T(8,128)(2,1)S(1)}, u32[]{:S(2)}, u32[]{:S(2)}) collective-permute-start(f16[16,1024]{1,0:T(8,128)(2,1)S(1)} %get-tuple-element.67), channel_id=1, source_target_pairs={{0,8},{2,10},{4,12},{6,14},{8,0},{10,2},{12,4},{14,6},{16,24},{18,... | collective-permute-start | bytes 98312 | tf_op jit(solution)/shard_map/ppermute | solution.py:325
  52.2 1.3 collective-permute-start.13
  53.9 5.3 %collective-permute-start.16 = (bf16[16,1024]{1,0:T(8,128)(2,1)S(1)}, bf16[16,1024]{1,0:T(8,128)(2,1)S(1)}, u32[]{:S(2)}, u32[]{:S(2)}) collective-permute-start(bf16[16,1024]{1,0:T(8,128)(2,1)S(1)} %get-tuple-element.40), channel_id=1, source_target_pairs={{0,16},{2,18},{4,20},{6,22},{8,24},{10,26},{12,28},{14,30},{16,0},... | collective-permute-start | bytes 98312 | tf_op jit(solution)/shard_map/ppermute | solution.py:325
  55.0 4.2 %collective-permute-start.15 = (bf16[16,1024]{1,0:T(8,128)(2,1)S(1)}, bf16[16,1024]{1,0:T(8,128)(2,1)S(1)}, u32[]{:S(2)}, u32[]{:S(2)}) collective-permute-start(bf16[16,1024]{1,0:T(8,128)(2,1)S(1)} %get-tuple-element.40), channel_id=1, source_target_pairs={{0,8},{2,10},{4,12},{6,14},{8,0},{10,2},{12,4},{14,6},{16,24},{18,... | collective-permute-start | bytes 98312 | tf_op jit(solution)/shard_map/ppermute | solution.py:325
  56.0 5.7 %collective-permute-start.14 = (bf16[16,1024]{1,0:T(8,128)(2,1)S(1)}, bf16[16,1024]{1,0:T(8,128)(2,1)S(1)}, u32[]{:S(2)}, u32[]{:S(2)}) collective-permute-start(bf16[16,1024]{1,0:T(8,128)(2,1)S(1)} %get-tuple-element.40), channel_id=1, source_target_pairs={{0,24},{2,26},{4,28},{6,30},{8,16},{10,18},{12,20},{14,22},{16,8},... | collective-permute-start | bytes 98312 | tf_op jit(solution)/shard_map/ppermute | solution.py:325
  61.8 6.6 %collective-permute-start.19 = (bf16[4,16,1024]{2,1,0:T(8,128)(2,1)S(1)}, bf16[4,16,1024]{2,1,0:T(8,128)(2,1)S(1)}, u32[]{:S(2)}, u32[]{:S(2)}) collective-permute-start(bf16[4,16,1024]{2,1,0:T(8,128)(2,1)S(1)} %pad_maximum_fusion.1.refs_0_.refs_1_), channel_id=1, source_target_pairs={{0,6},{2,4},{4,2},{6,0},{8,14},{10,12},{12,10},{14,8},{16,22},{18,... | collective-permute-start | bytes 393224 | tf_op jit(solution)/shard_map/ppermute | solution.py:325
  62.5 6.7 %collective-permute-start.18 = (bf16[4,16,1024]{2,1,0:T(8,128)(2,1)S(1)}, bf16[4,16,1024]{2,1,0:T(8,128)(2,1)S(1)}, u32[]{:S(2)}, u32[]{:S(2)}) collective-permute-start(bf16[4,16,1024]{2,1,0:T(8,128)(2,1)S(1)} %pad_maximum_fusion.1.refs_0_.refs_1_), channel_id=1, source_target_pairs={{0,4},{2,6},{4,0},{6,2},{8,12},{10,14},{12,8},{14,10},{16,20},{18,... | collective-permute-start | bytes 393224 | tf_op jit(solution)/shard_map/ppermute | solution.py:325
  63.9 5.4 %collective-permute-start.17 = (bf16[4,16,1024]{2,1,0:T(8,128)(2,1)S(1)}, bf16[4,16,1024]{2,1,0:T(8,128)(2,1)S(1)}, u32[]{:S(2)}, u32[]{:S(2)}) collective-permute-start(bf16[4,16,1024]{2,1,0:T(8,128)(2,1)S(1)} %pad_maximum_fusion.1.refs_0_.refs_1_), channel_id=1, source_target_pairs={{0,2},{2,0},{4,6},{6,4},{8,10},{10,8},{12,14},{14,12},{16,18},{18,... | collective-permute-start | bytes 393224 | tf_op jit(solution)/shard_map/ppermute | solution.py:325
  70.2 1.2 collective-permute-start.20
  71.9 6.4 %collective-permute-start.21 = (bf16[4,16,1024]{2,1,0:T(8,128)(2,1)S(1)}, bf16[4,16,1024]{2,1,0:T(8,128)(2,1)S(1)}, u32[]{:S(2)}, u32[]{:S(2)}) collective-permute-start(bf16[4,16,1024]{2,1,0:T(8,128)(2,1)S(1)} %get-tuple-element.43), channel_id=1, source_target_pairs={{0,2},{2,0},{4,6},{6,4},{8,10},{10,8},{12,14},{14,12},{16,18},{18,... | collective-permute-start | bytes 393224 | tf_op jit(solution)/shard_map/ppermute | solution.py:325
  73.0 8.1 %collective-permute-start.22 = (bf16[4,16,1024]{2,1,0:T(8,128)(2,1)S(1)}, bf16[4,16,1024]{2,1,0:T(8,128)(2,1)S(1)}, u32[]{:S(2)}, u32[]{:S(2)}) collective-permute-start(bf16[4,16,1024]{2,1,0:T(8,128)(2,1)S(1)} %get-tuple-element.44), channel_id=1, source_target_pairs={{0,4},{2,6},{4,0},{6,2},{8,12},{10,14},{12,8},{14,10},{16,20},{18,... | collective-permute-start | bytes 393224 | tf_op jit(solution)/shard_map/ppermute | solution.py:325
  73.8 7.3 %collective-permute-start.23 = (bf16[4,16,1024]{2,1,0:T(8,128)(2,1)S(1)}, bf16[4,16,1024]{2,1,0:T(8,128)(2,1)S(1)}, u32[]{:S(2)}, u32[]{:S(2)}) collective-permute-start(bf16[4,16,1024]{2,1,0:T(8,128)(2,1)S(1)} %get-tuple-element.45), channel_id=1, source_target_pairs={{0,6},{2,4},{4,2},{6,0},{8,14},{10,12},{12,10},{14,8},{16,22},{18,... | collective-permute-start | bytes 393224 | tf_op jit(solution)/shard_map/ppermute | solution.py:325
  81.2 5.8 %collective-permute-start.24 = (bf16[16,1024]{1,0:T(8,128)(2,1)S(1)}, bf16[16,1024]{1,0:T(8,128)(2,1)S(1)}, u32[]{:S(2)}, u32[]{:S(2)}) collective-permute-start(bf16[16,1024]{1,0:T(8,128)(2,1)S(1)} %get-tuple-element.47), channel_id=1, source_target_pairs={{0,24},{2,26},{4,28},{6,30},{8,16},{10,18},{12,20},{14,22},{16,8},... | collective-permute-start | bytes 98312 | tf_op jit(solution)/shard_map/ppermute | solution.py:325
  83.7 3.9 %collective-permute-start.25 = (bf16[16,1024]{1,0:T(8,128)(2,1)S(1)}, bf16[16,1024]{1,0:T(8,128)(2,1)S(1)}, u32[]{:S(2)}, u32[]{:S(2)}) collective-permute-start(bf16[16,1024]{1,0:T(8,128)(2,1)S(1)} %get-tuple-element.48), channel_id=1, source_target_pairs={{0,8},{2,10},{4,12},{6,14},{8,0},{10,2},{12,4},{14,6},{16,24},{18,... | collective-permute-start | bytes 98312 | tf_op jit(solution)/shard_map/ppermute | solution.py:325
  83.8 4.8 %collective-permute-start.26 = (bf16[16,1024]{1,0:T(8,128)(2,1)S(1)}, bf16[16,1024]{1,0:T(8,128)(2,1)S(1)}, u32[]{:S(2)}, u32[]{:S(2)}) collective-permute-start(bf16[16,1024]{1,0:T(8,128)(2,1)S(1)} %get-tuple-element.49), channel_id=1, source_target_pairs={{0,16},{2,18},{4,20},{6,22},{8,24},{10,26},{12,28},{14,30},{16,0},... | collective-permute-start | bytes 98312 | tf_op jit(solution)/shard_map/ppermute | solution.py:325
  101.4 1.3 collective-permute-start.27
  103.3 5.4 %collective-permute-start.30 = (bf16[16,1024]{1,0:T(8,128)(2,1)S(1)}, bf16[16,1024]{1,0:T(8,128)(2,1)S(1)}, u32[]{:S(2)}, u32[]{:S(2)}) collective-permute-start(bf16[16,1024]{1,0:T(8,128)(2,1)S(1)} %get-tuple-element.55), channel_id=1, source_target_pairs={{0,16},{2,18},{4,20},{6,22},{8,24},{10,26},{12,28},{14,30},{16,0},... | collective-permute-start | bytes 98312 | tf_op jit(solution)/shard_map/ppermute | solution.py:325
  104.4 4.3 %collective-permute-start.29 = (bf16[16,1024]{1,0:T(8,128)(2,1)S(1)}, bf16[16,1024]{1,0:T(8,128)(2,1)S(1)}, u32[]{:S(2)}, u32[]{:S(2)}) collective-permute-start(bf16[16,1024]{1,0:T(8,128)(2,1)S(1)} %get-tuple-element.55), channel_id=1, source_target_pairs={{0,8},{2,10},{4,12},{6,14},{8,0},{10,2},{12,4},{14,6},{16,24},{18,... | collective-permute-start | bytes 98312 | tf_op jit(solution)/shard_map/ppermute | solution.py:325
  105.7 5.7 %collective-permute-start.28 = (bf16[16,1024]{1,0:T(8,128)(2,1)S(1)}, bf16[16,1024]{1,0:T(8,128)(2,1)S(1)}, u32[]{:S(2)}, u32[]{:S(2)}) collective-permute-start(bf16[16,1024]{1,0:T(8,128)(2,1)S(1)} %get-tuple-element.55), channel_id=1, source_target_pairs={{0,24},{2,26},{4,28},{6,30},{8,16},{10,18},{12,20},{14,22},{16,8},... | collective-permute-start | bytes 98312 | tf_op jit(solution)/shard_map/ppermute | solution.py:325
  111.4 6.5 %collective-permute-start.33 = (bf16[4,16,1024]{2,1,0:T(8,128)(2,1)S(1)}, bf16[4,16,1024]{2,1,0:T(8,128)(2,1)S(1)}, u32[]{:S(2)}, u32[]{:S(2)}) collective-permute-start(bf16[4,16,1024]{2,1,0:T(8,128)(2,1)S(1)} %pad_maximum_fusion.2.refs_0_), channel_id=1, source_target_pairs={{0,6},{2,4},{4,2},{6,0},{8,14},{10,12},{12,10},{14,8},{16,22},{18,... | collective-permute-start | bytes 393224 | tf_op jit(solution)/shard_map/ppermute | solution.py:325
  112.2 6.5 %collective-permute-start.32 = (bf16[4,16,1024]{2,1,0:T(8,128)(2,1)S(1)}, bf16[4,16,1024]{2,1,0:T(8,128)(2,1)S(1)}, u32[]{:S(2)}, u32[]{:S(2)}) collective-permute-start(bf16[4,16,1024]{2,1,0:T(8,128)(2,1)S(1)} %pad_maximum_fusion.2.refs_0_), channel_id=1, source_target_pairs={{0,4},{2,6},{4,0},{6,2},{8,12},{10,14},{12,8},{14,10},{16,20},{18,... | collective-permute-start | bytes 393224 | tf_op jit(solution)/shard_map/ppermute | solution.py:325
  113.5 5.2 %collective-permute-start.31 = (bf16[4,16,1024]{2,1,0:T(8,128)(2,1)S(1)}, bf16[4,16,1024]{2,1,0:T(8,128)(2,1)S(1)}, u32[]{:S(2)}, u32[]{:S(2)}) collective-permute-start(bf16[4,16,1024]{2,1,0:T(8,128)(2,1)S(1)} %pad_maximum_fusion.2.refs_0_), channel_id=1, source_target_pairs={{0,2},{2,0},{4,6},{6,4},{8,10},{10,8},{12,14},{14,12},{16,18},{18,... | collective-permute-start | bytes 393224 | tf_op jit(solution)/shard_map/ppermute | solution.py:325
  119.6 1.2 collective-permute-start.34
where the time goes:
time: 134 us
  waiting for transfers between devices  41.7 us (31%)
  starting transfers between devices  41.4 us (31%)
  blocking collectives  37.3 us (28%)
  Pallas kernels  9.32 us (7%)
  local copies, waits for them, and re-layouts  2.31 us (2%)
  other arithmetic  1.79 us (1%)
    ppermute x30, starting transfers between devices, swap(): lax.ppermute(values, 'samp', [(i, i ^ distance) for i in range(samp)])  41.1 us
    all_to_all x3, blocking collectives, exchange(): return lax.all_to_all(blocks, 'samp', 0, 0)  37.3 us
    ppermute x30, waiting for transfers between devices, swap(): lax.ppermute(values, 'samp', [(i, i ^ distance) for i in range(samp)])  35.8 us
    pallas_call x17, Pallas kernels, call(): pl.pallas_call(body, out_shape=[jax.ShapeDtypeStruct(shape, dtype) for sh...  8.29 us
    ppermute x5, waiting for transfers between devices, feat_parts(): return (values, lax.ppermute(values, 'feat', [(0, 1), (1, 0)]))  5.87 us
  transfers between devices with their start and end apart: 35, of which 26 were waited for; matrix products, arithmetic and copies ran while one was open for 0% of the time, Pallas kernels for 2%

commit v1 on v0

--- a/solution.py
+++ b/solution.py
@@ -331,7 +331,10 @@
         return received
 
     def swap_near(values):
-        return [swap(value, distance) for value, distance in zip(values, near_order)]
+        received = []
+        for value, distance in zip(values, near_order):
+            received.append(swap(value, distance))
+        return received
 
     def gather(block):
         column = jnp.stack([block] + swap_far([block] * len(far_order)))

time: 134 us -> 134 us (level)
  no operation moved by 1% of the time
where the time goes in v1:
time: 134 us
  waiting for transfers between devices  41.7 us (31%)
  starting transfers between devices  41.4 us (31%)
  blocking collectives  37.3 us (28%)
  Pallas kernels  9.32 us (7%)
  local copies, waits for them, and re-layouts  2.31 us (2%)
  other arithmetic  1.79 us (1%)
    ppermute x30, starting transfers between devices, swap(): lax.ppermute(values, 'samp', [(i, i ^ distance) for i in range(samp)])  41.1 us
    all_to_all x3, blocking collectives, exchange(): return lax.all_to_all(blocks, 'samp', 0, 0)  37.3 us
    ppermute x30, waiting for transfers between devices, swap(): lax.ppermute(values, 'samp', [(i, i ^ distance) for i in range(samp)])  35.8 us
    pallas_call x17, Pallas kernels, call(): pl.pallas_call(body, out_shape=[jax.ShapeDtypeStruct(shape, dtype) for sh...  8.29 us
    ppermute x5, waiting for transfers between devices, feat_parts(): return (values, lax.ppermute(values, 'feat', [(0, 1), (1, 0)]))  5.87 us
  transfers between devices with their start and end apart: 35, of which 26 were waited for; matrix products, arithmetic and copies ran while one was open for 0% of the time, Pallas kernels for 2%

profile of v1, /device:TPU:0, one launch (start us, length us, event | category | flops | bytes accessed | tf_op | source)
XLA Modules:
  0.0 134.1 jit_solution(4909945394909832901)
XLA Ops:
  0.8 4.1 %collective-permute-start.2 = (bf16[16,1024]{1,0:T(8,128)(2,1)S(1)}, bf16[16,1024]{1,0:T(8,128)(2,1)S(1)}, u32[]{:S(2)}, u32[]{:S(2)}) collective-permute-start(bf16[16,1024]{1,0:T(8,128)(2,1)S(1)} %convert_element_type.48), channel_id=1, source_target_pairs={{0,16},{2,18},{4,20},{6,22},{8,24},{10,26},{12,28},{14,30},{16,0},... | collective-permute-start | bytes 98312 | tf_op jit(solution)/shard_map/ppermute | solution.py:325
  4.9 1.6 %collective-permute-start.1 = (bf16[16,1024]{1,0:T(8,128)(2,1)S(1)}, bf16[16,1024]{1,0:T(8,128)(2,1)S(1)}, u32[]{:S(2)}, u32[]{:S(2)}) collective-permute-start(bf16[16,1024]{1,0:T(8,128)(2,1)S(1)} %convert_element_type.48), channel_id=1, source_target_pairs={{0,8},{2,10},{4,12},{6,14},{8,0},{10,2},{12,4},{14,6},{16,24},{18,... | collective-permute-start | bytes 98312 | tf_op jit(solution)/shard_map/ppermute | solution.py:325
  7.3 1.6 %collective-permute-done.1 = bf16[16,1024]{1,0:T(8,128)(2,1)S(1)} collective-permute-done((bf16[16,1024]{1,0:T(8,128)(2,1)S(1)}, bf16[16,1024]{1,0:T(8,128)(2,1)S(1)}, u32[]{:S(2)}, u32[]{:S(2)}) %collective-permute-start.1) | collective-permute-done | bytes 32800 | tf_op jit(solution)/shard_map/ppermute | solution.py:325
  8.8 3.4 %collective-permute-done = bf16[16,1024]{1,0:T(8,128)(2,1)S(1)} collective-permute-done((bf16[16,1024]{1,0:T(8,128)(2,1)S(1)}, bf16[16,1024]{1,0:T(8,128)(2,1)S(1)}, u32[]{:S(2)}, u32[]{:S(2)}) %collective-permute-start) | collective-permute-done | bytes 32800 | tf_op jit(solution)/shard_map/ppermute | solution.py:325
  12.2 2.5 %collective-permute-start.5 = (bf16[4,16,1024]{2,1,0:T(8,128)(2,1)S(1)}, bf16[4,16,1024]{2,1,0:T(8,128)(2,1)S(1)}, u32[]{:S(2)}, u32[]{:S(2)}) collective-permute-start(bf16[4,16,1024]{2,1,0:T(8,128)(2,1)S(1)} %pad_maximum_fusion.refs_0_), channel_id=1, source_target_pairs={{0,6},{2,4},{4,2},{6,0},{8,14},{10,12},{12,10},{14,8},{16,22},{18,... | collective-permute-start | bytes 393224 | tf_op jit(solution)/shard_map/ppermute | solution.py:325
  16.4 2.2 %copy-done.1 = bf16[128,16384]{1,0:T(8,128)(2,1)S(1)} copy-done((bf16[128,16384]{1,0:T(8,128)(2,1)S(1)}, bf16[128,16384]{1,0:T(8,128)(2,1)}, u32[]{:S(2)}) %copy-start.1) | copy-done | bytes 4194328
  18.6 1.0 load.1.refs_1_.refs_3_.refs_2_.refs_6_
  20.3 0.9 shard_map.74.refs_0_
  21.3 1.2 collective-permute-done.6.refs_1_
  23.1 2.3 %collective-permute-start.9 = (f16[4,16,1024]{2,1,0:T(8,128)(2,1)S(1)}, f16[4,16,1024]{2,1,0:T(8,128)(2,1)S(1)}, u32[]{:S(2)}, u32[]{:S(2)}) collective-permute-start(f16[4,16,1024]{2,1,0:T(8,128)(2,1)S(1)} %convert_element_type.53), channel_id=1, source_target_pairs={{0,6},{2,4},{4,2},{6,0},{8,14},{10,12},{12,10},{14,8},{16,22},{18,... | collective-permute-start | bytes 393224 | tf_op jit(solution)/shard_map/ppermute | solution.py:325
  26.9 3.3 %collective-permute-done.9 = f16[4,16,1024]{2,1,0:T(8,128)(2,1)S(1)} collective-permute-done((f16[4,16,1024]{2,1,0:T(8,128)(2,1)S(1)}, f16[4,16,1024]{2,1,0:T(8,128)(2,1)S(1)}, u32[]{:S(2)}, u32[]{:S(2)}) %collective-permute-start.9) | collective-permute-done | bytes 131104 | tf_op jit(solution)/shard_map/ppermute | solution.py:325
  30.2 2.2 %collective-permute-done.8 = f16[4,16,1024]{2,1,0:T(8,128)(2,1)S(1)} collective-permute-done((f16[4,16,1024]{2,1,0:T(8,128)(2,1)S(1)}, f16[4,16,1024]{2,1,0:T(8,128)(2,1)S(1)}, u32[]{:S(2)}, u32[]{:S(2)}) %collective-permute-start.8) | collective-permute-done | bytes 131104 | tf_op jit(solution)/shard_map/ppermute | solution.py:325
  33.1 4.0 %collective-permute-start.11 = (f16[16,1024]{1,0:T(8,128)(2,1)S(1)}, f16[16,1024]{1,0:T(8,128)(2,1)S(1)}, u32[]{:S(2)}, u32[]{:S(2)}) collective-permute-start(f16[16,1024]{1,0:T(8,128)(2,1)S(1)} %get-tuple-element.67), channel_id=1, source_target_pairs={{0,8},{2,10},{4,12},{6,14},{8,0},{10,2},{12,4},{14,6},{16,24},{18,... | collective-permute-start | bytes 98312 | tf_op jit(solution)/shard_map/ppermute | solution.py:325
  37.0 1.4 %collective-permute-done.10 = f16[16,1024]{1,0:T(8,128)(2,1)S(1)} collective-permute-done((f16[16,1024]{1,0:T(8,128)(2,1)S(1)}, f16[16,1024]{1,0:T(8,128)(2,1)S(1)}, u32[]{:S(2)}, u32[]{:S(2)}) %collective-permute-start.10) | collective-permute-done | bytes 32800 | tf_op jit(solution)/shard_map/ppermute | solution.py:325
  39.3 12.8 %all_to_all.15 = bf16[16,16,384]{2,1,0:T(8,128)(2,1)S(1)} all-to-all(bf16[16,16,384]{2,1,0:T(8,128)(2,1)S(1)} %get-tuple-element.38), channel_id=1, replica_groups=mesh['samp'=16,'feat'=2] {'samp'}, dimensions={0} | all-to-all | bytes 393216 | tf_op jit(solution)/shard_map/all_to_all | solution.py:344
  52.3 1.2 collective-permute-done.13.other_ref
  53.9 1.1 collective-permute-start.16
  55.0 1.1 collective-permute-start.15
  56.0 2.2 %collective-permute-start.14 = (bf16[16,1024]{1,0:T(8,128)(2,1)S(1)}, bf16[16,1024]{1,0:T(8,128)(2,1)S(1)}, u32[]{:S(2)}, u32[]{:S(2)}) collective-permute-start(bf16[16,1024]{1,0:T(8,128)(2,1)S(1)} %get-tuple-element.40), channel_id=1, source_target_pairs={{0,24},{2,26},{4,28},{6,30},{8,16},{10,18},{12,20},{14,22},{16,8},... | collective-permute-start | bytes 98312 | tf_op jit(solution)/shard_map/ppermute | solution.py:325
  59.1 2.6 %collective-permute-done.14 = bf16[16,1024]{1,0:T(8,128)(2,1)S(1)} collective-permute-done((bf16[16,1024]{1,0:T(8,128)(2,1)S(1)}, bf16[16,1024]{1,0:T(8,128)(2,1)S(1)}, u32[]{:S(2)}, u32[]{:S(2)}) %collective-permute-start.14) | collective-permute-done | bytes 32800 | tf_op jit(solution)/shard_map/ppermute | solution.py:325
  62.5 1.3 collective-permute-start.18
  63.9 1.5 %collective-permute-start.17 = (bf16[4,16,1024]{2,1,0:T(8,128)(2,1)S(1)}, bf16[4,16,1024]{2,1,0:T(8,128)(2,1)S(1)}, u32[]{:S(2)}, u32[]{:S(2)}) collective-permute-start(bf16[4,16,1024]{2,1,0:T(8,128)(2,1)S(1)} %pad_maximum_fusion.1.refs_0_.refs_1_), channel_id=1, source_target_pairs={{0,2},{2,0},{4,6},{6,4},{8,10},{10,8},{12,14},{14,12},{16,18},{18,... | collective-permute-start | bytes 393224 | tf_op jit(solution)/shard_map/ppermute | solution.py:325
  65.7 2.7 %collective-permute-done.19.refs_2_.refs_5_ = bf16[4,16,1024]{2,1,0:T(8,128)(2,1)S(1)} collective-permute-done((bf16[4,16,1024]{2,1,0:T(8,128)(2,1)S(1)}, bf16[4,16,1024]{2,1,0:T(8,128)(2,1)S(1)}, u32[]{:S(2)}, u32[]{:S(2)}) %collective-permute-start.19) | collective-permute-done | bytes 131104 | tf_op jit(solution)/shard_map/ppermute | solution.py:325
  68.4 0.9 collective-permute-done.18.refs_1_.refs_4_
  69.3 0.9 shard_map.80.refs_0_
  70.2 1.2 collective-permute-done.20.refs_1_
  71.9 1.1 collective-permute-start.21
  73.8 1.6 %collective-permute-start.23 = (bf16[4,16,1024]{2,1,0:T(8,128)(2,1)S(1)}, bf16[4,16,1024]{2,1,0:T(8,128)(2,1)S(1)}, u32[]{:S(2)}, u32[]{:S(2)}) collective-permute-start(bf16[4,16,1024]{2,1,0:T(8,128)(2,1)S(1)} %get-tuple-element.45), channel_id=1, source_target_pairs={{0,6},{2,4},{4,2},{6,0},{8,14},{10,12},{12,10},{14,8},{16,22},{18,... | collective-permute-start | bytes 393224 | tf_op jit(solution)/shard_map/ppermute | solution.py:325
  75.7 2.6 %collective-permute-done.21.refs_0_ = bf16[4,16,1024]{2,1,0:T(8,128)(2,1)S(1)} collective-permute-done((bf16[4,16,1024]{2,1,0:T(8,128)(2,1)S(1)}, bf16[4,16,1024]{2,1,0:T(8,128)(2,1)S(1)}, u32[]{:S(2)}, u32[]{:S(2)}) %collective-permute-start.21) | collective-permute-done | bytes 131104 | tf_op jit(solution)/shard_map/ppermute | solution.py:325
  78.3 2.8 %collective-permute-done.22.refs_1_ = bf16[4,16,1024]{2,1,0:T(8,128)(2,1)S(1)} collective-permute-done((bf16[4,16,1024]{2,1,0:T(8,128)(2,1)S(1)}, bf16[4,16,1024]{2,1,0:T(8,128)(2,1)S(1)}, u32[]{:S(2)}, u32[]{:S(2)}) %collective-permute-start.22) | collective-permute-done | bytes 131104 | tf_op jit(solution)/shard_map/ppermute | solution.py:325
  81.2 2.6 %collective-permute-start.24 = (bf16[16,1024]{1,0:T(8,128)(2,1)S(1)}, bf16[16,1024]{1,0:T(8,128)(2,1)S(1)}, u32[]{:S(2)}, u32[]{:S(2)}) collective-permute-start(bf16[16,1024]{1,0:T(8,128)(2,1)S(1)} %get-tuple-element.47), channel_id=1, source_target_pairs={{0,24},{2,26},{4,28},{6,30},{8,16},{10,18},{12,20},{14,22},{16,8},... | collective-permute-start | bytes 98312 | tf_op jit(solution)/shard_map/ppermute | solution.py:325
  83.8 1.9 %collective-permute-start.26 = (bf16[16,1024]{1,0:T(8,128)(2,1)S(1)}, bf16[16,1024]{1,0:T(8,128)(2,1)S(1)}, u32[]{:S(2)}, u32[]{:S(2)}) collective-permute-start(bf16[16,1024]{1,0:T(8,128)(2,1)S(1)} %get-tuple-element.49), channel_id=1, source_target_pairs={{0,16},{2,18},{4,20},{6,22},{8,24},{10,26},{12,28},{14,30},{16,0},... | collective-permute-start | bytes 98312 | tf_op jit(solution)/shard_map/ppermute | solution.py:325
  85.6 1.3 collective-permute-done.24.refs_1_
  87.7 0.9 collective-permute-done.26.refs_3_
  88.9 12.5 %all_to_all.16 = bf16[16,16,512]{2,1,0:T(8,128)(2,1)S(1)} all-to-all(bf16[16,16,512]{2,1,0:T(8,128)(2,1)S(1)} %get-tuple-element.52), channel_id=1, replica_groups=mesh['samp'=16,'feat'=2] {'samp'}, dimensions={0} | all-to-all | bytes 524288 | tf_op jit(solution)/shard_map/all_to_all | solution.py:344
  101.5 1.2 collective-permute-done.27.other_ref
  103.3 1.1 collective-permute-start.30
  104.4 1.3 collective-permute-start.29
  105.7 2.0 %collective-permute-start.28 = (bf16[16,1024]{1,0:T(8,128)(2,1)S(1)}, bf16[16,1024]{1,0:T(8,128)(2,1)S(1)}, u32[]{:S(2)}, u32[]{:S(2)}) collective-permute-start(bf16[16,1024]{1,0:T(8,128)(2,1)S(1)} %get-tuple-element.55), channel_id=1, source_target_pairs={{0,24},{2,26},{4,28},{6,30},{8,16},{10,18},{12,20},{14,22},{16,8},... | collective-permute-start | bytes 98312 | tf_op jit(solution)/shard_map/ppermute | solution.py:325
  107.7 1.0 collective-permute-done.30
  108.7 2.7 %collective-permute-done.28 = bf16[16,1024]{1,0:T(8,128)(2,1)S(1)} collective-permute-done((bf16[16,1024]{1,0:T(8,128)(2,1)S(1)}, bf16[16,1024]{1,0:T(8,128)(2,1)S(1)}, u32[]{:S(2)}, u32[]{:S(2)}) %collective-permute-start.28) | collective-permute-done | bytes 32800 | tf_op jit(solution)/shard_map/ppermute | solution.py:325
  112.2 1.3 collective-permute-start.32
  113.5 1.5 %collective-permute-start.31 = (bf16[4,16,1024]{2,1,0:T(8,128)(2,1)S(1)}, bf16[4,16,1024]{2,1,0:T(8,128)(2,1)S(1)}, u32[]{:S(2)}, u32[]{:S(2)}) collective-permute-start(bf16[4,16,1024]{2,1,0:T(8,128)(2,1)S(1)} %pad_maximum_fusion.2.refs_0_), channel_id=1, source_target_pairs={{0,2},{2,0},{4,6},{6,4},{8,10},{10,8},{12,14},{14,12},{16,18},{18,... | collective-permute-start | bytes 393224 | tf_op jit(solution)/shard_map/ppermute | solution.py:325
  115.3 2.5 %collective-permute-done.33.refs_2_ = bf16[4,16,1024]{2,1,0:T(8,128)(2,1)S(1)} collective-permute-done((bf16[4,16,1024]{2,1,0:T(8,128)(2,1)S(1)}, bf16[4,16,1024]{2,1,0:T(8,128)(2,1)S(1)}, u32[]{:S(2)}, u32[]{:S(2)}) %collective-permute-start.33) | collective-permute-done | bytes 131104 | tf_op jit(solution)/shard_map/ppermute | solution.py:325
  118.7 1.0 shard_map.87.both_ref
  119.7 1.2 collective-permute-done.34.other_ref
  121.0 12.0 %all_to_all.17.received_ref = f32[16,8,128]{2,1,0:T(8,128)S(1)} all-to-all(f32[16,8,128]{2,1,0:T(8,128)S(1)} %get-tuple-element.58), channel_id=1, replica_groups=mesh['samp'=16,'feat'=2] {'samp'}, dimensions={0} | all-to-all | bytes 131072 | tf_op jit(solution)/shard_map/all_to_all | solution.py:344
  133.0 1.1 shard_map.89
  (71 shorter events, 15.8 us)
Async XLA Ops:
  0.8 6.4 %collective-permute-start.2 = (bf16[16,1024]{1,0:T(8,128)(2,1)S(1)}, bf16[16,1024]{1,0:T(8,128)(2,1)S(1)}, u32[]{:S(2)}, u32[]{:S(2)}) collective-permute-start(bf16[16,1024]{1,0:T(8,128)(2,1)S(1)} %convert_element_type.48), channel_id=1, source_target_pairs={{0,16},{2,18},{4,20},{6,22},{8,24},{10,26},{12,28},{14,30},{16,0},... | collective-permute-start | bytes 98312 | tf_op jit(solution)/shard_map/ppermute | solution.py:325
  4.9 3.9 %collective-permute-start.1 = (bf16[16,1024]{1,0:T(8,128)(2,1)S(1)}, bf16[16,1024]{1,0:T(8,128)(2,1)S(1)}, u32[]{:S(2)}, u32[]{:S(2)}) collective-permute-start(bf16[16,1024]{1,0:T(8,128)(2,1)S(1)} %convert_element_type.48), channel_id=1, source_target_pairs={{0,8},{2,10},{4,12},{6,14},{8,0},{10,2},{12,4},{14,6},{16,24},{18,... | collective-permute-start | bytes 98312 | tf_op jit(solution)/shard_map/ppermute | solution.py:325
  6.5 5.7 %collective-permute-start = (bf16[16,1024]{1,0:T(8,128)(2,1)S(1)}, bf16[16,1024]{1,0:T(8,128)(2,1)S(1)}, u32[]{:S(2)}, u32[]{:S(2)}) collective-permute-start(bf16[16,1024]{1,0:T(8,128)(2,1)S(1)} %convert_element_type.48), channel_id=1, source_target_pairs={{0,24},{2,26},{4,28},{6,30},{8,16},{10,18},{12,20},{14,22},{16,8},... | collective-permute-start | bytes 98312 | tf_op jit(solution)/shard_map/ppermute | solution.py:325
  12.2 7.8 %collective-permute-start.5 = (bf16[4,16,1024]{2,1,0:T(8,128)(2,1)S(1)}, bf16[4,16,1024]{2,1,0:T(8,128)(2,1)S(1)}, u32[]{:S(2)}, u32[]{:S(2)}) collective-permute-start(bf16[4,16,1024]{2,1,0:T(8,128)(2,1)S(1)} %pad_maximum_fusion.refs_0_), channel_id=1, source_target_pairs={{0,6},{2,4},{4,2},{6,0},{8,14},{10,12},{12,10},{14,8},{16,22},{18,... | collective-permute-start | bytes 393224 | tf_op jit(solution)/shard_map/ppermute | solution.py:325
  14.7 5.6 %collective-permute-start.4 = (bf16[4,16,1024]{2,1,0:T(8,128)(2,1)S(1)}, bf16[4,16,1024]{2,1,0:T(8,128)(2,1)S(1)}, u32[]{:S(2)}, u32[]{:S(2)}) collective-permute-start(bf16[4,16,1024]{2,1,0:T(8,128)(2,1)S(1)} %pad_maximum_fusion.refs_0_), channel_id=1, source_target_pairs={{0,4},{2,6},{4,0},{6,2},{8,12},{10,14},{12,8},{14,10},{16,20},{18,... | collective-permute-start | bytes 393224 | tf_op jit(solution)/shard_map/ppermute | solution.py:325
  15.2 5.1 %collective-permute-start.3 = (bf16[4,16,1024]{2,1,0:T(8,128)(2,1)S(1)}, bf16[4,16,1024]{2,1,0:T(8,128)(2,1)S(1)}, u32[]{:S(2)}, u32[]{:S(2)}) collective-permute-start(bf16[4,16,1024]{2,1,0:T(8,128)(2,1)S(1)} %pad_maximum_fusion.refs_0_), channel_id=1, source_target_pairs={{0,2},{2,0},{4,6},{6,4},{8,10},{10,8},{12,14},{14,12},{16,18},{18,... | collective-permute-start | bytes 393224 | tf_op jit(solution)/shard_map/ppermute | solution.py:325
  16.4 2.2 %copy-start.1 = (bf16[128,16384]{1,0:T(8,128)(2,1)S(1)}, bf16[128,16384]{1,0:T(8,128)(2,1)}, u32[]{:S(2)}) copy-start(bf16[128,16384]{1,0:T(8,128)(2,1)} %design_ref.1) | copy-start | bytes 12582916
  19.7 2.8 %copy-start.3 = (s32[128]{0:T(128)S(1)}, s32[128]{0:T(128)}, u32[]{:S(2)}) copy-start(s32[128]{0:T(128)} %param.8) | copy-start | bytes 1540
  21.3 1.2 collective-permute-start.6
  23.0 15.9 %copy-start.5 = (f32[16]{0:T(128)S(1)}, f32[16]{0:T(128)}, u32[]{:S(2)}) copy-start(f32[16]{0:T(128)} %param.10) | copy-start | bytes 196
  23.0 16.0 %copy-start = (bf16[1024,384]{1,0:T(8,128)(2,1)S(1)}, bf16[1024,384]{1,0:T(8,128)(2,1)}, u32[]{:S(2)}) copy-start(bf16[1024,384]{1,0:T(8,128)(2,1)} %sketch_ref.5) | copy-start | bytes 2359300
  23.0 16.0 %copy-start.2 = (f32[16,1024]{1,0:T(8,128)S(1)}, f32[16,1024]{1,0:T(8,128)}, u32[]{:S(2)}) copy-start(f32[16,1024]{1,0:T(8,128)} %weights_ref.3) | copy-start | bytes 196612
  23.0 29.2 %copy-start.4 = (f32[384]{0:T(512)S(1)}, f32[384]{0:T(512)}, u32[]{:S(2)}) copy-start(f32[384]{0:T(512)} %param.12) | copy-start | bytes 4612
  23.1 7.1 %collective-permute-start.9 = (f16[4,16,1024]{2,1,0:T(8,128)(2,1)S(1)}, f16[4,16,1024]{2,1,0:T(8,128)(2,1)S(1)}, u32[]{:S(2)}, u32[]{:S(2)}) collective-permute-start(f16[4,16,1024]{2,1,0:T(8,128)(2,1)S(1)} %convert_element_type.53), channel_id=1, source_target_pairs={{0,6},{2,4},{4,2},{6,0},{8,14},{10,12},{12,10},{14,8},{16,22},{18,... | collective-permute-start | bytes 393224 | tf_op jit(solution)/shard_map/ppermute | solution.py:325
  25.4 7.1 %collective-permute-start.8 = (f16[4,16,1024]{2,1,0:T(8,128)(2,1)S(1)}, f16[4,16,1024]{2,1,0:T(8,128)(2,1)S(1)}, u32[]{:S(2)}, u32[]{:S(2)}) collective-permute-start(f16[4,16,1024]{2,1,0:T(8,128)(2,1)S(1)} %convert_element_type.51), channel_id=1, source_target_pairs={{0,4},{2,6},{4,0},{6,2},{8,12},{10,14},{12,8},{14,10},{16,20},{18,... | collective-permute-start | bytes 393224 | tf_op jit(solution)/shard_map/ppermute | solution.py:325
  25.9 6.6 %collective-permute-start.7 = (f16[4,16,1024]{2,1,0:T(8,128)(2,1)S(1)}, f16[4,16,1024]{2,1,0:T(8,128)(2,1)S(1)}, u32[]{:S(2)}, u32[]{:S(2)}) collective-permute-start(f16[4,16,1024]{2,1,0:T(8,128)(2,1)S(1)} %convert_element_type.49), channel_id=1, source_target_pairs={{0,2},{2,0},{4,6},{6,4},{8,10},{10,8},{12,14},{14,12},{16,18},{18,... | collective-permute-start | bytes 393224 | tf_op jit(solution)/shard_map/ppermute | solution.py:325
  32.6 5.9 %collective-permute-start.10 = (f16[16,1024]{1,0:T(8,128)(2,1)S(1)}, f16[16,1024]{1,0:T(8,128)(2,1)S(1)}, u32[]{:S(2)}, u32[]{:S(2)}) collective-permute-start(f16[16,1024]{1,0:T(8,128)(2,1)S(1)} %get-tuple-element.65), channel_id=1, source_target_pairs={{0,24},{2,26},{4,28},{6,30},{8,16},{10,18},{12,20},{14,22},{16,8},... | collective-permute-start | bytes 98312 | tf_op jit(solution)/shard_map/ppermute | solution.py:325
  32.9 5.5 %collective-permute-start.12 = (f16[16,1024]{1,0:T(8,128)(2,1)S(1)}, f16[16,1024]{1,0:T(8,128)(2,1)S(1)}, u32[]{:S(2)}, u32[]{:S(2)}) collective-permute-start(f16[16,1024]{1,0:T(8,128)(2,1)S(1)} %get-tuple-element.66), channel_id=1, source_target_pairs={{0,16},{2,18},{4,20},{6,22},{8,24},{10,26},{12,28},{14,30},{16,0},... | collective-permute-start | bytes 98312 | tf_op jit(solution)/shard_map/ppermute | solution.py:325
  33.1 5.8 %collective-permute-start.11 = (f16[16,1024]{1,0:T(8,128)(2,1)S(1)}, f16[16,1024]{1,0:T(8,128)(2,1)S(1)}, u32[]{:S(2)}, u32[]{:S(2)}) collective-permute-start(f16[16,1024]{1,0:T(8,128)(2,1)S(1)} %get-tuple-element.67), channel_id=1, source_target_pairs={{0,8},{2,10},{4,12},{6,14},{8,0},{10,2},{12,4},{14,6},{16,24},{18,... | collective-permute-start | bytes 98312 | tf_op jit(solution)/shard_map/ppermute | solution.py:325
  52.2 1.3 collective-permute-start.13
  53.9 5.3 %collective-permute-start.16 = (bf16[16,1024]{1,0:T(8,128)(2,1)S(1)}, bf16[16,1024]{1,0:T(8,128)(2,1)S(1)}, u32[]{:S(2)}, u32[]{:S(2)}) collective-permute-start(bf16[16,1024]{1,0:T(8,128)(2,1)S(1)} %get-tuple-element.40), channel_id=1, source_target_pairs={{0,16},{2,18},{4,20},{6,22},{8,24},{10,26},{12,28},{14,30},{16,0},... | collective-permute-start | bytes 98312 | tf_op jit(solution)/shard_map/ppermute | solution.py:325
  55.0 4.2 %collective-permute-start.15 = (bf16[16,1024]{1,0:T(8,128)(2,1)S(1)}, bf16[16,1024]{1,0:T(8,128)(2,1)S(1)}, u32[]{:S(2)}, u32[]{:S(2)}) collective-permute-start(bf16[16,1024]{1,0:T(8,128)(2,1)S(1)} %get-tuple-element.40), channel_id=1, source_target_pairs={{0,8},{2,10},{4,12},{6,14},{8,0},{10,2},{12,4},{14,6},{16,24},{18,... | collective-permute-start | bytes 98312 | tf_op jit(solution)/shard_map/ppermute | solution.py:325
  56.0 5.7 %collective-permute-start.14 = (bf16[16,1024]{1,0:T(8,128)(2,1)S(1)}, bf16[16,1024]{1,0:T(8,128)(2,1)S(1)}, u32[]{:S(2)}, u32[]{:S(2)}) collective-permute-start(bf16[16,1024]{1,0:T(8,128)(2,1)S(1)} %get-tuple-element.40), channel_id=1, source_target_pairs={{0,24},{2,26},{4,28},{6,30},{8,16},{10,18},{12,20},{14,22},{16,8},... | collective-permute-start | bytes 98312 | tf_op jit(solution)/shard_map/ppermute | solution.py:325
  61.8 6.6 %collective-permute-start.19 = (bf16[4,16,1024]{2,1,0:T(8,128)(2,1)S(1)}, bf16[4,16,1024]{2,1,0:T(8,128)(2,1)S(1)}, u32[]{:S(2)}, u32[]{:S(2)}) collective-permute-start(bf16[4,16,1024]{2,1,0:T(8,128)(2,1)S(1)} %pad_maximum_fusion.1.refs_0_.refs_1_), channel_id=1, source_target_pairs={{0,6},{2,4},{4,2},{6,0},{8,14},{10,12},{12,10},{14,8},{16,22},{18,... | collective-permute-start | bytes 393224 | tf_op jit(solution)/shard_map/ppermute | solution.py:325
  62.5 6.7 %collective-permute-start.18 = (bf16[4,16,1024]{2,1,0:T(8,128)(2,1)S(1)}, bf16[4,16,1024]{2,1,0:T(8,128)(2,1)S(1)}, u32[]{:S(2)}, u32[]{:S(2)}) collective-permute-start(bf16[4,16,1024]{2,1,0:T(8,128)(2,1)S(1)} %pad_maximum_fusion.1.refs_0_.refs_1_), channel_id=1, source_target_pairs={{0,4},{2,6},{4,0},{6,2},{8,12},{10,14},{12,8},{14,10},{16,20},{18,... | collective-permute-start | bytes 393224 | tf_op jit(solution)/shard_map/ppermute | solution.py:325
  63.9 5.4 %collective-permute-start.17 = (bf16[4,16,1024]{2,1,0:T(8,128)(2,1)S(1)}, bf16[4,16,1024]{2,1,0:T(8,128)(2,1)S(1)}, u32[]{:S(2)}, u32[]{:S(2)}) collective-permute-start(bf16[4,16,1024]{2,1,0:T(8,128)(2,1)S(1)} %pad_maximum_fusion.1.refs_0_.refs_1_), channel_id=1, source_target_pairs={{0,2},{2,0},{4,6},{6,4},{8,10},{10,8},{12,14},{14,12},{16,18},{18,... | collective-permute-start | bytes 393224 | tf_op jit(solution)/shard_map/ppermute | solution.py:325
  70.2 1.2 collective-permute-start.20
  71.9 6.4 %collective-permute-start.21 = (bf16[4,16,1024]{2,1,0:T(8,128)(2,1)S(1)}, bf16[4,16,1024]{2,1,0:T(8,128)(2,1)S(1)}, u32[]{:S(2)}, u32[]{:S(2)}) collective-permute-start(bf16[4,16,1024]{2,1,0:T(8,128)(2,1)S(1)} %get-tuple-element.43), channel_id=1, source_target_pairs={{0,2},{2,0},{4,6},{6,4},{8,10},{10,8},{12,14},{14,12},{16,18},{18,... | collective-permute-start | bytes 393224 | tf_op jit(solution)/shard_map/ppermute | solution.py:325
  73.0 8.1 %collective-permute-start.22 = (bf16[4,16,1024]{2,1,0:T(8,128)(2,1)S(1)}, bf16[4,16,1024]{2,1,0:T(8,128)(2,1)S(1)}, u32[]{:S(2)}, u32[]{:S(2)}) collective-permute-start(bf16[4,16,1024]{2,1,0:T(8,128)(2,1)S(1)} %get-tuple-element.44), channel_id=1, source_target_pairs={{0,4},{2,6},{4,0},{6,2},{8,12},{10,14},{12,8},{14,10},{16,20},{18,... | collective-permute-start | bytes 393224 | tf_op jit(solution)/shard_map/ppermute | solution.py:325
  73.8 7.3 %collective-permute-start.23 = (bf16[4,16,1024]{2,1,0:T(8,128)(2,1)S(1)}, bf16[4,16,1024]{2,1,0:T(8,128)(2,1)S(1)}, u32[]{:S(2)}, u32[]{:S(2)}) collective-permute-start(bf16[4,16,1024]{2,1,0:T(8,128)(2,1)S(1)} %get-tuple-element.45), channel_id=1, source_target_pairs={{0,6},{2,4},{4,2},{6,0},{8,14},{10,12},{12,10},{14,8},{16,22},{18,... | collective-permute-start | bytes 393224 | tf_op jit(solution)/shard_map/ppermute | solution.py:325
  81.2 5.8 %collective-permute-start.24 = (bf16[16,1024]{1,0:T(8,128)(2,1)S(1)}, bf16[16,1024]{1,0:T(8,128)(2,1)S(1)}, u32[]{:S(2)}, u32[]{:S(2)}) collective-permute-start(bf16[16,1024]{1,0:T(8,128)(2,1)S(1)} %get-tuple-element.47), channel_id=1, source_target_pairs={{0,24},{2,26},{4,28},{6,30},{8,16},{10,18},{12,20},{14,22},{16,8},... | collective-permute-start | bytes 98312 | tf_op jit(solution)/shard_map/ppermute | solution.py:325
  83.7 3.9 %collective-permute-start.25 = (bf16[16,1024]{1,0:T(8,128)(2,1)S(1)}, bf16[16,1024]{1,0:T(8,128)(2,1)S(1)}, u32[]{:S(2)}, u32[]{:S(2)}) collective-permute-start(bf16[16,1024]{1,0:T(8,128)(2,1)S(1)} %get-tuple-element.48), channel_id=1, source_target_pairs={{0,8},{2,10},{4,12},{6,14},{8,0},{10,2},{12,4},{14,6},{16,24},{18,... | collective-permute-start | bytes 98312 | tf_op jit(solution)/shard_map/ppermute | solution.py:325
  83.8 4.8 %collective-permute-start.26 = (bf16[16,1024]{1,0:T(8,128)(2,1)S(1)}, bf16[16,1024]{1,0:T(8,128)(2,1)S(1)}, u32[]{:S(2)}, u32[]{:S(2)}) collective-permute-start(bf16[16,1024]{1,0:T(8,128)(2,1)S(1)} %get-tuple-element.49), channel_id=1, source_target_pairs={{0,16},{2,18},{4,20},{6,22},{8,24},{10,26},{12,28},{14,30},{16,0},... | collective-permute-start | bytes 98312 | tf_op jit(solution)/shard_map/ppermute | solution.py:325
  101.4 1.3 collective-permute-start.27
  103.3 5.4 %collective-permute-start.30 = (bf16[16,1024]{1,0:T(8,128)(2,1)S(1)}, bf16[16,1024]{1,0:T(8,128)(2,1)S(1)}, u32[]{:S(2)}, u32[]{:S(2)}) collective-permute-start(bf16[16,1024]{1,0:T(8,128)(2,1)S(1)} %get-tuple-element.55), channel_id=1, source_target_pairs={{0,16},{2,18},{4,20},{6,22},{8,24},{10,26},{12,28},{14,30},{16,0},... | collective-permute-start | bytes 98312 | tf_op jit(solution)/shard_map/ppermute | solution.py:325
  104.4 4.3 %collective-permute-start.29 = (bf16[16,1024]{1,0:T(8,128)(2,1)S(1)}, bf16[16,1024]{1,0:T(8,128)(2,1)S(1)}, u32[]{:S(2)}, u32[]{:S(2)}) collective-permute-start(bf16[16,1024]{1,0:T(8,128)(2,1)S(1)} %get-tuple-element.55), channel_id=1, source_target_pairs={{0,8},{2,10},{4,12},{6,14},{8,0},{10,2},{12,4},{14,6},{16,24},{18,... | collective-permute-start | bytes 98312 | tf_op jit(solution)/shard_map/ppermute | solution.py:325
  105.7 5.7 %collective-permute-start.28 = (bf16[16,1024]{1,0:T(8,128)(2,1)S(1)}, bf16[16,1024]{1,0:T(8,128)(2,1)S(1)}, u32[]{:S(2)}, u32[]{:S(2)}) collective-permute-start(bf16[16,1024]{1,0:T(8,128)(2,1)S(1)} %get-tuple-element.55), channel_id=1, source_target_pairs={{0,24},{2,26},{4,28},{6,30},{8,16},{10,18},{12,20},{14,22},{16,8},... | collective-permute-start | bytes 98312 | tf_op jit(solution)/shard_map/ppermute | solution.py:325
  111.4 6.5 %collective-permute-start.33 = (bf16[4,16,1024]{2,1,0:T(8,128)(2,1)S(1)}, bf16[4,16,1024]{2,1,0:T(8,128)(2,1)S(1)}, u32[]{:S(2)}, u32[]{:S(2)}) collective-permute-start(bf16[4,16,1024]{2,1,0:T(8,128)(2,1)S(1)} %pad_maximum_fusion.2.refs_0_), channel_id=1, source_target_pairs={{0,6},{2,4},{4,2},{6,0},{8,14},{10,12},{12,10},{14,8},{16,22},{18,... | collective-permute-start | bytes 393224 | tf_op jit(solution)/shard_map/ppermute | solution.py:325
  112.2 6.5 %collective-permute-start.32 = (bf16[4,16,1024]{2,1,0:T(8,128)(2,1)S(1)}, bf16[4,16,1024]{2,1,0:T(8,128)(2,1)S(1)}, u32[]{:S(2)}, u32[]{:S(2)}) collective-permute-start(bf16[4,16,1024]{2,1,0:T(8,128)(2,1)S(1)} %pad_maximum_fusion.2.refs_0_), channel_id=1, source_target_pairs={{0,4},{2,6},{4,0},{6,2},{8,12},{10,14},{12,8},{14,10},{16,20},{18,... | collective-permute-start | bytes 393224 | tf_op jit(solution)/shard_map/ppermute | solution.py:325
  113.5 5.2 %collective-permute-start.31 = (bf16[4,16,1024]{2,1,0:T(8,128)(2,1)S(1)}, bf16[4,16,1024]{2,1,0:T(8,128)(2,1)S(1)}, u32[]{:S(2)}, u32[]{:S(2)}) collective-permute-start(bf16[4,16,1024]{2,1,0:T(8,128)(2,1)S(1)} %pad_maximum_fusion.2.refs_0_), channel_id=1, source_target_pairs={{0,2},{2,0},{4,6},{6,4},{8,10},{10,8},{12,14},{14,12},{16,18},{18,... | collective-permute-start | bytes 393224 | tf_op jit(solution)/shard_map/ppermute | solution.py:325
  119.6 1.2 collective-permute-start.34

commit v2 on v1

--- a/solution.py
+++ b/solution.py
@@ -338,7 +338,7 @@
 
     def gather(block):
         column = jnp.stack([block] + swap_far([block] * len(far_order)))
-        return [column], swap_near([column] * len(near_order))
+        return [column] + swap_near([column] * len(near_order))
 
     def exchange(blocks):
         return lax.all_to_all(blocks, "samp", 0, 0)
@@ -375,10 +375,12 @@
 
         def apply_rows(fields, earlier, base):
             both = base
-            for places, blocks, old in zip((column_places, plane_places), fields, earlier):
+            for part in [0] + list(range(1, near))[::-1]:
+                places = list(range(part * far, (part + 1) * far))
+                old = earlier[part : part + 1]
                 both = call(
                     lambda *refs: rows_body(places, len(old) > 0, *refs),
-                    [((strengths, samples + LANES), single)], *blocks, *old, design, both,
+                    [((strengths, samples + LANES), single)], fields[part], *old, design, both,
                 )[0]
             return feat_parts(both)
 
@@ -392,7 +394,7 @@
         hessian_diag, miss_rows, *outs = call(
             lambda *refs: miss_body(scale, plane_places, *refs),
             [(sample_field, single), (sample_field, half)] + [(column, single)] * (near - 1),
-            *apply_rows(gather(start), ([], []), nothing), labels, design,
+            *apply_rows(gather(start), [], nothing), labels, design,
         )
         folded = call(
             lambda *refs: more_body(scale, column_places, *refs),
@@ -414,7 +416,7 @@
         image_rows, image, known, *outs = call(
             lambda *refs: image_body(plane_places, *refs),
             [(sample_field, single), (sample_field, half), scalars] + [(column, half)] * (near - 1),
-            *apply_rows(whole, ([], []), nothing), hessian_diag, design,
+            *apply_rows(whole, [], nothing), hessian_diag, design,
         )
         own = call(
             lambda *refs: more_body(None, column_places, *refs),

time: 134 us -> 134 us (level)
    pallas_call x17 -> x23, Pallas kernels: 8.29 us -> 8.96 us  [call(): pl.pallas_call(body, out_shape=[jax.ShapeDtypeStruct(shape, dtype) for sh...]
  transfers between devices with their start and end apart: 35 -> 35, of which waited for: 26 -> 27; matrix products, arithmetic and copies ran while one was open for 0% -> 0% of each run, Pallas kernels for 2% -> 4%
where the time goes in v2:
time: 134 us; the launch traced here: 133 us
  starting transfers between devices  41.4 us (31%)
  waiting for transfers between devices  40.8 us (30%)
  blocking collectives  36.9 us (28%)
  Pallas kernels  9.99 us (7%)
  local copies, waits for them, and re-layouts  2.31 us (2%)
  other arithmetic  1.79 us (1%)
    ppermute x30, starting transfers between devices, swap(): lax.ppermute(values, 'samp', [(i, i ^ distance) for i in range(samp)])  41.1 us
    all_to_all x3, blocking collectives, exchange(): return lax.all_to_all(blocks, 'samp', 0, 0)  36.9 us
    ppermute x30, waiting for transfers between devices, swap(): lax.ppermute(values, 'samp', [(i, i ^ distance) for i in range(samp)])  34.9 us
    pallas_call x23, Pallas kernels, call(): pl.pallas_call(body, out_shape=[jax.ShapeDtypeStruct(shape, dtype) for sh...  8.96 us
    ppermute x5, waiting for transfers between devices, feat_parts(): return (values, lax.ppermute(values, 'feat', [(0, 1), (1, 0)]))  5.87 us
  transfers between devices with their start and end apart: 35, of which 27 were waited for; matrix products, arithmetic and copies ran while one was open for 0% of the time, Pallas kernels for 4%

profile of v2, /device:TPU:0, one launch (start us, length us, event | category | flops | bytes accessed | tf_op | source)
XLA Modules:
  0.0 133.3 jit_solution(9293466050069598054)
XLA Ops:
  0.0 0.8 convert_element_type.48
  0.8 4.1 %collective-permute-start.2 = (bf16[16,1024]{1,0:T(8,128)(2,1)S(1)}, bf16[16,1024]{1,0:T(8,128)(2,1)S(1)}, u32[]{:S(2)}, u32[]{:S(2)}) collective-permute-start(bf16[16,1024]{1,0:T(8,128)(2,1)S(1)} %convert_element_type.48), channel_id=1, source_target_pairs={{0,16},{2,18},{4,20},{6,22},{8,24},{10,26},{12,28},{14,30},{16,0},... | collective-permute-start | bytes 98312 | tf_op jit(solution)/shard_map/ppermute | solution.py:325
  4.9 1.6 %collective-permute-start.1 = (bf16[16,1024]{1,0:T(8,128)(2,1)S(1)}, bf16[16,1024]{1,0:T(8,128)(2,1)S(1)}, u32[]{:S(2)}, u32[]{:S(2)}) collective-permute-start(bf16[16,1024]{1,0:T(8,128)(2,1)S(1)} %convert_element_type.48), channel_id=1, source_target_pairs={{0,8},{2,10},{4,12},{6,14},{8,0},{10,2},{12,4},{14,6},{16,24},{18,... | collective-permute-start | bytes 98312 | tf_op jit(solution)/shard_map/ppermute | solution.py:325
  7.3 1.6 %collective-permute-done.1 = bf16[16,1024]{1,0:T(8,128)(2,1)S(1)} collective-permute-done((bf16[16,1024]{1,0:T(8,128)(2,1)S(1)}, bf16[16,1024]{1,0:T(8,128)(2,1)S(1)}, u32[]{:S(2)}, u32[]{:S(2)}) %collective-permute-start.1) | collective-permute-done | bytes 32800 | tf_op jit(solution)/shard_map/ppermute | solution.py:325
  8.8 3.4 %collective-permute-done = bf16[16,1024]{1,0:T(8,128)(2,1)S(1)} collective-permute-done((bf16[16,1024]{1,0:T(8,128)(2,1)S(1)}, bf16[16,1024]{1,0:T(8,128)(2,1)S(1)}, u32[]{:S(2)}, u32[]{:S(2)}) %collective-permute-start) | collective-permute-done | bytes 32800 | tf_op jit(solution)/shard_map/ppermute | solution.py:325
  12.2 2.5 %collective-permute-start.5 = (bf16[4,16,1024]{2,1,0:T(8,128)(2,1)S(1)}, bf16[4,16,1024]{2,1,0:T(8,128)(2,1)S(1)}, u32[]{:S(2)}, u32[]{:S(2)}) collective-permute-start(bf16[4,16,1024]{2,1,0:T(8,128)(2,1)S(1)} %pad_maximum_fusion.refs_0_), channel_id=1, source_target_pairs={{0,6},{2,4},{4,2},{6,0},{8,14},{10,12},{12,10},{14,8},{16,22},{18,... | collective-permute-start | bytes 393224 | tf_op jit(solution)/shard_map/ppermute | solution.py:325
  16.4 2.2 %copy-done.1 = bf16[128,16384]{1,0:T(8,128)(2,1)S(1)} copy-done((bf16[128,16384]{1,0:T(8,128)(2,1)S(1)}, bf16[128,16384]{1,0:T(8,128)(2,1)}, u32[]{:S(2)}) %copy-start.1) | copy-done | bytes 4194328
  18.6 1.0 load.1.refs_1_.refs_3_.refs_2_
  21.3 1.2 collective-permute-done.6.refs_1_
  23.1 2.5 %collective-permute-start.9 = (f16[4,16,1024]{2,1,0:T(8,128)(2,1)S(1)}, f16[4,16,1024]{2,1,0:T(8,128)(2,1)S(1)}, u32[]{:S(2)}, u32[]{:S(2)}) collective-permute-start(f16[4,16,1024]{2,1,0:T(8,128)(2,1)S(1)} %convert_element_type.53), channel_id=1, source_target_pairs={{0,6},{2,4},{4,2},{6,0},{8,14},{10,12},{12,10},{14,8},{16,22},{18,... | collective-permute-start | bytes 393224 | tf_op jit(solution)/shard_map/ppermute | solution.py:325
  26.9 3.1 %collective-permute-done.9 = f16[4,16,1024]{2,1,0:T(8,128)(2,1)S(1)} collective-permute-done((f16[4,16,1024]{2,1,0:T(8,128)(2,1)S(1)}, f16[4,16,1024]{2,1,0:T(8,128)(2,1)S(1)}, u32[]{:S(2)}, u32[]{:S(2)}) %collective-permute-start.9) | collective-permute-done | bytes 131104 | tf_op jit(solution)/shard_map/ppermute | solution.py:325
  30.0 2.5 %collective-permute-done.8 = f16[4,16,1024]{2,1,0:T(8,128)(2,1)S(1)} collective-permute-done((f16[4,16,1024]{2,1,0:T(8,128)(2,1)S(1)}, f16[4,16,1024]{2,1,0:T(8,128)(2,1)S(1)}, u32[]{:S(2)}, u32[]{:S(2)}) %collective-permute-start.8) | collective-permute-done | bytes 131104 | tf_op jit(solution)/shard_map/ppermute | solution.py:325
  33.2 3.9 %collective-permute-start.11 = (f16[16,1024]{1,0:T(8,128)(2,1)S(1)}, f16[16,1024]{1,0:T(8,128)(2,1)S(1)}, u32[]{:S(2)}, u32[]{:S(2)}) collective-permute-start(f16[16,1024]{1,0:T(8,128)(2,1)S(1)} %get-tuple-element.67), channel_id=1, source_target_pairs={{0,8},{2,10},{4,12},{6,14},{8,0},{10,2},{12,4},{14,6},{16,24},{18,... | collective-permute-start | bytes 98312 | tf_op jit(solution)/shard_map/ppermute | solution.py:325
  37.1 1.3 %collective-permute-done.10 = f16[16,1024]{1,0:T(8,128)(2,1)S(1)} collective-permute-done((f16[16,1024]{1,0:T(8,128)(2,1)S(1)}, f16[16,1024]{1,0:T(8,128)(2,1)S(1)}, u32[]{:S(2)}, u32[]{:S(2)}) %collective-permute-start.10) | collective-permute-done | bytes 32800 | tf_op jit(solution)/shard_map/ppermute | solution.py:325
  39.4 12.7 %all_to_all.15 = bf16[16,16,384]{2,1,0:T(8,128)(2,1)S(1)} all-to-all(bf16[16,16,384]{2,1,0:T(8,128)(2,1)S(1)} %get-tuple-element.38), channel_id=1, replica_groups=mesh['samp'=16,'feat'=2] {'samp'}, dimensions={0} | all-to-all | bytes 393216 | tf_op jit(solution)/shard_map/all_to_all | solution.py:344
  52.2 1.2 collective-permute-done.13.other_ref
  53.9 1.1 collective-permute-start.16
  54.9 1.1 collective-permute-start.15
  56.0 2.2 %collective-permute-start.14 = (bf16[16,1024]{1,0:T(8,128)(2,1)S(1)}, bf16[16,1024]{1,0:T(8,128)(2,1)S(1)}, u32[]{:S(2)}, u32[]{:S(2)}) collective-permute-start(bf16[16,1024]{1,0:T(8,128)(2,1)S(1)} %get-tuple-element.40), channel_id=1, source_target_pairs={{0,24},{2,26},{4,28},{6,30},{8,16},{10,18},{12,20},{14,22},{16,8},... | collective-permute-start | bytes 98312 | tf_op jit(solution)/shard_map/ppermute | solution.py:325
  58.3 0.9 collective-permute-done.16
  59.1 2.6 %collective-permute-done.14 = bf16[16,1024]{1,0:T(8,128)(2,1)S(1)} collective-permute-done((bf16[16,1024]{1,0:T(8,128)(2,1)S(1)}, bf16[16,1024]{1,0:T(8,128)(2,1)S(1)}, u32[]{:S(2)}, u32[]{:S(2)}) %collective-permute-start.14) | collective-permute-done | bytes 32800 | tf_op jit(solution)/shard_map/ppermute | solution.py:325
  62.5 1.3 collective-permute-start.18
  63.8 1.5 %collective-permute-start.17 = (bf16[4,16,1024]{2,1,0:T(8,128)(2,1)S(1)}, bf16[4,16,1024]{2,1,0:T(8,128)(2,1)S(1)}, u32[]{:S(2)}, u32[]{:S(2)}) collective-permute-start(bf16[4,16,1024]{2,1,0:T(8,128)(2,1)S(1)} %pad_maximum_fusion.1.refs_0_.refs_1_), channel_id=1, source_target_pairs={{0,2},{2,0},{4,6},{6,4},{8,10},{10,8},{12,14},{14,12},{16,18},{18,... | collective-permute-start | bytes 393224 | tf_op jit(solution)/shard_map/ppermute | solution.py:325
  65.7 2.7 %collective-permute-done.19.refs_0_.refs_1_ = bf16[4,16,1024]{2,1,0:T(8,128)(2,1)S(1)} collective-permute-done((bf16[4,16,1024]{2,1,0:T(8,128)(2,1)S(1)}, bf16[4,16,1024]{2,1,0:T(8,128)(2,1)S(1)}, u32[]{:S(2)}, u32[]{:S(2)}) %collective-permute-start.19) | collective-permute-done | bytes 131104 | tf_op jit(solution)/shard_map/ppermute | solution.py:325
  70.0 1.2 collective-permute-done.20.refs_1_
  71.7 0.9 collective-permute-start.21
  72.6 0.9 collective-permute-start.22
  73.6 1.7 %collective-permute-start.23 = (bf16[4,16,1024]{2,1,0:T(8,128)(2,1)S(1)}, bf16[4,16,1024]{2,1,0:T(8,128)(2,1)S(1)}, u32[]{:S(2)}, u32[]{:S(2)}) collective-permute-start(bf16[4,16,1024]{2,1,0:T(8,128)(2,1)S(1)} %get-tuple-element.45), channel_id=1, source_target_pairs={{0,6},{2,4},{4,2},{6,0},{8,14},{10,12},{12,10},{14,8},{16,22},{18,... | collective-permute-start | bytes 393224 | tf_op jit(solution)/shard_map/ppermute | solution.py:325
  75.5 2.6 %collective-permute-done.21.refs_0_ = bf16[4,16,1024]{2,1,0:T(8,128)(2,1)S(1)} collective-permute-done((bf16[4,16,1024]{2,1,0:T(8,128)(2,1)S(1)}, bf16[4,16,1024]{2,1,0:T(8,128)(2,1)S(1)}, u32[]{:S(2)}, u32[]{:S(2)}) %collective-permute-start.21) | collective-permute-done | bytes 131104 | tf_op jit(solution)/shard_map/ppermute | solution.py:325
  78.7 2.0 %collective-permute-done.23.refs_2_ = bf16[4,16,1024]{2,1,0:T(8,128)(2,1)S(1)} collective-permute-done((bf16[4,16,1024]{2,1,0:T(8,128)(2,1)S(1)}, bf16[4,16,1024]{2,1,0:T(8,128)(2,1)S(1)}, u32[]{:S(2)}, u32[]{:S(2)}) %collective-permute-start.23) | collective-permute-done | bytes 131104 | tf_op jit(solution)/shard_map/ppermute | solution.py:325
  80.8 2.8 %collective-permute-start.24 = (bf16[16,1024]{1,0:T(8,128)(2,1)S(1)}, bf16[16,1024]{1,0:T(8,128)(2,1)S(1)}, u32[]{:S(2)}, u32[]{:S(2)}) collective-permute-start(bf16[16,1024]{1,0:T(8,128)(2,1)S(1)} %get-tuple-element.47), channel_id=1, source_target_pairs={{0,24},{2,26},{4,28},{6,30},{8,16},{10,18},{12,20},{14,22},{16,8},... | collective-permute-start | bytes 98312 | tf_op jit(solution)/shard_map/ppermute | solution.py:325
  83.6 1.6 %collective-permute-start.26 = (bf16[16,1024]{1,0:T(8,128)(2,1)S(1)}, bf16[16,1024]{1,0:T(8,128)(2,1)S(1)}, u32[]{:S(2)}, u32[]{:S(2)}) collective-permute-start(bf16[16,1024]{1,0:T(8,128)(2,1)S(1)} %get-tuple-element.49), channel_id=1, source_target_pairs={{0,16},{2,18},{4,20},{6,22},{8,24},{10,26},{12,28},{14,30},{16,0},... | collective-permute-start | bytes 98312 | tf_op jit(solution)/shard_map/ppermute | solution.py:325
  85.2 1.3 collective-permute-done.24.refs_1_
  86.6 0.9 collective-permute-done.25.refs_2_
  87.5 0.9 collective-permute-done.26.refs_3_
  88.7 12.5 %all_to_all.16 = bf16[16,16,512]{2,1,0:T(8,128)(2,1)S(1)} all-to-all(bf16[16,16,512]{2,1,0:T(8,128)(2,1)S(1)} %get-tuple-element.52), channel_id=1, replica_groups=mesh['samp'=16,'feat'=2] {'samp'}, dimensions={0} | all-to-all | bytes 524288 | tf_op jit(solution)/shard_map/all_to_all | solution.py:344
  101.3 1.2 collective-permute-done.27.other_ref
  103.1 1.1 collective-permute-start.30
  104.2 1.3 collective-permute-start.29
  105.5 2.0 %collective-permute-start.28 = (bf16[16,1024]{1,0:T(8,128)(2,1)S(1)}, bf16[16,1024]{1,0:T(8,128)(2,1)S(1)}, u32[]{:S(2)}, u32[]{:S(2)}) collective-permute-start(bf16[16,1024]{1,0:T(8,128)(2,1)S(1)} %get-tuple-element.55), channel_id=1, source_target_pairs={{0,24},{2,26},{4,28},{6,30},{8,16},{10,18},{12,20},{14,22},{16,8},... | collective-permute-start | bytes 98312 | tf_op jit(solution)/shard_map/ppermute | solution.py:325
  107.5 1.0 collective-permute-done.30
  108.5 2.7 %collective-permute-done.28 = bf16[16,1024]{1,0:T(8,128)(2,1)S(1)} collective-permute-done((bf16[16,1024]{1,0:T(8,128)(2,1)S(1)}, bf16[16,1024]{1,0:T(8,128)(2,1)S(1)}, u32[]{:S(2)}, u32[]{:S(2)}) %collective-permute-start.28) | collective-permute-done | bytes 32800 | tf_op jit(solution)/shard_map/ppermute | solution.py:325
  112.0 1.3 collective-permute-start.32
  113.3 1.5 %collective-permute-start.31 = (bf16[4,16,1024]{2,1,0:T(8,128)(2,1)S(1)}, bf16[4,16,1024]{2,1,0:T(8,128)(2,1)S(1)}, u32[]{:S(2)}, u32[]{:S(2)}) collective-permute-start(bf16[4,16,1024]{2,1,0:T(8,128)(2,1)S(1)} %pad_maximum_fusion.2.refs_0_), channel_id=1, source_target_pairs={{0,2},{2,0},{4,6},{6,4},{8,10},{10,8},{12,14},{14,12},{16,18},{18,... | collective-permute-start | bytes 393224 | tf_op jit(solution)/shard_map/ppermute | solution.py:325
  115.2 2.5 %collective-permute-done.33.refs_0_ = bf16[4,16,1024]{2,1,0:T(8,128)(2,1)S(1)} collective-permute-done((bf16[4,16,1024]{2,1,0:T(8,128)(2,1)S(1)}, bf16[4,16,1024]{2,1,0:T(8,128)(2,1)S(1)}, u32[]{:S(2)}, u32[]{:S(2)}) %collective-permute-start.33) | collective-permute-done | bytes 131104 | tf_op jit(solution)/shard_map/ppermute | solution.py:325
  119.4 1.2 collective-permute-done.34.other_ref
  120.6 11.6 %all_to_all.17.received_ref = f32[16,8,128]{2,1,0:T(8,128)S(1)} all-to-all(f32[16,8,128]{2,1,0:T(8,128)S(1)} %get-tuple-element.58), channel_id=1, replica_groups=mesh['samp'=16,'feat'=2] {'samp'}, dimensions={0} | all-to-all | bytes 131072 | tf_op jit(solution)/shard_map/all_to_all | solution.py:344
  132.3 1.1 shard_map.95
  (77 shorter events, 16.3 us)
Async XLA Ops:
  0.8 6.4 %collective-permute-start.2 = (bf16[16,1024]{1,0:T(8,128)(2,1)S(1)}, bf16[16,1024]{1,0:T(8,128)(2,1)S(1)}, u32[]{:S(2)}, u32[]{:S(2)}) collective-permute-start(bf16[16,1024]{1,0:T(8,128)(2,1)S(1)} %convert_element_type.48), channel_id=1, source_target_pairs={{0,16},{2,18},{4,20},{6,22},{8,24},{10,26},{12,28},{14,30},{16,0},... | collective-permute-start | bytes 98312 | tf_op jit(solution)/shard_map/ppermute | solution.py:325
  4.9 3.9 %collective-permute-start.1 = (bf16[16,1024]{1,0:T(8,128)(2,1)S(1)}, bf16[16,1024]{1,0:T(8,128)(2,1)S(1)}, u32[]{:S(2)}, u32[]{:S(2)}) collective-permute-start(bf16[16,1024]{1,0:T(8,128)(2,1)S(1)} %convert_element_type.48), channel_id=1, source_target_pairs={{0,8},{2,10},{4,12},{6,14},{8,0},{10,2},{12,4},{14,6},{16,24},{18,... | collective-permute-start | bytes 98312 | tf_op jit(solution)/shard_map/ppermute | solution.py:325
  6.5 5.7 %collective-permute-start = (bf16[16,1024]{1,0:T(8,128)(2,1)S(1)}, bf16[16,1024]{1,0:T(8,128)(2,1)S(1)}, u32[]{:S(2)}, u32[]{:S(2)}) collective-permute-start(bf16[16,1024]{1,0:T(8,128)(2,1)S(1)} %convert_element_type.48), channel_id=1, source_target_pairs={{0,24},{2,26},{4,28},{6,30},{8,16},{10,18},{12,20},{14,22},{16,8},... | collective-permute-start | bytes 98312 | tf_op jit(solution)/shard_map/ppermute | solution.py:325
  12.2 7.8 %collective-permute-start.5 = (bf16[4,16,1024]{2,1,0:T(8,128)(2,1)S(1)}, bf16[4,16,1024]{2,1,0:T(8,128)(2,1)S(1)}, u32[]{:S(2)}, u32[]{:S(2)}) collective-permute-start(bf16[4,16,1024]{2,1,0:T(8,128)(2,1)S(1)} %pad_maximum_fusion.refs_0_), channel_id=1, source_target_pairs={{0,6},{2,4},{4,2},{6,0},{8,14},{10,12},{12,10},{14,8},{16,22},{18,... | collective-permute-start | bytes 393224 | tf_op jit(solution)/shard_map/ppermute | solution.py:325
  14.7 5.7 %collective-permute-start.4 = (bf16[4,16,1024]{2,1,0:T(8,128)(2,1)S(1)}, bf16[4,16,1024]{2,1,0:T(8,128)(2,1)S(1)}, u32[]{:S(2)}, u32[]{:S(2)}) collective-permute-start(bf16[4,16,1024]{2,1,0:T(8,128)(2,1)S(1)} %pad_maximum_fusion.refs_0_), channel_id=1, source_target_pairs={{0,4},{2,6},{4,0},{6,2},{8,12},{10,14},{12,8},{14,10},{16,20},{18,... | collective-permute-start | bytes 393224 | tf_op jit(solution)/shard_map/ppermute | solution.py:325
  15.2 5.6 %collective-permute-start.3 = (bf16[4,16,1024]{2,1,0:T(8,128)(2,1)S(1)}, bf16[4,16,1024]{2,1,0:T(8,128)(2,1)S(1)}, u32[]{:S(2)}, u32[]{:S(2)}) collective-permute-start(bf16[4,16,1024]{2,1,0:T(8,128)(2,1)S(1)} %pad_maximum_fusion.refs_0_), channel_id=1, source_target_pairs={{0,2},{2,0},{4,6},{6,4},{8,10},{10,8},{12,14},{14,12},{16,18},{18,... | collective-permute-start | bytes 393224 | tf_op jit(solution)/shard_map/ppermute | solution.py:325
  16.4 2.2 %copy-start.1 = (bf16[128,16384]{1,0:T(8,128)(2,1)S(1)}, bf16[128,16384]{1,0:T(8,128)(2,1)}, u32[]{:S(2)}) copy-start(bf16[128,16384]{1,0:T(8,128)(2,1)} %design_ref.1) | copy-start | bytes 12582916
  20.4 2.0 %copy-start.3 = (s32[128]{0:T(128)S(1)}, s32[128]{0:T(128)}, u32[]{:S(2)}) copy-start(s32[128]{0:T(128)} %param.8) | copy-start | bytes 1540
  21.2 1.2 collective-permute-start.6
  23.0 16.0 %copy-start.5 = (f32[16]{0:T(128)S(1)}, f32[16]{0:T(128)}, u32[]{:S(2)}) copy-start(f32[16]{0:T(128)} %param.10) | copy-start | bytes 196
  23.0 16.1 %copy-start = (bf16[1024,384]{1,0:T(8,128)(2,1)S(1)}, bf16[1024,384]{1,0:T(8,128)(2,1)}, u32[]{:S(2)}) copy-start(bf16[1024,384]{1,0:T(8,128)(2,1)} %sketch_ref.5) | copy-start | bytes 2359300
  23.0 16.1 %copy-start.2 = (f32[16,1024]{1,0:T(8,128)S(1)}, f32[16,1024]{1,0:T(8,128)}, u32[]{:S(2)}) copy-start(f32[16,1024]{1,0:T(8,128)} %weights_ref.3) | copy-start | bytes 196612
  23.0 29.2 %copy-start.4 = (f32[384]{0:T(512)S(1)}, f32[384]{0:T(512)}, u32[]{:S(2)}) copy-start(f32[384]{0:T(512)} %param.12) | copy-start | bytes 4612
  23.1 6.9 %collective-permute-start.9 = (f16[4,16,1024]{2,1,0:T(8,128)(2,1)S(1)}, f16[4,16,1024]{2,1,0:T(8,128)(2,1)S(1)}, u32[]{:S(2)}, u32[]{:S(2)}) collective-permute-start(f16[4,16,1024]{2,1,0:T(8,128)(2,1)S(1)} %convert_element_type.53), channel_id=1, source_target_pairs={{0,6},{2,4},{4,2},{6,0},{8,14},{10,12},{12,10},{14,8},{16,22},{18,... | collective-permute-start | bytes 393224 | tf_op jit(solution)/shard_map/ppermute | solution.py:325
  25.6 6.8 %collective-permute-start.8 = (f16[4,16,1024]{2,1,0:T(8,128)(2,1)S(1)}, f16[4,16,1024]{2,1,0:T(8,128)(2,1)S(1)}, u32[]{:S(2)}, u32[]{:S(2)}) collective-permute-start(f16[4,16,1024]{2,1,0:T(8,128)(2,1)S(1)} %convert_element_type.51), channel_id=1, source_target_pairs={{0,4},{2,6},{4,0},{6,2},{8,12},{10,14},{12,8},{14,10},{16,20},{18,... | collective-permute-start | bytes 393224 | tf_op jit(solution)/shard_map/ppermute | solution.py:325
  26.1 6.4 %collective-permute-start.7 = (f16[4,16,1024]{2,1,0:T(8,128)(2,1)S(1)}, f16[4,16,1024]{2,1,0:T(8,128)(2,1)S(1)}, u32[]{:S(2)}, u32[]{:S(2)}) collective-permute-start(f16[4,16,1024]{2,1,0:T(8,128)(2,1)S(1)} %convert_element_type.49), channel_id=1, source_target_pairs={{0,2},{2,0},{4,6},{6,4},{8,10},{10,8},{12,14},{14,12},{16,18},{18,... | collective-permute-start | bytes 393224 | tf_op jit(solution)/shard_map/ppermute | solution.py:325
  32.6 5.8 %collective-permute-start.10 = (f16[16,1024]{1,0:T(8,128)(2,1)S(1)}, f16[16,1024]{1,0:T(8,128)(2,1)S(1)}, u32[]{:S(2)}, u32[]{:S(2)}) collective-permute-start(f16[16,1024]{1,0:T(8,128)(2,1)S(1)} %get-tuple-element.65), channel_id=1, source_target_pairs={{0,24},{2,26},{4,28},{6,30},{8,16},{10,18},{12,20},{14,22},{16,8},... | collective-permute-start | bytes 98312 | tf_op jit(solution)/shard_map/ppermute | solution.py:325
  33.0 5.4 %collective-permute-start.12 = (f16[16,1024]{1,0:T(8,128)(2,1)S(1)}, f16[16,1024]{1,0:T(8,128)(2,1)S(1)}, u32[]{:S(2)}, u32[]{:S(2)}) collective-permute-start(f16[16,1024]{1,0:T(8,128)(2,1)S(1)} %get-tuple-element.66), channel_id=1, source_target_pairs={{0,16},{2,18},{4,20},{6,22},{8,24},{10,26},{12,28},{14,30},{16,0},... | collective-permute-start | bytes 98312 | tf_op jit(solution)/shard_map/ppermute | solution.py:325
  33.2 5.8 %collective-permute-start.11 = (f16[16,1024]{1,0:T(8,128)(2,1)S(1)}, f16[16,1024]{1,0:T(8,128)(2,1)S(1)}, u32[]{:S(2)}, u32[]{:S(2)}) collective-permute-start(f16[16,1024]{1,0:T(8,128)(2,1)S(1)} %get-tuple-element.67), channel_id=1, source_target_pairs={{0,8},{2,10},{4,12},{6,14},{8,0},{10,2},{12,4},{14,6},{16,24},{18,... | collective-permute-start | bytes 98312 | tf_op jit(solution)/shard_map/ppermute | solution.py:325
  52.1 1.3 collective-permute-start.13
  53.9 5.3 %collective-permute-start.16 = (bf16[16,1024]{1,0:T(8,128)(2,1)S(1)}, bf16[16,1024]{1,0:T(8,128)(2,1)S(1)}, u32[]{:S(2)}, u32[]{:S(2)}) collective-permute-start(bf16[16,1024]{1,0:T(8,128)(2,1)S(1)} %get-tuple-element.40), channel_id=1, source_target_pairs={{0,16},{2,18},{4,20},{6,22},{8,24},{10,26},{12,28},{14,30},{16,0},... | collective-permute-start | bytes 98312 | tf_op jit(solution)/shard_map/ppermute | solution.py:325
  54.9 4.2 %collective-permute-start.15 = (bf16[16,1024]{1,0:T(8,128)(2,1)S(1)}, bf16[16,1024]{1,0:T(8,128)(2,1)S(1)}, u32[]{:S(2)}, u32[]{:S(2)}) collective-permute-start(bf16[16,1024]{1,0:T(8,128)(2,1)S(1)} %get-tuple-element.40), channel_id=1, source_target_pairs={{0,8},{2,10},{4,12},{6,14},{8,0},{10,2},{12,4},{14,6},{16,24},{18,... | collective-permute-start | bytes 98312 | tf_op jit(solution)/shard_map/ppermute | solution.py:325
  56.0 5.7 %collective-permute-start.14 = (bf16[16,1024]{1,0:T(8,128)(2,1)S(1)}, bf16[16,1024]{1,0:T(8,128)(2,1)S(1)}, u32[]{:S(2)}, u32[]{:S(2)}) collective-permute-start(bf16[16,1024]{1,0:T(8,128)(2,1)S(1)} %get-tuple-element.40), channel_id=1, source_target_pairs={{0,24},{2,26},{4,28},{6,30},{8,16},{10,18},{12,20},{14,22},{16,8},... | collective-permute-start | bytes 98312 | tf_op jit(solution)/shard_map/ppermute | solution.py:325
  61.8 6.6 %collective-permute-start.19 = (bf16[4,16,1024]{2,1,0:T(8,128)(2,1)S(1)}, bf16[4,16,1024]{2,1,0:T(8,128)(2,1)S(1)}, u32[]{:S(2)}, u32[]{:S(2)}) collective-permute-start(bf16[4,16,1024]{2,1,0:T(8,128)(2,1)S(1)} %pad_maximum_fusion.1.refs_0_.refs_1_), channel_id=1, source_target_pairs={{0,6},{2,4},{4,2},{6,0},{8,14},{10,12},{12,10},{14,8},{16,22},{18,... | collective-permute-start | bytes 393224 | tf_op jit(solution)/shard_map/ppermute | solution.py:325
  62.5 6.7 %collective-permute-start.18 = (bf16[4,16,1024]{2,1,0:T(8,128)(2,1)S(1)}, bf16[4,16,1024]{2,1,0:T(8,128)(2,1)S(1)}, u32[]{:S(2)}, u32[]{:S(2)}) collective-permute-start(bf16[4,16,1024]{2,1,0:T(8,128)(2,1)S(1)} %pad_maximum_fusion.1.refs_0_.refs_1_), channel_id=1, source_target_pairs={{0,4},{2,6},{4,0},{6,2},{8,12},{10,14},{12,8},{14,10},{16,20},{18,... | collective-permute-start | bytes 393224 | tf_op jit(solution)/shard_map/ppermute | solution.py:325
  63.8 5.8 %collective-permute-start.17 = (bf16[4,16,1024]{2,1,0:T(8,128)(2,1)S(1)}, bf16[4,16,1024]{2,1,0:T(8,128)(2,1)S(1)}, u32[]{:S(2)}, u32[]{:S(2)}) collective-permute-start(bf16[4,16,1024]{2,1,0:T(8,128)(2,1)S(1)} %pad_maximum_fusion.1.refs_0_.refs_1_), channel_id=1, source_target_pairs={{0,2},{2,0},{4,6},{6,4},{8,10},{10,8},{12,14},{14,12},{16,18},{18,... | collective-permute-start | bytes 393224 | tf_op jit(solution)/shard_map/ppermute | solution.py:325
  70.0 1.2 collective-permute-start.20
  71.7 6.4 %collective-permute-start.21 = (bf16[4,16,1024]{2,1,0:T(8,128)(2,1)S(1)}, bf16[4,16,1024]{2,1,0:T(8,128)(2,1)S(1)}, u32[]{:S(2)}, u32[]{:S(2)}) collective-permute-start(bf16[4,16,1024]{2,1,0:T(8,128)(2,1)S(1)} %get-tuple-element.43), channel_id=1, source_target_pairs={{0,2},{2,0},{4,6},{6,4},{8,10},{10,8},{12,14},{14,12},{16,18},{18,... | collective-permute-start | bytes 393224 | tf_op jit(solution)/shard_map/ppermute | solution.py:325
  72.6 6.1 %collective-permute-start.22 = (bf16[4,16,1024]{2,1,0:T(8,128)(2,1)S(1)}, bf16[4,16,1024]{2,1,0:T(8,128)(2,1)S(1)}, u32[]{:S(2)}, u32[]{:S(2)}) collective-permute-start(bf16[4,16,1024]{2,1,0:T(8,128)(2,1)S(1)} %get-tuple-element.44), channel_id=1, source_target_pairs={{0,4},{2,6},{4,0},{6,2},{8,12},{10,14},{12,8},{14,10},{16,20},{18,... | collective-permute-start | bytes 393224 | tf_op jit(solution)/shard_map/ppermute | solution.py:325
  73.6 7.1 %collective-permute-start.23 = (bf16[4,16,1024]{2,1,0:T(8,128)(2,1)S(1)}, bf16[4,16,1024]{2,1,0:T(8,128)(2,1)S(1)}, u32[]{:S(2)}, u32[]{:S(2)}) collective-permute-start(bf16[4,16,1024]{2,1,0:T(8,128)(2,1)S(1)} %get-tuple-element.45), channel_id=1, source_target_pairs={{0,6},{2,4},{4,2},{6,0},{8,14},{10,12},{12,10},{14,8},{16,22},{18,... | collective-permute-start | bytes 393224 | tf_op jit(solution)/shard_map/ppermute | solution.py:325
  80.8 5.8 %collective-permute-start.24 = (bf16[16,1024]{1,0:T(8,128)(2,1)S(1)}, bf16[16,1024]{1,0:T(8,128)(2,1)S(1)}, u32[]{:S(2)}, u32[]{:S(2)}) collective-permute-start(bf16[16,1024]{1,0:T(8,128)(2,1)S(1)} %get-tuple-element.47), channel_id=1, source_target_pairs={{0,24},{2,26},{4,28},{6,30},{8,16},{10,18},{12,20},{14,22},{16,8},... | collective-permute-start | bytes 98312 | tf_op jit(solution)/shard_map/ppermute | solution.py:325
  83.6 3.9 %collective-permute-start.25 = (bf16[16,1024]{1,0:T(8,128)(2,1)S(1)}, bf16[16,1024]{1,0:T(8,128)(2,1)S(1)}, u32[]{:S(2)}, u32[]{:S(2)}) collective-permute-start(bf16[16,1024]{1,0:T(8,128)(2,1)S(1)} %get-tuple-element.48), channel_id=1, source_target_pairs={{0,8},{2,10},{4,12},{6,14},{8,0},{10,2},{12,4},{14,6},{16,24},{18,... | collective-permute-start | bytes 98312 | tf_op jit(solution)/shard_map/ppermute | solution.py:325
  83.6 4.8 %collective-permute-start.26 = (bf16[16,1024]{1,0:T(8,128)(2,1)S(1)}, bf16[16,1024]{1,0:T(8,128)(2,1)S(1)}, u32[]{:S(2)}, u32[]{:S(2)}) collective-permute-start(bf16[16,1024]{1,0:T(8,128)(2,1)S(1)} %get-tuple-element.49), channel_id=1, source_target_pairs={{0,16},{2,18},{4,20},{6,22},{8,24},{10,26},{12,28},{14,30},{16,0},... | collective-permute-start | bytes 98312 | tf_op jit(solution)/shard_map/ppermute | solution.py:325
  101.3 1.3 collective-permute-start.27
  103.1 5.4 %collective-permute-start.30 = (bf16[16,1024]{1,0:T(8,128)(2,1)S(1)}, bf16[16,1024]{1,0:T(8,128)(2,1)S(1)}, u32[]{:S(2)}, u32[]{:S(2)}) collective-permute-start(bf16[16,1024]{1,0:T(8,128)(2,1)S(1)} %get-tuple-element.55), channel_id=1, source_target_pairs={{0,16},{2,18},{4,20},{6,22},{8,24},{10,26},{12,28},{14,30},{16,0},... | collective-permute-start | bytes 98312 | tf_op jit(solution)/shard_map/ppermute | solution.py:325
  104.2 4.3 %collective-permute-start.29 = (bf16[16,1024]{1,0:T(8,128)(2,1)S(1)}, bf16[16,1024]{1,0:T(8,128)(2,1)S(1)}, u32[]{:S(2)}, u32[]{:S(2)}) collective-permute-start(bf16[16,1024]{1,0:T(8,128)(2,1)S(1)} %get-tuple-element.55), channel_id=1, source_target_pairs={{0,8},{2,10},{4,12},{6,14},{8,0},{10,2},{12,4},{14,6},{16,24},{18,... | collective-permute-start | bytes 98312 | tf_op jit(solution)/shard_map/ppermute | solution.py:325
  105.5 5.7 %collective-permute-start.28 = (bf16[16,1024]{1,0:T(8,128)(2,1)S(1)}, bf16[16,1024]{1,0:T(8,128)(2,1)S(1)}, u32[]{:S(2)}, u32[]{:S(2)}) collective-permute-start(bf16[16,1024]{1,0:T(8,128)(2,1)S(1)} %get-tuple-element.55), channel_id=1, source_target_pairs={{0,24},{2,26},{4,28},{6,30},{8,16},{10,18},{12,20},{14,22},{16,8},... | collective-permute-start | bytes 98312 | tf_op jit(solution)/shard_map/ppermute | solution.py:325
  111.2 6.5 %collective-permute-start.33 = (bf16[4,16,1024]{2,1,0:T(8,128)(2,1)S(1)}, bf16[4,16,1024]{2,1,0:T(8,128)(2,1)S(1)}, u32[]{:S(2)}, u32[]{:S(2)}) collective-permute-start(bf16[4,16,1024]{2,1,0:T(8,128)(2,1)S(1)} %pad_maximum_fusion.2.refs_0_), channel_id=1, source_target_pairs={{0,6},{2,4},{4,2},{6,0},{8,14},{10,12},{12,10},{14,8},{16,22},{18,... | collective-permute-start | bytes 393224 | tf_op jit(solution)/shard_map/ppermute | solution.py:325
  112.0 6.5 %collective-permute-start.32 = (bf16[4,16,1024]{2,1,0:T(8,128)(2,1)S(1)}, bf16[4,16,1024]{2,1,0:T(8,128)(2,1)S(1)}, u32[]{:S(2)}, u32[]{:S(2)}) collective-permute-start(bf16[4,16,1024]{2,1,0:T(8,128)(2,1)S(1)} %pad_maximum_fusion.2.refs_0_), channel_id=1, source_target_pairs={{0,4},{2,6},{4,0},{6,2},{8,12},{10,14},{12,8},{14,10},{16,20},{18,... | collective-permute-start | bytes 393224 | tf_op jit(solution)/shard_map/ppermute | solution.py:325
  113.3 5.6 %collective-permute-start.31 = (bf16[4,16,1024]{2,1,0:T(8,128)(2,1)S(1)}, bf16[4,16,1024]{2,1,0:T(8,128)(2,1)S(1)}, u32[]{:S(2)}, u32[]{:S(2)}) collective-permute-start(bf16[4,16,1024]{2,1,0:T(8,128)(2,1)S(1)} %pad_maximum_fusion.2.refs_0_), channel_id=1, source_target_pairs={{0,2},{2,0},{4,6},{6,4},{8,10},{10,8},{12,14},{14,12},{16,18},{18,... | collective-permute-start | bytes 393224 | tf_op jit(solution)/shard_map/ppermute | solution.py:325
  119.3 1.2 collective-permute-start.34

commit v3 on v2

--- a/solution.py
+++ b/solution.py
@@ -25,7 +25,7 @@
 def exact_dot(values, other, contract):
     rows = values.shape[0]
     product = lax.dot_general(
-        jnp.concatenate(split(values), axis=0),
+        jnp.concatenate([part.astype(jnp.float32) for part in split(values)], axis=0).astype(jnp.bfloat16),
         other,
         (((1,), (contract,)), ((), ())),
         preferred_element_type=jnp.float32,
@@ -52,19 +52,22 @@
         out_ref[part] = block
 
 
-def load_body(offsets_ref, design_ref, out_ref, sems):
-    parts = offsets_ref.shape[0]
-    width = design_ref.shape[1] // parts
+def load_body(order, *refs):
+    *design_refs, out_ref, sems = refs
+    mine = lax.axis_index("samp")
+    width = design_refs[0].shape[1] // len(order)
     copies = []
-    for part in range(parts):
-        offset = pl.multiple_of(offsets_ref[part], width)
-        copies.append(
-            pltpu.make_async_copy(
-                design_ref.at[:, pl.ds(offset, width)],
-                out_ref.at[:, pl.ds(part * width, width)],
-                sems.at[part],
+    for part, place in enumerate(order):
+        offset = pl.multiple_of(jnp.bitwise_xor(mine, place) * width, width)
+        for index, design_ref in enumerate(design_refs):
+            slot = part * len(design_refs) + index
+            copies.append(
+                pltpu.make_async_copy(
+                    design_ref.at[:, pl.ds(offset, width)],
+                    out_ref.at[:, pl.ds(slot * width, width)],
+                    sems.at[slot],
+                )
             )
-        )
     for copy in copies:
         copy.start()
     for copy in copies:
@@ -299,20 +302,21 @@
         out_shape=[jax.ShapeDtypeStruct(shape, dtype) for shape, dtype in shapes],
         in_specs=[VMEM] * len(operands),
         out_specs=[VMEM] * len(shapes),
-        compiler_params=pltpu.CompilerParams(vmem_limit_bytes=8 << 20),
+        compiler_params=pltpu.CompilerParams(vmem_limit_bytes=24 << 20),
     )(*operands)
 
 
-def load(design, offsets):
+def load(designs, order):
+    rows, block = designs[0].shape
     return pl.pallas_call(
-        load_body,
-        out_shape=pltpu.VMEM(design.shape, design.dtype),
-        in_specs=[pl.BlockSpec(memory_space=pltpu.SMEM), pl.BlockSpec(memory_space=pltpu.HBM)],
+        lambda *refs: load_body(order, *refs),
+        out_shape=pltpu.VMEM((rows, block * len(designs)), designs[0].dtype),
+        in_specs=[pl.BlockSpec(memory_space=pltpu.HBM)] * len(designs),
         out_specs=VMEM,
-        scratch_shapes=[pltpu.SemaphoreType.DMA((offsets.shape[0],))],
+        scratch_shapes=[pltpu.SemaphoreType.DMA((len(order) * len(designs),))],
         compiler_params=pltpu.CompilerParams(vmem_limit_bytes=1 << 20),
         name="load",
-    )(offsets, design)
+    )(*designs)
 
 
 def make_shards(samp, feat):
@@ -343,14 +347,40 @@
     def exchange(blocks):
         return lax.all_to_all(blocks, "samp", 0, 0)
 
+    paired = feat == 2
+
     def feat_parts(values):
-        if feat == 2:
-            return values, lax.ppermute(values, "feat", [(0, 1), (1, 0)])
+        if paired:
+            return values, jnp.zeros_like(values)
         return lax.psum(values, "feat"), jnp.zeros_like(values)
 
+    def partner(values):
+        return lax.ppermute(values, "feat", [(0, 1), (1, 0)])
+
     def shards(design_matrix, labels, weights, lambdas, sketch, sketch_values):
+        if not paired:
+            return solve([design_matrix], labels, weights, lambdas, sketch, sketch_values)
+        core = lax.axis_index("feat")
+        count = weights.shape[0] // 2
+        width = weights.shape[1]
+        mine = lax.dynamic_slice_in_dim(weights, core * count, count, 0)
+        theirs = partner(lax.dynamic_slice_in_dim(weights, (1 - core) * count, count, 0))
+        result = solve(
+            [design_matrix, partner(design_matrix)],
+            labels,
+            jnp.concatenate([mine, theirs], axis=1),
+            lax.dynamic_slice_in_dim(lambdas, core * count, count, 0),
+            jnp.concatenate([sketch, partner(sketch)], axis=0),
+            sketch_values,
+        )
+        kept, other = result[:, :width], partner(result[:, width:])
+        first = jnp.where(core == 0, kept, other)
+        second = jnp.where(core == 0, other, kept)
+        return jnp.concatenate([first, second], axis=0)
+
+    def solve(designs, labels, weights, lambdas, sketch, sketch_values):
         strengths, width = weights.shape
-        samples = design_matrix.shape[0]
+        samples = designs[0].shape[0]
         rank = sketch.shape[1]
         single, half = jnp.float32, jnp.bfloat16
         field = ((strengths, width), single)
@@ -363,12 +393,12 @@
         labels = labels[None, :]
         values = sketch_values[None, :]
         places = [k * near + j for j in [0] + near_order for k in [0] + far_order]
-        places = jnp.bitwise_xor(lax.axis_index("samp"), jnp.array(places, jnp.int32))
         if width % LANES == 0:
-            design = load(design_matrix, places * width)
+            design = load(designs, places)
         else:
-            design = design_matrix.reshape(samples, samp, width)
-            design = jnp.take(design, places, axis=1).reshape(design_matrix.shape)
+            places = jnp.bitwise_xor(lax.axis_index("samp"), jnp.array(places, jnp.int32))
+            design = designs[0].reshape(samples, samp, width)
+            design = jnp.take(design, places, axis=1).reshape(designs[0].shape)
 
         column_places = list(range(far))
         plane_places = list(range(far, samp))

time: 134 us -> 139 us (1.037)
  blocking collectives: 36.9 us -> 23.3 us
  Pallas kernels: 9.99 us -> 16.4 us
  starting transfers between devices: 41.4 us -> 47.7 us
  local copies, waits for them, and re-layouts: 2.31 us -> 8.61 us
    all_to_all x3 -> x2, blocking collectives: 36.9 us -> 23.3 us  [exchange(): return lax.all_to_all(blocks, 'samp', 0, 0)]
    ppermute x30, waiting for transfers between devices: 34.9 us -> 25.6 us  [swap(): lax.ppermute(values, 'samp', [(i, i ^ distance) for i in range(samp)])]
    all_to_all x0 -> x1, waiting for transfers between devices: none -> 7.94 us  [exchange(): return lax.all_to_all(blocks, 'samp', 0, 0)]
    all_to_all x0 -> x1, starting transfers between devices: none -> 5.26 us  [exchange(): return lax.all_to_all(blocks, 'samp', 0, 0)]
    pallas_call x23, Pallas kernels: 8.96 us -> 13.9 us  [call(): pl.pallas_call(body, out_shape=[jax.ShapeDtypeStruct(shape, dtype) for sh...]
    unnamed x12 -> x15, local copies, waits for them, and re-layouts: 2.21 us -> 6.83 us
    ppermute x5 -> x4, waiting for transfers between devices: 5.87 us -> 7.52 us  [partner(): return lax.ppermute(values, 'feat', [(0, 1), (1, 0)])]
    dynamic_slice x0 -> x2, local copies, waits for them, and re-layouts: none -> 1.51 us  [the longest x1 0.78 us: shards(): mine = lax.dynamic_slice_in_dim(weights, core * count, count, 0)]
  transfers between devices with their start and end apart: 35 -> 35, of which waited for: 27 -> 22; matrix products, arithmetic and copies ran while one was open for 0% -> 2% of each run, Pallas kernels for 4% -> 8%
where the time goes in v3:
time: 139 us; the launch traced here: 138 us
  starting transfers between devices  47.7 us (34%)
  waiting for transfers between devices  41 us (29%)
  blocking collectives  23.3 us (17%)
  Pallas kernels  16.4 us (12%)
  local copies, waits for them, and re-layouts  8.61 us (6%)
    ppermute x30, starting transfers between devices, swap(): lax.ppermute(values, 'samp', [(i, i ^ distance) for i in range(samp)])  41.8 us
    ppermute x30, waiting for transfers between devices, swap(): lax.ppermute(values, 'samp', [(i, i ^ distance) for i in range(samp)])  25.6 us
    all_to_all x2, blocking collectives, exchange(): return lax.all_to_all(blocks, 'samp', 0, 0)  23.3 us
    pallas_call x23, Pallas kernels, call(): pl.pallas_call(body, out_shape=[jax.ShapeDtypeStruct(shape, dtype) for sh...  13.9 us
    all_to_all x1, waiting for transfers between devices, exchange(): return lax.all_to_all(blocks, 'samp', 0, 0)  7.94 us
    ppermute x4, waiting for transfers between devices, partner(): return lax.ppermute(values, 'feat', [(0, 1), (1, 0)])  7.52 us
    unnamed x15, local copies, waits for them, and re-layouts  6.83 us
    all_to_all x1, starting transfers between devices, exchange(): return lax.all_to_all(blocks, 'samp', 0, 0)  5.26 us
  transfers between devices with their start and end apart: 35, of which 22 were waited for; matrix products, arithmetic and copies ran while one was open for 2% of the time, Pallas kernels for 8%

profile of v3, /device:TPU:0, one launch (start us, length us, event | category | flops | bytes accessed | tf_op | source)
XLA Modules:
  0.0 138.3 jit_solution(1595158656689227310)
XLA Ops:
  0.5 0.8 constant_dynamic-slice_fusion.1
  1.3 6.3 %collective-permute-done = f32[8,1024]{1,0:T(8,128)S(1)} collective-permute-done((f32[8,1024]{1,0:T(8,128)S(1)}, f32[8,1024]{1,0:T(8,128)S(1)}, u32[]{:S(2)}, u32[]{:S(2)}) %collective-permute-start) | collective-permute-done | bytes 32800 | tf_op jit(solution)/shard_map/ppermute | solution.py:358
  7.6 5.0 %collective-permute-start.1 = (bf16[8,2048]{1,0:T(8,128)(2,1)S(1)}, bf16[8,2048]{1,0:T(8,128)(2,1)S(1)}, u32[]{:S(2)}, u32[]{:S(2)}) collective-permute-start(bf16[8,2048]{1,0:T(8,128)(2,1)S(1)} %fusion.4), channel_id=1, source_target_pairs={{0,24},{2,26},{4,28},{6,30},{8,16},{10,18},{12,20},{14,22},{16,8},... | collective-permute-start | bytes 98312 | tf_op jit(solution)/shard_map/ppermute | solution.py:329
  13.2 0.7 dynamic_slice.11
  14.6 2.0 %collective-permute-done.2 = bf16[8,2048]{1,0:T(8,128)(2,1)S(1)} collective-permute-done((bf16[8,2048]{1,0:T(8,128)(2,1)S(1)}, bf16[8,2048]{1,0:T(8,128)(2,1)S(1)}, u32[]{:S(2)}, u32[]{:S(2)}) %collective-permute-start.2) | collective-permute-done | bytes 32800 | tf_op jit(solution)/shard_map/ppermute | solution.py:329
  16.6 1.1 collective-permute-done.3
  17.8 2.5 %collective-permute-start.7 = (bf16[4,8,2048]{2,1,0:T(8,128)(2,1)S(1)}, bf16[4,8,2048]{2,1,0:T(8,128)(2,1)S(1)}, u32[]{:S(2)}, u32[]{:S(2)}) collective-permute-start(bf16[4,8,2048]{2,1,0:T(8,128)(2,1)S(1)} %pad_maximum_fusion.refs_0_), channel_id=1, source_target_pairs={{0,6},{2,4},{4,2},{6,0},{8,14},{10,12},{12,10},{14,8},{16,22},{18,... | collective-permute-start | bytes 393224 | tf_op jit(solution)/shard_map/ppermute | solution.py:329
  21.3 1.2 constant_dynamic-update-slice_fusion.1
  22.6 2.2 %copy-done.2 = bf16[128,16384]{1,0:T(8,128)(2,1)S(1)} copy-done((bf16[128,16384]{1,0:T(8,128)(2,1)S(1)}, bf16[128,16384]{1,0:T(8,128)(2,1)}, u32[]{:S(2)}) %copy-start.2) | copy-done | bytes 4194328
  24.7 2.5 %load.1.refs_1_.refs_3_.refs_2_ = bf16[128,32768]{1,0:T(8,128)(2,1)S(1)} custom-call(bf16[128,16384]{1,0:T(8,128)(2,1)S(1)} %copy-done.2, bf16[128,16384]{1,0:T(8,128)(2,1)} %collective-permute-done.5.refs_1_), custom_call_target="tpu_custom_call" | custom-call | tf_op jit(solution)/shard_map/load/pallas_call | solution.py:311
  30.0 0.9 shard_map.68
  31.0 2.5 %collective-permute-start.10 = (f16[4,8,2048]{2,1,0:T(8,128)(2,1)S(1)}, f16[4,8,2048]{2,1,0:T(8,128)(2,1)S(1)}, u32[]{:S(2)}, u32[]{:S(2)}) collective-permute-start(f16[4,8,2048]{2,1,0:T(8,128)(2,1)S(1)} %convert_element_type.53), channel_id=1, source_target_pairs={{0,6},{2,4},{4,2},{6,0},{8,14},{10,12},{12,10},{14,8},{16,22},{18,... | collective-permute-start | bytes 393224 | tf_op jit(solution)/shard_map/ppermute | solution.py:329
  35.1 1.8 %collective-permute-done.10 = f16[4,8,2048]{2,1,0:T(8,128)(2,1)S(1)} collective-permute-done((f16[4,8,2048]{2,1,0:T(8,128)(2,1)S(1)}, f16[4,8,2048]{2,1,0:T(8,128)(2,1)S(1)}, u32[]{:S(2)}, u32[]{:S(2)}) %collective-permute-start.10) | collective-permute-done | bytes 131104 | tf_op jit(solution)/shard_map/ppermute | solution.py:329
  36.9 1.6 %collective-permute-done.8 = f16[4,8,2048]{2,1,0:T(8,128)(2,1)S(1)} collective-permute-done((f16[4,8,2048]{2,1,0:T(8,128)(2,1)S(1)}, f16[4,8,2048]{2,1,0:T(8,128)(2,1)S(1)}, u32[]{:S(2)}, u32[]{:S(2)}) %collective-permute-start.8) | collective-permute-done | bytes 131104 | tf_op jit(solution)/shard_map/ppermute | solution.py:329
  39.2 1.2 collective-permute-start.11
  41.1 2.6 %collective-permute-start.13 = (f16[8,2048]{1,0:T(8,128)(2,1)S(1)}, f16[8,2048]{1,0:T(8,128)(2,1)S(1)}, u32[]{:S(2)}, u32[]{:S(2)}) collective-permute-start(f16[8,2048]{1,0:T(8,128)(2,1)S(1)} %get-tuple-element.66), channel_id=1, source_target_pairs={{0,16},{2,18},{4,20},{6,22},{8,24},{10,26},{12,28},{14,30},{16,0},... | collective-permute-start | bytes 98312 | tf_op jit(solution)/shard_map/ppermute | solution.py:329
  43.9 1.2 collective-permute-done.11
  45.0 0.9 collective-permute-done.13
  46.0 1.0 shard_map.70
  47.0 5.3 %all-to-all-start = ((bf16[16,8,384]{2,1,0:T(8,128)(2,1)}), bf16[16,8,384]{2,1,0:T(8,128)(2,1)S(1)}, u32[]{:S(2)}, u32[]{:S(2)}) async-start(bf16[16,8,384]{2,1,0:T(8,128)(2,1)} %get-tuple-element.38), calls=%async_computation | async-start | bytes 196608 | tf_op jit(solution)/shard_map/all_to_all | solution.py:348
  52.3 7.9 %all-to-all-done = bf16[16,8,384]{2,1,0:T(8,128)(2,1)S(1)} async-done(((bf16[16,8,384]{2,1,0:T(8,128)(2,1)}), bf16[16,8,384]{2,1,0:T(8,128)(2,1)S(1)}, u32[]{:S(2)}, u32[]{:S(2)}) %all-to-all-start) | async-done | bytes 98336 | tf_op jit(solution)/shard_map/all_to_all | solution.py:348
  61.0 1.2 collective-permute-start.15
  62.7 2.7 %collective-permute-start.17 = (bf16[8,2048]{1,0:T(8,128)(2,1)S(1)}, bf16[8,2048]{1,0:T(8,128)(2,1)S(1)}, u32[]{:S(2)}, u32[]{:S(2)}) collective-permute-start(bf16[8,2048]{1,0:T(8,128)(2,1)S(1)} %get-tuple-element.40), channel_id=1, source_target_pairs={{0,16},{2,18},{4,20},{6,22},{8,24},{10,26},{12,28},{14,30},{16,0},... | collective-permute-start | bytes 98312 | tf_op jit(solution)/shard_map/ppermute | solution.py:329
  65.4 1.3 collective-permute-done.15
  66.7 0.7 collective-permute-done.17
  68.0 2.1 %collective-permute-start.19 = (bf16[4,8,2048]{2,1,0:T(8,128)(2,1)S(1)}, bf16[4,8,2048]{2,1,0:T(8,128)(2,1)S(1)}, u32[]{:S(2)}, u32[]{:S(2)}) collective-permute-start(bf16[4,8,2048]{2,1,0:T(8,128)(2,1)S(1)} %pad_maximum_fusion.1.refs_0_.refs_1_), channel_id=1, source_target_pairs={{0,4},{2,6},{4,0},{6,2},{8,12},{10,14},{12,8},{14,10},{16,20},{18,... | collective-permute-start | bytes 393224 | tf_op jit(solution)/shard_map/ppermute | solution.py:329
  70.1 1.0 collective-permute-start.18
  71.1 3.4 %copy-done.1 = bf16[128,32768]{1,0:T(8,128)(2,1)S(1)} copy-done((bf16[128,32768]{1,0:T(8,128)(2,1)S(1)}, bf16[128,32768]{1,0:T(8,128)(2,1)}, u32[]{:S(2)}) %copy-start.1) | copy-done | bytes 8388632
  77.1 0.9 shard_map.76
  78.0 2.5 %collective-permute-start.21 = (bf16[4,8,2048]{2,1,0:T(8,128)(2,1)S(1)}, bf16[4,8,2048]{2,1,0:T(8,128)(2,1)S(1)}, u32[]{:S(2)}, u32[]{:S(2)}) collective-permute-start(bf16[4,8,2048]{2,1,0:T(8,128)(2,1)S(1)} %get-tuple-element.43), channel_id=1, source_target_pairs={{0,2},{2,0},{4,6},{6,4},{8,10},{10,8},{12,14},{14,12},{16,18},{18,... | collective-permute-start | bytes 393224 | tf_op jit(solution)/shard_map/ppermute | solution.py:329
  80.9 1.2 collective-permute-start.23
  82.5 1.0 collective-permute-done.21.refs_0_
  83.5 3.4 %collective-permute-done.22.refs_1_ = bf16[4,8,2048]{2,1,0:T(8,128)(2,1)S(1)} collective-permute-done((bf16[4,8,2048]{2,1,0:T(8,128)(2,1)S(1)}, bf16[4,8,2048]{2,1,0:T(8,128)(2,1)S(1)}, u32[]{:S(2)}, u32[]{:S(2)}) %collective-permute-start.22) | collective-permute-done | bytes 131104 | tf_op jit(solution)/shard_map/ppermute | solution.py:329
  87.0 2.7 %collective-permute-start.24 = (bf16[8,2048]{1,0:T(8,128)(2,1)S(1)}, bf16[8,2048]{1,0:T(8,128)(2,1)S(1)}, u32[]{:S(2)}, u32[]{:S(2)}) collective-permute-start(bf16[8,2048]{1,0:T(8,128)(2,1)S(1)} %get-tuple-element.47), channel_id=1, source_target_pairs={{0,24},{2,26},{4,28},{6,30},{8,16},{10,18},{12,20},{14,22},{16,8},... | collective-permute-start | bytes 98312 | tf_op jit(solution)/shard_map/ppermute | solution.py:329
  89.7 1.3 collective-permute-start.25
  91.5 1.7 %collective-permute-done.24.refs_1_ = bf16[8,2048]{1,0:T(8,128)(2,1)S(1)} collective-permute-done((bf16[8,2048]{1,0:T(8,128)(2,1)S(1)}, bf16[8,2048]{1,0:T(8,128)(2,1)S(1)}, u32[]{:S(2)}, u32[]{:S(2)}) %collective-permute-start.24) | collective-permute-done | bytes 32800 | tf_op jit(solution)/shard_map/ppermute | solution.py:329
  93.6 2.5 %collective-permute-done.26.refs_3_ = bf16[8,2048]{1,0:T(8,128)(2,1)S(1)} collective-permute-done((bf16[8,2048]{1,0:T(8,128)(2,1)S(1)}, bf16[8,2048]{1,0:T(8,128)(2,1)S(1)}, u32[]{:S(2)}, u32[]{:S(2)}) %collective-permute-start.26) | collective-permute-done | bytes 32800 | tf_op jit(solution)/shard_map/ppermute | solution.py:329
  96.6 10.9 %all_to_all.15 = bf16[16,8,512]{2,1,0:T(8,128)(2,1)S(1)} all-to-all(bf16[16,8,512]{2,1,0:T(8,128)(2,1)S(1)} %get-tuple-element.52), channel_id=1, replica_groups=mesh['samp'=16,'feat'=2] {'samp'}, dimensions={0} | all-to-all | bytes 262144 | tf_op jit(solution)/shard_map/all_to_all | solution.py:348
  107.5 0.8 shard_map.80
  108.4 1.3 collective-permute-start.27
  110.0 2.8 %collective-permute-start.29 = (bf16[8,2048]{1,0:T(8,128)(2,1)S(1)}, bf16[8,2048]{1,0:T(8,128)(2,1)S(1)}, u32[]{:S(2)}, u32[]{:S(2)}) collective-permute-start(bf16[8,2048]{1,0:T(8,128)(2,1)S(1)} %get-tuple-element.55), channel_id=1, source_target_pairs={{0,16},{2,18},{4,20},{6,22},{8,24},{10,26},{12,28},{14,30},{16,0},... | collective-permute-start | bytes 98312 | tf_op jit(solution)/shard_map/ppermute | solution.py:329
  112.8 1.3 collective-permute-done.27
  114.8 0.9 collective-permute-start.32
  115.7 1.6 %collective-permute-start.31 = (bf16[4,8,2048]{2,1,0:T(8,128)(2,1)S(1)}, bf16[4,8,2048]{2,1,0:T(8,128)(2,1)S(1)}, u32[]{:S(2)}, u32[]{:S(2)}) collective-permute-start(bf16[4,8,2048]{2,1,0:T(8,128)(2,1)S(1)} %pad_maximum_fusion.2.refs_0_), channel_id=1, source_target_pairs={{0,4},{2,6},{4,0},{6,2},{8,12},{10,14},{12,8},{14,10},{16,20},{18,... | collective-permute-start | bytes 393224 | tf_op jit(solution)/shard_map/ppermute | solution.py:329
  117.3 1.1 collective-permute-start.30
  119.1 1.8 %collective-permute-done.32.refs_0_ = bf16[4,8,2048]{2,1,0:T(8,128)(2,1)S(1)} collective-permute-done((bf16[4,8,2048]{2,1,0:T(8,128)(2,1)S(1)}, bf16[4,8,2048]{2,1,0:T(8,128)(2,1)S(1)}, u32[]{:S(2)}, u32[]{:S(2)}) %collective-permute-start.32) | collective-permute-done | bytes 131104 | tf_op jit(solution)/shard_map/ppermute | solution.py:329
  123.5 12.4 %all_to_all.16.received_ref = f32[16,8,128]{2,1,0:T(8,128)S(1)} all-to-all(f32[16,8,128]{2,1,0:T(8,128)S(1)} %get-tuple-element.58), channel_id=1, replica_groups=mesh['samp'=16,'feat'=2] {'samp'}, dimensions={0} | all-to-all | bytes 131072 | tf_op jit(solution)/shard_map/all_to_all | solution.py:348
  136.4 1.2 collective-permute-done.33
  (89 shorter events, 20.7 us)
Async XLA Ops:
  0.0 22.5 %collective-permute-start.5 = (bf16[128,16384]{1,0:T(8,128)(2,1)}, bf16[128,16384]{1,0:T(8,128)(2,1)}, u32[]{:S(2)}, u32[]{:S(2)}) collective-permute-start(bf16[128,16384]{1,0:T(8,128)(2,1)} %refs_0_.1), channel_id=1, source_target_pairs={{0,1},{1,0},{2,3},{3,2},{4,5},{5,4},{6,7},{7,6},{8,9},{9,8},{10,11... | collective-permute-start | bytes 12582920 | tf_op jit(solution)/shard_map/ppermute | solution.py:358
  1.3 6.3 %collective-permute-start = (f32[8,1024]{1,0:T(8,128)S(1)}, f32[8,1024]{1,0:T(8,128)S(1)}, u32[]{:S(2)}, u32[]{:S(2)}) collective-permute-start(f32[8,1024]{1,0:T(8,128)S(1)} %get-tuple-element.71), channel_id=1, source_target_pairs={{0,1},{1,0},{2,3},{3,2},{4,5},{5,4},{6,7},{7,6},{8,9},{9,8},{10,11... | collective-permute-start | bytes 98312 | tf_op jit(solution)/shard_map/ppermute | solution.py:358
  7.6 7.0 %collective-permute-start.1 = (bf16[8,2048]{1,0:T(8,128)(2,1)S(1)}, bf16[8,2048]{1,0:T(8,128)(2,1)S(1)}, u32[]{:S(2)}, u32[]{:S(2)}) collective-permute-start(bf16[8,2048]{1,0:T(8,128)(2,1)S(1)} %fusion.4), channel_id=1, source_target_pairs={{0,24},{2,26},{4,28},{6,30},{8,16},{10,18},{12,20},{14,22},{16,8},... | collective-permute-start | bytes 98312 | tf_op jit(solution)/shard_map/ppermute | solution.py:329
  12.6 4.1 %collective-permute-start.2 = (bf16[8,2048]{1,0:T(8,128)(2,1)S(1)}, bf16[8,2048]{1,0:T(8,128)(2,1)S(1)}, u32[]{:S(2)}, u32[]{:S(2)}) collective-permute-start(bf16[8,2048]{1,0:T(8,128)(2,1)S(1)} %fusion.4), channel_id=1, source_target_pairs={{0,8},{2,10},{4,12},{6,14},{8,0},{10,2},{12,4},{14,6},{16,24},{18,... | collective-permute-start | bytes 98312 | tf_op jit(solution)/shard_map/ppermute | solution.py:329
  12.6 5.2 %collective-permute-start.3 = (bf16[8,2048]{1,0:T(8,128)(2,1)S(1)}, bf16[8,2048]{1,0:T(8,128)(2,1)S(1)}, u32[]{:S(2)}, u32[]{:S(2)}) collective-permute-start(bf16[8,2048]{1,0:T(8,128)(2,1)S(1)} %fusion.4), channel_id=1, source_target_pairs={{0,16},{2,18},{4,20},{6,22},{8,24},{10,26},{12,28},{14,30},{16,0},... | collective-permute-start | bytes 98312 | tf_op jit(solution)/shard_map/ppermute | solution.py:329
  13.2 30.5 %collective-permute-start.14 = (bf16[1024,384]{1,0:T(8,128)(2,1)}, bf16[1024,384]{1,0:T(8,128)(2,1)S(1)}, u32[]{:S(2)}, u32[]{:S(2)}) collective-permute-start(bf16[1024,384]{1,0:T(8,128)(2,1)} %param.10), channel_id=1, source_target_pairs={{0,1},{1,0},{2,3},{3,2},{4,5},{5,4},{6,7},{7,6},{8,9},{9,8},{10,11... | collective-permute-start | bytes 2359304 | tf_op jit(solution)/shard_map/ppermute | solution.py:358
  17.8 10.2 %collective-permute-start.7 = (bf16[4,8,2048]{2,1,0:T(8,128)(2,1)S(1)}, bf16[4,8,2048]{2,1,0:T(8,128)(2,1)S(1)}, u32[]{:S(2)}, u32[]{:S(2)}) collective-permute-start(bf16[4,8,2048]{2,1,0:T(8,128)(2,1)S(1)} %pad_maximum_fusion.refs_0_), channel_id=1, source_target_pairs={{0,6},{2,4},{4,2},{6,0},{8,14},{10,12},{12,10},{14,8},{16,22},{18,... | collective-permute-start | bytes 393224 | tf_op jit(solution)/shard_map/ppermute | solution.py:329
  20.3 8.3 %collective-permute-start.6 = (bf16[4,8,2048]{2,1,0:T(8,128)(2,1)S(1)}, bf16[4,8,2048]{2,1,0:T(8,128)(2,1)S(1)}, u32[]{:S(2)}, u32[]{:S(2)}) collective-permute-start(bf16[4,8,2048]{2,1,0:T(8,128)(2,1)S(1)} %pad_maximum_fusion.refs_0_), channel_id=1, source_target_pairs={{0,4},{2,6},{4,0},{6,2},{8,12},{10,14},{12,8},{14,10},{16,20},{18,... | collective-permute-start | bytes 393224 | tf_op jit(solution)/shard_map/ppermute | solution.py:329
  20.8 8.5 %collective-permute-start.4 = (bf16[4,8,2048]{2,1,0:T(8,128)(2,1)S(1)}, bf16[4,8,2048]{2,1,0:T(8,128)(2,1)S(1)}, u32[]{:S(2)}, u32[]{:S(2)}) collective-permute-start(bf16[4,8,2048]{2,1,0:T(8,128)(2,1)S(1)} %pad_maximum_fusion.refs_0_), channel_id=1, source_target_pairs={{0,2},{2,0},{4,6},{6,4},{8,10},{10,8},{12,14},{14,12},{16,18},{18,... | collective-permute-start | bytes 393224 | tf_op jit(solution)/shard_map/ppermute | solution.py:329
  22.6 2.2 %copy-start.2 = (bf16[128,16384]{1,0:T(8,128)(2,1)S(1)}, bf16[128,16384]{1,0:T(8,128)(2,1)}, u32[]{:S(2)}) copy-start(bf16[128,16384]{1,0:T(8,128)(2,1)} %refs_0_.1) | copy-start | bytes 12582916
  27.3 7.4 %copy-start = (bf16[128,32768]{1,0:T(8,128)(2,1)}, bf16[128,32768]{1,0:T(8,128)(2,1)S(1)}, u32[]{:S(2)}) copy-start(bf16[128,32768]{1,0:T(8,128)(2,1)S(1)} %load.1.refs_1_.refs_3_.refs_2_) | copy-start | bytes 25165828
  29.3 0.7 copy-start.3
  31.0 5.9 %collective-permute-start.10 = (f16[4,8,2048]{2,1,0:T(8,128)(2,1)S(1)}, f16[4,8,2048]{2,1,0:T(8,128)(2,1)S(1)}, u32[]{:S(2)}, u32[]{:S(2)}) collective-permute-start(f16[4,8,2048]{2,1,0:T(8,128)(2,1)S(1)} %convert_element_type.53), channel_id=1, source_target_pairs={{0,6},{2,4},{4,2},{6,0},{8,14},{10,12},{12,10},{14,8},{16,22},{18,... | collective-permute-start | bytes 393224 | tf_op jit(solution)/shard_map/ppermute | solution.py:329
  33.5 5.0 %collective-permute-start.8 = (f16[4,8,2048]{2,1,0:T(8,128)(2,1)S(1)}, f16[4,8,2048]{2,1,0:T(8,128)(2,1)S(1)}, u32[]{:S(2)}, u32[]{:S(2)}) collective-permute-start(f16[4,8,2048]{2,1,0:T(8,128)(2,1)S(1)} %convert_element_type.49), channel_id=1, source_target_pairs={{0,2},{2,0},{4,6},{6,4},{8,10},{10,8},{12,14},{14,12},{16,18},{18,... | collective-permute-start | bytes 393224 | tf_op jit(solution)/shard_map/ppermute | solution.py:329
  34.1 5.0 %collective-permute-start.9 = (f16[4,8,2048]{2,1,0:T(8,128)(2,1)S(1)}, f16[4,8,2048]{2,1,0:T(8,128)(2,1)S(1)}, u32[]{:S(2)}, u32[]{:S(2)}) collective-permute-start(f16[4,8,2048]{2,1,0:T(8,128)(2,1)S(1)} %convert_element_type.51), channel_id=1, source_target_pairs={{0,4},{2,6},{4,0},{6,2},{8,12},{10,14},{12,8},{14,10},{16,20},{18,... | collective-permute-start | bytes 393224 | tf_op jit(solution)/shard_map/ppermute | solution.py:329
  39.2 5.8 %collective-permute-start.11 = (f16[8,2048]{1,0:T(8,128)(2,1)S(1)}, f16[8,2048]{1,0:T(8,128)(2,1)S(1)}, u32[]{:S(2)}, u32[]{:S(2)}) collective-permute-start(f16[8,2048]{1,0:T(8,128)(2,1)S(1)} %get-tuple-element.65), channel_id=1, source_target_pairs={{0,24},{2,26},{4,28},{6,30},{8,16},{10,18},{12,20},{14,22},{16,8},... | collective-permute-start | bytes 98312 | tf_op jit(solution)/shard_map/ppermute | solution.py:329
  40.4 4.6 %collective-permute-start.12 = (f16[8,2048]{1,0:T(8,128)(2,1)S(1)}, f16[8,2048]{1,0:T(8,128)(2,1)S(1)}, u32[]{:S(2)}, u32[]{:S(2)}) collective-permute-start(f16[8,2048]{1,0:T(8,128)(2,1)S(1)} %get-tuple-element.67), channel_id=1, source_target_pairs={{0,8},{2,10},{4,12},{6,14},{8,0},{10,2},{12,4},{14,6},{16,24},{18,... | collective-permute-start | bytes 98312 | tf_op jit(solution)/shard_map/ppermute | solution.py:329
  41.1 11.2 %copy-start.4 = (f32[384]{0:T(512)S(1)}, f32[384]{0:T(512)}, u32[]{:S(2)}) copy-start(f32[384]{0:T(512)} %param.11) | copy-start | bytes 4612
  41.1 4.8 %collective-permute-start.13 = (f16[8,2048]{1,0:T(8,128)(2,1)S(1)}, f16[8,2048]{1,0:T(8,128)(2,1)S(1)}, u32[]{:S(2)}, u32[]{:S(2)}) collective-permute-start(f16[8,2048]{1,0:T(8,128)(2,1)S(1)} %get-tuple-element.66), channel_id=1, source_target_pairs={{0,16},{2,18},{4,20},{6,22},{8,24},{10,26},{12,28},{14,30},{16,0},... | collective-permute-start | bytes 98312 | tf_op jit(solution)/shard_map/ppermute | solution.py:329
  47.0 13.2 %all-to-all-start = ((bf16[16,8,384]{2,1,0:T(8,128)(2,1)}), bf16[16,8,384]{2,1,0:T(8,128)(2,1)S(1)}, u32[]{:S(2)}, u32[]{:S(2)}) async-start(bf16[16,8,384]{2,1,0:T(8,128)(2,1)} %get-tuple-element.38), calls=%async_computation | async-start | bytes 196608 | tf_op jit(solution)/shard_map/all_to_all | solution.py:348
  61.0 5.8 %collective-permute-start.15 = (bf16[8,2048]{1,0:T(8,128)(2,1)S(1)}, bf16[8,2048]{1,0:T(8,128)(2,1)S(1)}, u32[]{:S(2)}, u32[]{:S(2)}) collective-permute-start(bf16[8,2048]{1,0:T(8,128)(2,1)S(1)} %get-tuple-element.40), channel_id=1, source_target_pairs={{0,24},{2,26},{4,28},{6,30},{8,16},{10,18},{12,20},{14,22},{16,8},... | collective-permute-start | bytes 98312 | tf_op jit(solution)/shard_map/ppermute | solution.py:329
  62.2 4.5 %collective-permute-start.16 = (bf16[8,2048]{1,0:T(8,128)(2,1)S(1)}, bf16[8,2048]{1,0:T(8,128)(2,1)S(1)}, u32[]{:S(2)}, u32[]{:S(2)}) collective-permute-start(bf16[8,2048]{1,0:T(8,128)(2,1)S(1)} %get-tuple-element.40), channel_id=1, source_target_pairs={{0,8},{2,10},{4,12},{6,14},{8,0},{10,2},{12,4},{14,6},{16,24},{18,... | collective-permute-start | bytes 98312 | tf_op jit(solution)/shard_map/ppermute | solution.py:329
  62.7 4.8 %collective-permute-start.17 = (bf16[8,2048]{1,0:T(8,128)(2,1)S(1)}, bf16[8,2048]{1,0:T(8,128)(2,1)S(1)}, u32[]{:S(2)}, u32[]{:S(2)}) collective-permute-start(bf16[8,2048]{1,0:T(8,128)(2,1)S(1)} %get-tuple-element.40), channel_id=1, source_target_pairs={{0,16},{2,18},{4,20},{6,22},{8,24},{10,26},{12,28},{14,30},{16,0},... | collective-permute-start | bytes 98312 | tf_op jit(solution)/shard_map/ppermute | solution.py:329
  67.5 7.6 %collective-permute-start.20 = (bf16[4,8,2048]{2,1,0:T(8,128)(2,1)S(1)}, bf16[4,8,2048]{2,1,0:T(8,128)(2,1)S(1)}, u32[]{:S(2)}, u32[]{:S(2)}) collective-permute-start(bf16[4,8,2048]{2,1,0:T(8,128)(2,1)S(1)} %pad_maximum_fusion.1.refs_0_.refs_1_), channel_id=1, source_target_pairs={{0,6},{2,4},{4,2},{6,0},{8,14},{10,12},{12,10},{14,8},{16,22},{18,... | collective-permute-start | bytes 393224 | tf_op jit(solution)/shard_map/ppermute | solution.py:329
  68.0 7.8 %collective-permute-start.19 = (bf16[4,8,2048]{2,1,0:T(8,128)(2,1)S(1)}, bf16[4,8,2048]{2,1,0:T(8,128)(2,1)S(1)}, u32[]{:S(2)}, u32[]{:S(2)}) collective-permute-start(bf16[4,8,2048]{2,1,0:T(8,128)(2,1)S(1)} %pad_maximum_fusion.1.refs_0_.refs_1_), channel_id=1, source_target_pairs={{0,4},{2,6},{4,0},{6,2},{8,12},{10,14},{12,8},{14,10},{16,20},{18,... | collective-permute-start | bytes 393224 | tf_op jit(solution)/shard_map/ppermute | solution.py:329
  70.1 6.4 %collective-permute-start.18 = (bf16[4,8,2048]{2,1,0:T(8,128)(2,1)S(1)}, bf16[4,8,2048]{2,1,0:T(8,128)(2,1)S(1)}, u32[]{:S(2)}, u32[]{:S(2)}) collective-permute-start(bf16[4,8,2048]{2,1,0:T(8,128)(2,1)S(1)} %pad_maximum_fusion.1.refs_0_.refs_1_), channel_id=1, source_target_pairs={{0,2},{2,0},{4,6},{6,4},{8,10},{10,8},{12,14},{14,12},{16,18},{18,... | collective-permute-start | bytes 393224 | tf_op jit(solution)/shard_map/ppermute | solution.py:329
  71.1 3.4 %copy-start.1 = (bf16[128,32768]{1,0:T(8,128)(2,1)S(1)}, bf16[128,32768]{1,0:T(8,128)(2,1)}, u32[]{:S(2)}) copy-start(bf16[128,32768]{1,0:T(8,128)(2,1)} %copy-done) | copy-start | bytes 25165828
  77.1 41.3 %slice-start = ((s8[8388608]{0:T(1024)(128)(4,1)}), s8[4194304]{0:T(1024)(128)(4,1)S(1)}, s32[]{:S(2)}) async-start(s8[8388608]{0:T(1024)(128)(4,1)} %bitcast.29), calls=%async_computation.3 | async-start | bytes 8388608
  78.0 5.5 %collective-permute-start.21 = (bf16[4,8,2048]{2,1,0:T(8,128)(2,1)S(1)}, bf16[4,8,2048]{2,1,0:T(8,128)(2,1)S(1)}, u32[]{:S(2)}, u32[]{:S(2)}) collective-permute-start(bf16[4,8,2048]{2,1,0:T(8,128)(2,1)S(1)} %get-tuple-element.43), channel_id=1, source_target_pairs={{0,2},{2,0},{4,6},{6,4},{8,10},{10,8},{12,14},{14,12},{16,18},{18,... | collective-permute-start | bytes 393224 | tf_op jit(solution)/shard_map/ppermute | solution.py:329
  80.6 6.4 %collective-permute-start.22 = (bf16[4,8,2048]{2,1,0:T(8,128)(2,1)S(1)}, bf16[4,8,2048]{2,1,0:T(8,128)(2,1)S(1)}, u32[]{:S(2)}, u32[]{:S(2)}) collective-permute-start(bf16[4,8,2048]{2,1,0:T(8,128)(2,1)S(1)} %get-tuple-element.44), channel_id=1, source_target_pairs={{0,4},{2,6},{4,0},{6,2},{8,12},{10,14},{12,8},{14,10},{16,20},{18,... | collective-permute-start | bytes 393224 | tf_op jit(solution)/shard_map/ppermute | solution.py:329
  80.9 6.0 %collective-permute-start.23 = (bf16[4,8,2048]{2,1,0:T(8,128)(2,1)S(1)}, bf16[4,8,2048]{2,1,0:T(8,128)(2,1)S(1)}, u32[]{:S(2)}, u32[]{:S(2)}) collective-permute-start(bf16[4,8,2048]{2,1,0:T(8,128)(2,1)S(1)} %get-tuple-element.45), channel_id=1, source_target_pairs={{0,6},{2,4},{4,2},{6,0},{8,14},{10,12},{12,10},{14,8},{16,22},{18,... | collective-permute-start | bytes 393224 | tf_op jit(solution)/shard_map/ppermute | solution.py:329
  82.1 36.3 %slice-start.1 = ((s8[8388608]{0:T(1024)(128)(4,1)}), s8[4194304]{0:T(1024)(128)(4,1)S(1)}, s32[]{:S(2)}) async-start(s8[8388608]{0:T(1024)(128)(4,1)} %bitcast.29), calls=%async_computation.4 | async-start | bytes 8388608
  87.0 6.1 %collective-permute-start.24 = (bf16[8,2048]{1,0:T(8,128)(2,1)S(1)}, bf16[8,2048]{1,0:T(8,128)(2,1)S(1)}, u32[]{:S(2)}, u32[]{:S(2)}) collective-permute-start(bf16[8,2048]{1,0:T(8,128)(2,1)S(1)} %get-tuple-element.47), channel_id=1, source_target_pairs={{0,24},{2,26},{4,28},{6,30},{8,16},{10,18},{12,20},{14,22},{16,8},... | collective-permute-start | bytes 98312 | tf_op jit(solution)/shard_map/ppermute | solution.py:329
  89.7 3.9 %collective-permute-start.25 = (bf16[8,2048]{1,0:T(8,128)(2,1)S(1)}, bf16[8,2048]{1,0:T(8,128)(2,1)S(1)}, u32[]{:S(2)}, u32[]{:S(2)}) collective-permute-start(bf16[8,2048]{1,0:T(8,128)(2,1)S(1)} %get-tuple-element.48), channel_id=1, source_target_pairs={{0,8},{2,10},{4,12},{6,14},{8,0},{10,2},{12,4},{14,6},{16,24},{18,... | collective-permute-start | bytes 98312 | tf_op jit(solution)/shard_map/ppermute | solution.py:329
  91.0 5.2 %collective-permute-start.26 = (bf16[8,2048]{1,0:T(8,128)(2,1)S(1)}, bf16[8,2048]{1,0:T(8,128)(2,1)S(1)}, u32[]{:S(2)}, u32[]{:S(2)}) collective-permute-start(bf16[8,2048]{1,0:T(8,128)(2,1)S(1)} %get-tuple-element.49), channel_id=1, source_target_pairs={{0,16},{2,18},{4,20},{6,22},{8,24},{10,26},{12,28},{14,30},{16,0},... | collective-permute-start | bytes 98312 | tf_op jit(solution)/shard_map/ppermute | solution.py:329
  108.4 5.8 %collective-permute-start.27 = (bf16[8,2048]{1,0:T(8,128)(2,1)S(1)}, bf16[8,2048]{1,0:T(8,128)(2,1)S(1)}, u32[]{:S(2)}, u32[]{:S(2)}) collective-permute-start(bf16[8,2048]{1,0:T(8,128)(2,1)S(1)} %get-tuple-element.55), channel_id=1, source_target_pairs={{0,24},{2,26},{4,28},{6,30},{8,16},{10,18},{12,20},{14,22},{16,8},... | collective-permute-start | bytes 98312 | tf_op jit(solution)/shard_map/ppermute | solution.py:329
  109.7 4.5 %collective-permute-start.28 = (bf16[8,2048]{1,0:T(8,128)(2,1)S(1)}, bf16[8,2048]{1,0:T(8,128)(2,1)S(1)}, u32[]{:S(2)}, u32[]{:S(2)}) collective-permute-start(bf16[8,2048]{1,0:T(8,128)(2,1)S(1)} %get-tuple-element.55), channel_id=1, source_target_pairs={{0,8},{2,10},{4,12},{6,14},{8,0},{10,2},{12,4},{14,6},{16,24},{18,... | collective-permute-start | bytes 98312 | tf_op jit(solution)/shard_map/ppermute | solution.py:329
  110.0 4.8 %collective-permute-start.29 = (bf16[8,2048]{1,0:T(8,128)(2,1)S(1)}, bf16[8,2048]{1,0:T(8,128)(2,1)S(1)}, u32[]{:S(2)}, u32[]{:S(2)}) collective-permute-start(bf16[8,2048]{1,0:T(8,128)(2,1)S(1)} %get-tuple-element.55), channel_id=1, source_target_pairs={{0,16},{2,18},{4,20},{6,22},{8,24},{10,26},{12,28},{14,30},{16,0},... | collective-permute-start | bytes 98312 | tf_op jit(solution)/shard_map/ppermute | solution.py:329
  114.8 6.0 %collective-permute-start.32 = (bf16[4,8,2048]{2,1,0:T(8,128)(2,1)S(1)}, bf16[4,8,2048]{2,1,0:T(8,128)(2,1)S(1)}, u32[]{:S(2)}, u32[]{:S(2)}) collective-permute-start(bf16[4,8,2048]{2,1,0:T(8,128)(2,1)S(1)} %pad_maximum_fusion.2.refs_0_), channel_id=1, source_target_pairs={{0,6},{2,4},{4,2},{6,0},{8,14},{10,12},{12,10},{14,8},{16,22},{18,... | collective-permute-start | bytes 393224 | tf_op jit(solution)/shard_map/ppermute | solution.py:329
  115.7 6.4 %collective-permute-start.31 = (bf16[4,8,2048]{2,1,0:T(8,128)(2,1)S(1)}, bf16[4,8,2048]{2,1,0:T(8,128)(2,1)S(1)}, u32[]{:S(2)}, u32[]{:S(2)}) collective-permute-start(bf16[4,8,2048]{2,1,0:T(8,128)(2,1)S(1)} %pad_maximum_fusion.2.refs_0_), channel_id=1, source_target_pairs={{0,4},{2,6},{4,0},{6,2},{8,12},{10,14},{12,8},{14,10},{16,20},{18,... | collective-permute-start | bytes 393224 | tf_op jit(solution)/shard_map/ppermute | solution.py:329
  117.3 5.4 %collective-permute-start.30 = (bf16[4,8,2048]{2,1,0:T(8,128)(2,1)S(1)}, bf16[4,8,2048]{2,1,0:T(8,128)(2,1)S(1)}, u32[]{:S(2)}, u32[]{:S(2)}) collective-permute-start(bf16[4,8,2048]{2,1,0:T(8,128)(2,1)S(1)} %pad_maximum_fusion.2.refs_0_), channel_id=1, source_target_pairs={{0,2},{2,0},{4,6},{6,4},{8,10},{10,8},{12,14},{14,12},{16,18},{18,... | collective-permute-start | bytes 393224 | tf_op jit(solution)/shard_map/ppermute | solution.py:329
  136.3 1.3 collective-permute-start.33

commit v4 on v3

--- a/solution.py
+++ b/solution.py
@@ -166,7 +166,10 @@
     return (smallest + lam) / (values + lam) - 1.0
 
 
-def gradient_body(summed_ref, weights_ref, lam_ref, sketch_ref, residual_ref, payload_ref):
+def gradient_body(
+    summed_ref, weights_ref, lam_ref, values_ref, sketch_ref, residual_ref, payload_ref
+):
+    del values_ref
     residual = -(summed_ref[...] + lam_ref[:, :1] * weights_ref[...])
     residual_ref[...] = residual
     repeat(payload_ref, exact_dot(residual, sketch_ref[...], 0).astype(jnp.bfloat16))
@@ -365,6 +368,7 @@
         width = weights.shape[1]
         mine = lax.dynamic_slice_in_dim(weights, core * count, count, 0)
         theirs = partner(lax.dynamic_slice_in_dim(weights, (1 - core) * count, count, 0))
+        theirs, design_matrix, sketch = lax.optimization_barrier((theirs, design_matrix, sketch))
         result = solve(
             [design_matrix, partner(design_matrix)],
             labels,
@@ -436,7 +440,7 @@
         for received in swap_far([folded[k].astype(jnp.float16) for k in range(1, far)]):
             summed = summed + received.astype(single)
         residual, blocks = call(
-            gradient_body, [field, payload], summed * (1.0 / scale), weights, lam, sketch
+            gradient_body, [field, payload], summed * (1.0 / scale), weights, lam, values, sketch,
         )
         direction, projected, block = call(
             first_body, [field, ((strengths, rank), single), spread],

time: 139 us -> 129 us (0.928)
  blocking collectives: 23.3 us -> 36 us
  waiting for transfers between devices: 41 us -> 30.2 us
  starting transfers between devices: 47.7 us -> 42 us
  local copies, waits for them, and re-layouts: 8.61 us -> 4.73 us
  Pallas kernels: 16.4 us -> 14.2 us
    all_to_all x2 -> x3, blocking collectives: 23.3 us -> 36 us  [exchange(): return lax.all_to_all(blocks, 'samp', 0, 0)]
    all_to_all x1 -> x0, waiting for transfers between devices: 7.94 us -> none  [exchange(): return lax.all_to_all(blocks, 'samp', 0, 0)]
    ppermute x4, waiting for transfers between devices: 7.52 us -> 2.05 us  [partner(): return lax.ppermute(values, 'feat', [(0, 1), (1, 0)])]
    all_to_all x1 -> x0, starting transfers between devices: 5.26 us -> none  [exchange(): return lax.all_to_all(blocks, 'samp', 0, 0)]
    unnamed x15 -> x7, local copies, waits for them, and re-layouts: 6.83 us -> 2.28 us
    ppermute x30, waiting for transfers between devices: 25.6 us -> 28.1 us  [swap(): lax.ppermute(values, 'samp', [(i, i ^ distance) for i in range(samp)])]
    pallas_call x1, Pallas kernels: 2.52 us -> 0.96 us  [load(): pl.pallas_call(lambda *refs: load_body(order, *refs), out_shape=pltpu.VME...]
  transfers between devices with their start and end apart: 35 -> 34, of which waited for: 22 -> 27; matrix products, arithmetic and copies ran while one was open for 2% -> 1% of each run, Pallas kernels for 8% -> 7%
where the time goes in v4:
time: 129 us; the launch traced here: 128 us
  starting transfers between devices  42 us (33%)
  blocking collectives  36 us (28%)
  waiting for transfers between devices  30.2 us (23%)
  Pallas kernels  14.2 us (11%)
  local copies, waits for them, and re-layouts  4.73 us (4%)
    ppermute x30, starting transfers between devices, swap(): lax.ppermute(values, 'samp', [(i, i ^ distance) for i in range(samp)])  41.1 us
    all_to_all x3, blocking collectives, exchange(): return lax.all_to_all(blocks, 'samp', 0, 0)  36 us
    ppermute x30, waiting for transfers between devices, swap(): lax.ppermute(values, 'samp', [(i, i ^ distance) for i in range(samp)])  28.1 us
    pallas_call x23, Pallas kernels, call(): pl.pallas_call(body, out_shape=[jax.ShapeDtypeStruct(shape, dtype) for sh...  13.2 us
  transfers between devices with their start and end apart: 34, of which 27 were waited for; matrix products, arithmetic and copies ran while one was open for 1% of the time, Pallas kernels for 7%

profile of v4, /device:TPU:0, one launch (start us, length us, event | category | flops | bytes accessed | tf_op | source)
XLA Modules:
  0.0 128.3 jit_solution(15392131924814610942)
XLA Ops:
  0.0 0.8 constant_dynamic-slice_fusion.1
  1.3 0.9 collective-permute-done
  2.5 4.7 %collective-permute-start.1 = (bf16[8,2048]{1,0:T(8,128)(2,1)S(1)}, bf16[8,2048]{1,0:T(8,128)(2,1)S(1)}, u32[]{:S(2)}, u32[]{:S(2)}) collective-permute-start(bf16[8,2048]{1,0:T(8,128)(2,1)S(1)} %fusion.4), channel_id=1, source_target_pairs={{0,24},{2,26},{4,28},{6,30},{8,16},{10,18},{12,20},{14,22},{16,8},... | collective-permute-start | bytes 98312 | tf_op jit(solution)/shard_map/ppermute | solution.py:332
  7.9 0.7 dynamic_slice.11
  9.5 2.0 %collective-permute-done.2 = bf16[8,2048]{1,0:T(8,128)(2,1)S(1)} collective-permute-done((bf16[8,2048]{1,0:T(8,128)(2,1)S(1)}, bf16[8,2048]{1,0:T(8,128)(2,1)S(1)}, u32[]{:S(2)}, u32[]{:S(2)}) %collective-permute-start.2) | collective-permute-done | bytes 32800 | tf_op jit(solution)/shard_map/ppermute | solution.py:332
  12.1 2.5 %collective-permute-start.7 = (bf16[4,8,2048]{2,1,0:T(8,128)(2,1)S(1)}, bf16[4,8,2048]{2,1,0:T(8,128)(2,1)S(1)}, u32[]{:S(2)}, u32[]{:S(2)}) collective-permute-start(bf16[4,8,2048]{2,1,0:T(8,128)(2,1)S(1)} %pad_maximum_fusion.refs_0_), channel_id=1, source_target_pairs={{0,6},{2,4},{4,2},{6,0},{8,14},{10,12},{12,10},{14,8},{16,22},{18,... | collective-permute-start | bytes 393224 | tf_op jit(solution)/shard_map/ppermute | solution.py:332
  15.7 2.2 %copy-done = bf16[128,16384]{1,0:T(8,128)(2,1)S(1)} copy-done((bf16[128,16384]{1,0:T(8,128)(2,1)S(1)}, bf16[128,16384]{1,0:T(8,128)(2,1)}, u32[]{:S(2)}) %copy-start) | copy-done | bytes 4194328
  17.8 1.0 load.1.refs_1_.refs_3_.refs_2_
  21.5 0.9 shard_map.68
  22.5 2.5 %collective-permute-start.10 = (f16[4,8,2048]{2,1,0:T(8,128)(2,1)S(1)}, f16[4,8,2048]{2,1,0:T(8,128)(2,1)S(1)}, u32[]{:S(2)}, u32[]{:S(2)}) collective-permute-start(f16[4,8,2048]{2,1,0:T(8,128)(2,1)S(1)} %convert_element_type.53), channel_id=1, source_target_pairs={{0,6},{2,4},{4,2},{6,0},{8,14},{10,12},{12,10},{14,8},{16,22},{18,... | collective-permute-start | bytes 393224 | tf_op jit(solution)/shard_map/ppermute | solution.py:332
  26.7 2.8 %collective-permute-done.10 = f16[4,8,2048]{2,1,0:T(8,128)(2,1)S(1)} collective-permute-done((f16[4,8,2048]{2,1,0:T(8,128)(2,1)S(1)}, f16[4,8,2048]{2,1,0:T(8,128)(2,1)S(1)}, u32[]{:S(2)}, u32[]{:S(2)}) %collective-permute-start.10) | collective-permute-done | bytes 131104 | tf_op jit(solution)/shard_map/ppermute | solution.py:332
  29.5 1.5 %collective-permute-done.8 = f16[4,8,2048]{2,1,0:T(8,128)(2,1)S(1)} collective-permute-done((f16[4,8,2048]{2,1,0:T(8,128)(2,1)S(1)}, f16[4,8,2048]{2,1,0:T(8,128)(2,1)S(1)}, u32[]{:S(2)}, u32[]{:S(2)}) %collective-permute-start.8) | collective-permute-done | bytes 131104 | tf_op jit(solution)/shard_map/ppermute | solution.py:332
  31.3 3.2 %collective-permute-start.11 = (f16[8,2048]{1,0:T(8,128)(2,1)S(1)}, f16[8,2048]{1,0:T(8,128)(2,1)S(1)}, u32[]{:S(2)}, u32[]{:S(2)}) collective-permute-start(f16[8,2048]{1,0:T(8,128)(2,1)S(1)} %get-tuple-element.71), channel_id=1, source_target_pairs={{0,24},{2,26},{4,28},{6,30},{8,16},{10,18},{12,20},{14,22},{16,8},... | collective-permute-start | bytes 98312 | tf_op jit(solution)/shard_map/ppermute | solution.py:332
  34.5 1.3 collective-permute-start.13
  35.9 1.2 collective-permute-done.11
  37.1 1.3 %collective-permute-done.12 = f16[8,2048]{1,0:T(8,128)(2,1)S(1)} collective-permute-done((f16[8,2048]{1,0:T(8,128)(2,1)S(1)}, f16[8,2048]{1,0:T(8,128)(2,1)S(1)}, u32[]{:S(2)}, u32[]{:S(2)}) %collective-permute-start.12) | collective-permute-done | bytes 32800 | tf_op jit(solution)/shard_map/ppermute | solution.py:332
  38.4 0.9 collective-permute-done.13
  39.8 11.8 %all_to_all.15 = bf16[16,8,384]{2,1,0:T(8,128)(2,1)S(1)} all-to-all(bf16[16,8,384]{2,1,0:T(8,128)(2,1)S(1)} %get-tuple-element.44), channel_id=1, replica_groups=mesh['samp'=16,'feat'=2] {'samp'}, dimensions={0} | all-to-all | bytes 196608 | tf_op jit(solution)/shard_map/all_to_all | solution.py:351
  52.3 1.2 collective-permute-start.15
  53.8 3.0 %collective-permute-start.17 = (bf16[8,2048]{1,0:T(8,128)(2,1)S(1)}, bf16[8,2048]{1,0:T(8,128)(2,1)S(1)}, u32[]{:S(2)}, u32[]{:S(2)}) collective-permute-start(bf16[8,2048]{1,0:T(8,128)(2,1)S(1)} %get-tuple-element.46), channel_id=1, source_target_pairs={{0,16},{2,18},{4,20},{6,22},{8,24},{10,26},{12,28},{14,30},{16,0},... | collective-permute-start | bytes 98312 | tf_op jit(solution)/shard_map/ppermute | solution.py:332
  56.8 1.3 %collective-permute-done.15 = bf16[8,2048]{1,0:T(8,128)(2,1)S(1)} collective-permute-done((bf16[8,2048]{1,0:T(8,128)(2,1)S(1)}, bf16[8,2048]{1,0:T(8,128)(2,1)S(1)}, u32[]{:S(2)}, u32[]{:S(2)}) %collective-permute-start.15) | collective-permute-done | bytes 32800 | tf_op jit(solution)/shard_map/ppermute | solution.py:332
  58.7 0.8 collective-permute-start.20
  59.4 1.7 %collective-permute-start.19 = (bf16[4,8,2048]{2,1,0:T(8,128)(2,1)S(1)}, bf16[4,8,2048]{2,1,0:T(8,128)(2,1)S(1)}, u32[]{:S(2)}, u32[]{:S(2)}) collective-permute-start(bf16[4,8,2048]{2,1,0:T(8,128)(2,1)S(1)} %pad_maximum_fusion.1.refs_0_.refs_1_), channel_id=1, source_target_pairs={{0,4},{2,6},{4,0},{6,2},{8,12},{10,14},{12,8},{14,10},{16,20},{18,... | collective-permute-start | bytes 393224 | tf_op jit(solution)/shard_map/ppermute | solution.py:332
  61.2 1.1 collective-permute-start.18
  62.9 1.8 %collective-permute-done.20.refs_0_.refs_1_ = bf16[4,8,2048]{2,1,0:T(8,128)(2,1)S(1)} collective-permute-done((bf16[4,8,2048]{2,1,0:T(8,128)(2,1)S(1)}, bf16[4,8,2048]{2,1,0:T(8,128)(2,1)S(1)}, u32[]{:S(2)}, u32[]{:S(2)}) %collective-permute-start.20) | collective-permute-done | bytes 131104 | tf_op jit(solution)/shard_map/ppermute | solution.py:332
  66.4 1.1 collective-permute-done.18.refs_0_.refs_1_
  68.1 0.9 shard_map.76
  69.1 0.8 collective-permute-start.21
  69.8 1.1 collective-permute-start.22
  70.9 1.7 %collective-permute-start.23 = (bf16[4,8,2048]{2,1,0:T(8,128)(2,1)S(1)}, bf16[4,8,2048]{2,1,0:T(8,128)(2,1)S(1)}, u32[]{:S(2)}, u32[]{:S(2)}) collective-permute-start(bf16[4,8,2048]{2,1,0:T(8,128)(2,1)S(1)} %get-tuple-element.51), channel_id=1, source_target_pairs={{0,6},{2,4},{4,2},{6,0},{8,14},{10,12},{12,10},{14,8},{16,22},{18,... | collective-permute-start | bytes 393224 | tf_op jit(solution)/shard_map/ppermute | solution.py:332
  73.0 1.1 collective-permute-done.21.refs_0_
  74.8 2.0 %collective-permute-done.23.refs_2_ = bf16[4,8,2048]{2,1,0:T(8,128)(2,1)S(1)} collective-permute-done((bf16[4,8,2048]{2,1,0:T(8,128)(2,1)S(1)}, bf16[4,8,2048]{2,1,0:T(8,128)(2,1)S(1)}, u32[]{:S(2)}, u32[]{:S(2)}) %collective-permute-start.23) | collective-permute-done | bytes 131104 | tf_op jit(solution)/shard_map/ppermute | solution.py:332
  76.8 2.4 %collective-permute-start.24 = (bf16[8,2048]{1,0:T(8,128)(2,1)S(1)}, bf16[8,2048]{1,0:T(8,128)(2,1)S(1)}, u32[]{:S(2)}, u32[]{:S(2)}) collective-permute-start(bf16[8,2048]{1,0:T(8,128)(2,1)S(1)} %get-tuple-element.53), channel_id=1, source_target_pairs={{0,24},{2,26},{4,28},{6,30},{8,16},{10,18},{12,20},{14,22},{16,8},... | collective-permute-start | bytes 98312 | tf_op jit(solution)/shard_map/ppermute | solution.py:332
  79.3 1.1 collective-permute-start.25
  80.4 0.9 collective-permute-start.26
  81.3 1.4 %collective-permute-done.24.refs_1_ = bf16[8,2048]{1,0:T(8,128)(2,1)S(1)} collective-permute-done((bf16[8,2048]{1,0:T(8,128)(2,1)S(1)}, bf16[8,2048]{1,0:T(8,128)(2,1)S(1)}, u32[]{:S(2)}, u32[]{:S(2)}) %collective-permute-start.24) | collective-permute-done | bytes 32800 | tf_op jit(solution)/shard_map/ppermute | solution.py:332
  83.4 1.9 %collective-permute-done.26.refs_3_ = bf16[8,2048]{1,0:T(8,128)(2,1)S(1)} collective-permute-done((bf16[8,2048]{1,0:T(8,128)(2,1)S(1)}, bf16[8,2048]{1,0:T(8,128)(2,1)S(1)}, u32[]{:S(2)}, u32[]{:S(2)}) %collective-permute-start.26) | collective-permute-done | bytes 32800 | tf_op jit(solution)/shard_map/ppermute | solution.py:332
  85.6 12.2 %all_to_all.16 = bf16[16,8,512]{2,1,0:T(8,128)(2,1)S(1)} all-to-all(bf16[16,8,512]{2,1,0:T(8,128)(2,1)S(1)} %get-tuple-element.58), channel_id=1, replica_groups=mesh['samp'=16,'feat'=2] {'samp'}, dimensions={0} | all-to-all | bytes 262144 | tf_op jit(solution)/shard_map/all_to_all | solution.py:351
  97.9 0.8 shard_map.80
  98.7 1.2 collective-permute-start.27
  100.3 2.9 %collective-permute-start.29 = (bf16[8,2048]{1,0:T(8,128)(2,1)S(1)}, bf16[8,2048]{1,0:T(8,128)(2,1)S(1)}, u32[]{:S(2)}, u32[]{:S(2)}) collective-permute-start(bf16[8,2048]{1,0:T(8,128)(2,1)S(1)} %get-tuple-element.61), channel_id=1, source_target_pairs={{0,16},{2,18},{4,20},{6,22},{8,24},{10,26},{12,28},{14,30},{16,0},... | collective-permute-start | bytes 98312 | tf_op jit(solution)/shard_map/ppermute | solution.py:332
  103.2 1.3 %collective-permute-done.27 = bf16[8,2048]{1,0:T(8,128)(2,1)S(1)} collective-permute-done((bf16[8,2048]{1,0:T(8,128)(2,1)S(1)}, bf16[8,2048]{1,0:T(8,128)(2,1)S(1)}, u32[]{:S(2)}, u32[]{:S(2)}) %collective-permute-start.27) | collective-permute-done | bytes 32800 | tf_op jit(solution)/shard_map/ppermute | solution.py:332
  105.1 0.9 collective-permute-start.32
  106.0 1.6 %collective-permute-start.31 = (bf16[4,8,2048]{2,1,0:T(8,128)(2,1)S(1)}, bf16[4,8,2048]{2,1,0:T(8,128)(2,1)S(1)}, u32[]{:S(2)}, u32[]{:S(2)}) collective-permute-start(bf16[4,8,2048]{2,1,0:T(8,128)(2,1)S(1)} %pad_maximum_fusion.2.refs_0_), channel_id=1, source_target_pairs={{0,4},{2,6},{4,0},{6,2},{8,12},{10,14},{12,8},{14,10},{16,20},{18,... | collective-permute-start | bytes 393224 | tf_op jit(solution)/shard_map/ppermute | solution.py:332
  107.6 1.0 collective-permute-start.30
  109.3 1.9 %collective-permute-done.32.refs_0_ = bf16[4,8,2048]{2,1,0:T(8,128)(2,1)S(1)} collective-permute-done((bf16[4,8,2048]{2,1,0:T(8,128)(2,1)S(1)}, bf16[4,8,2048]{2,1,0:T(8,128)(2,1)S(1)}, u32[]{:S(2)}, u32[]{:S(2)}) %collective-permute-start.32) | collective-permute-done | bytes 131104 | tf_op jit(solution)/shard_map/ppermute | solution.py:332
  113.8 12.1 %all_to_all.17.received_ref = f32[16,8,128]{2,1,0:T(8,128)S(1)} all-to-all(f32[16,8,128]{2,1,0:T(8,128)S(1)} %get-tuple-element.64), channel_id=1, replica_groups=mesh['samp'=16,'feat'=2] {'samp'}, dimensions={0} | all-to-all | bytes 131072 | tf_op jit(solution)/shard_map/all_to_all | solution.py:351
  126.4 1.2 collective-permute-done.33
  (79 shorter events, 21.5 us)
Async XLA Ops:
  0.8 1.4 %collective-permute-start = (f32[8,1024]{1,0:T(8,128)S(1)}, f32[8,1024]{1,0:T(8,128)S(1)}, u32[]{:S(2)}, u32[]{:S(2)}) collective-permute-start(f32[8,1024]{1,0:T(8,128)S(1)} %get-tuple-element.77), channel_id=1, source_target_pairs={{0,1},{1,0},{2,3},{3,2},{4,5},{5,4},{6,7},{7,6},{8,9},{9,8},{10,11... | collective-permute-start | bytes 98312 | tf_op jit(solution)/shard_map/ppermute | solution.py:361
  2.1 13.5 %collective-permute-start.5 = (bf16[128,16384]{1,0:T(8,128)(2,1)}, bf16[128,16384]{1,0:T(8,128)(2,1)S(1)}, u32[]{:S(2)}, u32[]{:S(2)}) collective-permute-start(bf16[128,16384]{1,0:T(8,128)(2,1)} %refs_0_), channel_id=1, source_target_pairs={{0,1},{1,0},{2,3},{3,2},{4,5},{5,4},{6,7},{7,6},{8,9},{9,8},{10,11... | collective-permute-start | bytes 12582920 | tf_op jit(solution)/shard_map/ppermute | solution.py:361
  2.5 7.0 %collective-permute-start.1 = (bf16[8,2048]{1,0:T(8,128)(2,1)S(1)}, bf16[8,2048]{1,0:T(8,128)(2,1)S(1)}, u32[]{:S(2)}, u32[]{:S(2)}) collective-permute-start(bf16[8,2048]{1,0:T(8,128)(2,1)S(1)} %fusion.4), channel_id=1, source_target_pairs={{0,24},{2,26},{4,28},{6,30},{8,16},{10,18},{12,20},{14,22},{16,8},... | collective-permute-start | bytes 98312 | tf_op jit(solution)/shard_map/ppermute | solution.py:332
  7.2 4.3 %collective-permute-start.2 = (bf16[8,2048]{1,0:T(8,128)(2,1)S(1)}, bf16[8,2048]{1,0:T(8,128)(2,1)S(1)}, u32[]{:S(2)}, u32[]{:S(2)}) collective-permute-start(bf16[8,2048]{1,0:T(8,128)(2,1)S(1)} %fusion.4), channel_id=1, source_target_pairs={{0,8},{2,10},{4,12},{6,14},{8,0},{10,2},{12,4},{14,6},{16,24},{18,... | collective-permute-start | bytes 98312 | tf_op jit(solution)/shard_map/ppermute | solution.py:332
  7.2 4.8 %collective-permute-start.3 = (bf16[8,2048]{1,0:T(8,128)(2,1)S(1)}, bf16[8,2048]{1,0:T(8,128)(2,1)S(1)}, u32[]{:S(2)}, u32[]{:S(2)}) collective-permute-start(bf16[8,2048]{1,0:T(8,128)(2,1)S(1)} %fusion.4), channel_id=1, source_target_pairs={{0,16},{2,18},{4,20},{6,22},{8,24},{10,26},{12,28},{14,30},{16,0},... | collective-permute-start | bytes 98312 | tf_op jit(solution)/shard_map/ppermute | solution.py:332
  9.3 26.5 %collective-permute-start.14 = (bf16[1024,384]{1,0:T(8,128)(2,1)}, bf16[1024,384]{1,0:T(8,128)(2,1)S(1)}, u32[]{:S(2)}, u32[]{:S(2)}) collective-permute-start(bf16[1024,384]{1,0:T(8,128)(2,1)} %param.10), channel_id=1, source_target_pairs={{0,1},{1,0},{2,3},{3,2},{4,5},{5,4},{6,7},{7,6},{8,9},{9,8},{10,11... | collective-permute-start | bytes 2359304 | tf_op jit(solution)/shard_map/ppermute | solution.py:361
  12.1 7.4 %collective-permute-start.7 = (bf16[4,8,2048]{2,1,0:T(8,128)(2,1)S(1)}, bf16[4,8,2048]{2,1,0:T(8,128)(2,1)S(1)}, u32[]{:S(2)}, u32[]{:S(2)}) collective-permute-start(bf16[4,8,2048]{2,1,0:T(8,128)(2,1)S(1)} %pad_maximum_fusion.refs_0_), channel_id=1, source_target_pairs={{0,6},{2,4},{4,2},{6,0},{8,14},{10,12},{12,10},{14,8},{16,22},{18,... | collective-permute-start | bytes 393224 | tf_op jit(solution)/shard_map/ppermute | solution.py:332
  14.6 5.6 %collective-permute-start.6 = (bf16[4,8,2048]{2,1,0:T(8,128)(2,1)S(1)}, bf16[4,8,2048]{2,1,0:T(8,128)(2,1)S(1)}, u32[]{:S(2)}, u32[]{:S(2)}) collective-permute-start(bf16[4,8,2048]{2,1,0:T(8,128)(2,1)S(1)} %pad_maximum_fusion.refs_0_), channel_id=1, source_target_pairs={{0,4},{2,6},{4,0},{6,2},{8,12},{10,14},{12,8},{14,10},{16,20},{18,... | collective-permute-start | bytes 393224 | tf_op jit(solution)/shard_map/ppermute | solution.py:332
  15.1 5.7 %collective-permute-start.4 = (bf16[4,8,2048]{2,1,0:T(8,128)(2,1)S(1)}, bf16[4,8,2048]{2,1,0:T(8,128)(2,1)S(1)}, u32[]{:S(2)}, u32[]{:S(2)}) collective-permute-start(bf16[4,8,2048]{2,1,0:T(8,128)(2,1)S(1)} %pad_maximum_fusion.refs_0_), channel_id=1, source_target_pairs={{0,2},{2,0},{4,6},{6,4},{8,10},{10,8},{12,14},{14,12},{16,18},{18,... | collective-permute-start | bytes 393224 | tf_op jit(solution)/shard_map/ppermute | solution.py:332
  15.7 2.2 %copy-start = (bf16[128,16384]{1,0:T(8,128)(2,1)S(1)}, bf16[128,16384]{1,0:T(8,128)(2,1)}, u32[]{:S(2)}) copy-start(bf16[128,16384]{1,0:T(8,128)(2,1)} %refs_0_) | copy-start | bytes 12582916
  20.8 0.7 copy-start.1
  22.5 3.8 %copy-start.2 = (bf16[1024,384]{1,0:T(8,128)(2,1)S(1)}, bf16[1024,384]{1,0:T(8,128)(2,1)}, u32[]{:S(2)}) copy-start(bf16[1024,384]{1,0:T(8,128)(2,1)} %param.10) | copy-start | bytes 2359300
  22.5 7.0 %collective-permute-start.10 = (f16[4,8,2048]{2,1,0:T(8,128)(2,1)S(1)}, f16[4,8,2048]{2,1,0:T(8,128)(2,1)S(1)}, u32[]{:S(2)}, u32[]{:S(2)}) collective-permute-start(f16[4,8,2048]{2,1,0:T(8,128)(2,1)S(1)} %convert_element_type.53), channel_id=1, source_target_pairs={{0,6},{2,4},{4,2},{6,0},{8,14},{10,12},{12,10},{14,8},{16,22},{18,... | collective-permute-start | bytes 393224 | tf_op jit(solution)/shard_map/ppermute | solution.py:332
  25.0 6.0 %collective-permute-start.8 = (f16[4,8,2048]{2,1,0:T(8,128)(2,1)S(1)}, f16[4,8,2048]{2,1,0:T(8,128)(2,1)S(1)}, u32[]{:S(2)}, u32[]{:S(2)}) collective-permute-start(f16[4,8,2048]{2,1,0:T(8,128)(2,1)S(1)} %convert_element_type.49), channel_id=1, source_target_pairs={{0,2},{2,0},{4,6},{6,4},{8,10},{10,8},{12,14},{14,12},{16,18},{18,... | collective-permute-start | bytes 393224 | tf_op jit(solution)/shard_map/ppermute | solution.py:332
  25.7 5.5 %collective-permute-start.9 = (f16[4,8,2048]{2,1,0:T(8,128)(2,1)S(1)}, f16[4,8,2048]{2,1,0:T(8,128)(2,1)S(1)}, u32[]{:S(2)}, u32[]{:S(2)}) collective-permute-start(f16[4,8,2048]{2,1,0:T(8,128)(2,1)S(1)} %convert_element_type.51), channel_id=1, source_target_pairs={{0,4},{2,6},{4,0},{6,2},{8,12},{10,14},{12,8},{14,10},{16,20},{18,... | collective-permute-start | bytes 393224 | tf_op jit(solution)/shard_map/ppermute | solution.py:332
  31.3 5.8 %collective-permute-start.11 = (f16[8,2048]{1,0:T(8,128)(2,1)S(1)}, f16[8,2048]{1,0:T(8,128)(2,1)S(1)}, u32[]{:S(2)}, u32[]{:S(2)}) collective-permute-start(f16[8,2048]{1,0:T(8,128)(2,1)S(1)} %get-tuple-element.71), channel_id=1, source_target_pairs={{0,24},{2,26},{4,28},{6,30},{8,16},{10,18},{12,20},{14,22},{16,8},... | collective-permute-start | bytes 98312 | tf_op jit(solution)/shard_map/ppermute | solution.py:332
  34.5 3.9 %collective-permute-start.12 = (f16[8,2048]{1,0:T(8,128)(2,1)S(1)}, f16[8,2048]{1,0:T(8,128)(2,1)S(1)}, u32[]{:S(2)}, u32[]{:S(2)}) collective-permute-start(f16[8,2048]{1,0:T(8,128)(2,1)S(1)} %get-tuple-element.73), channel_id=1, source_target_pairs={{0,8},{2,10},{4,12},{6,14},{8,0},{10,2},{12,4},{14,6},{16,24},{18,... | collective-permute-start | bytes 98312 | tf_op jit(solution)/shard_map/ppermute | solution.py:332
  34.5 4.8 %collective-permute-start.13 = (f16[8,2048]{1,0:T(8,128)(2,1)S(1)}, f16[8,2048]{1,0:T(8,128)(2,1)S(1)}, u32[]{:S(2)}, u32[]{:S(2)}) collective-permute-start(f16[8,2048]{1,0:T(8,128)(2,1)S(1)} %get-tuple-element.72), channel_id=1, source_target_pairs={{0,16},{2,18},{4,20},{6,22},{8,24},{10,26},{12,28},{14,30},{16,0},... | collective-permute-start | bytes 98312 | tf_op jit(solution)/shard_map/ppermute | solution.py:332
  52.3 5.8 %collective-permute-start.15 = (bf16[8,2048]{1,0:T(8,128)(2,1)S(1)}, bf16[8,2048]{1,0:T(8,128)(2,1)S(1)}, u32[]{:S(2)}, u32[]{:S(2)}) collective-permute-start(bf16[8,2048]{1,0:T(8,128)(2,1)S(1)} %get-tuple-element.46), channel_id=1, source_target_pairs={{0,24},{2,26},{4,28},{6,30},{8,16},{10,18},{12,20},{14,22},{16,8},... | collective-permute-start | bytes 98312 | tf_op jit(solution)/shard_map/ppermute | solution.py:332
  53.5 4.6 %collective-permute-start.16 = (bf16[8,2048]{1,0:T(8,128)(2,1)S(1)}, bf16[8,2048]{1,0:T(8,128)(2,1)S(1)}, u32[]{:S(2)}, u32[]{:S(2)}) collective-permute-start(bf16[8,2048]{1,0:T(8,128)(2,1)S(1)} %get-tuple-element.46), channel_id=1, source_target_pairs={{0,8},{2,10},{4,12},{6,14},{8,0},{10,2},{12,4},{14,6},{16,24},{18,... | collective-permute-start | bytes 98312 | tf_op jit(solution)/shard_map/ppermute | solution.py:332
  53.8 4.9 %collective-permute-start.17 = (bf16[8,2048]{1,0:T(8,128)(2,1)S(1)}, bf16[8,2048]{1,0:T(8,128)(2,1)S(1)}, u32[]{:S(2)}, u32[]{:S(2)}) collective-permute-start(bf16[8,2048]{1,0:T(8,128)(2,1)S(1)} %get-tuple-element.46), channel_id=1, source_target_pairs={{0,16},{2,18},{4,20},{6,22},{8,24},{10,26},{12,28},{14,30},{16,0},... | collective-permute-start | bytes 98312 | tf_op jit(solution)/shard_map/ppermute | solution.py:332
  58.7 6.0 %collective-permute-start.20 = (bf16[4,8,2048]{2,1,0:T(8,128)(2,1)S(1)}, bf16[4,8,2048]{2,1,0:T(8,128)(2,1)S(1)}, u32[]{:S(2)}, u32[]{:S(2)}) collective-permute-start(bf16[4,8,2048]{2,1,0:T(8,128)(2,1)S(1)} %pad_maximum_fusion.1.refs_0_.refs_1_), channel_id=1, source_target_pairs={{0,6},{2,4},{4,2},{6,0},{8,14},{10,12},{12,10},{14,8},{16,22},{18,... | collective-permute-start | bytes 393224 | tf_op jit(solution)/shard_map/ppermute | solution.py:332
  59.4 6.4 %collective-permute-start.19 = (bf16[4,8,2048]{2,1,0:T(8,128)(2,1)S(1)}, bf16[4,8,2048]{2,1,0:T(8,128)(2,1)S(1)}, u32[]{:S(2)}, u32[]{:S(2)}) collective-permute-start(bf16[4,8,2048]{2,1,0:T(8,128)(2,1)S(1)} %pad_maximum_fusion.1.refs_0_.refs_1_), channel_id=1, source_target_pairs={{0,4},{2,6},{4,0},{6,2},{8,12},{10,14},{12,8},{14,10},{16,20},{18,... | collective-permute-start | bytes 393224 | tf_op jit(solution)/shard_map/ppermute | solution.py:332
  61.2 6.3 %collective-permute-start.18 = (bf16[4,8,2048]{2,1,0:T(8,128)(2,1)S(1)}, bf16[4,8,2048]{2,1,0:T(8,128)(2,1)S(1)}, u32[]{:S(2)}, u32[]{:S(2)}) collective-permute-start(bf16[4,8,2048]{2,1,0:T(8,128)(2,1)S(1)} %pad_maximum_fusion.1.refs_0_.refs_1_), channel_id=1, source_target_pairs={{0,2},{2,0},{4,6},{6,4},{8,10},{10,8},{12,14},{14,12},{16,18},{18,... | collective-permute-start | bytes 393224 | tf_op jit(solution)/shard_map/ppermute | solution.py:332
  69.1 5.0 %collective-permute-start.21 = (bf16[4,8,2048]{2,1,0:T(8,128)(2,1)S(1)}, bf16[4,8,2048]{2,1,0:T(8,128)(2,1)S(1)}, u32[]{:S(2)}, u32[]{:S(2)}) collective-permute-start(bf16[4,8,2048]{2,1,0:T(8,128)(2,1)S(1)} %get-tuple-element.49), channel_id=1, source_target_pairs={{0,2},{2,0},{4,6},{6,4},{8,10},{10,8},{12,14},{14,12},{16,18},{18,... | collective-permute-start | bytes 393224 | tf_op jit(solution)/shard_map/ppermute | solution.py:332
  69.8 5.0 %collective-permute-start.22 = (bf16[4,8,2048]{2,1,0:T(8,128)(2,1)S(1)}, bf16[4,8,2048]{2,1,0:T(8,128)(2,1)S(1)}, u32[]{:S(2)}, u32[]{:S(2)}) collective-permute-start(bf16[4,8,2048]{2,1,0:T(8,128)(2,1)S(1)} %get-tuple-element.50), channel_id=1, source_target_pairs={{0,4},{2,6},{4,0},{6,2},{8,12},{10,14},{12,8},{14,10},{16,20},{18,... | collective-permute-start | bytes 393224 | tf_op jit(solution)/shard_map/ppermute | solution.py:332
  70.9 5.9 %collective-permute-start.23 = (bf16[4,8,2048]{2,1,0:T(8,128)(2,1)S(1)}, bf16[4,8,2048]{2,1,0:T(8,128)(2,1)S(1)}, u32[]{:S(2)}, u32[]{:S(2)}) collective-permute-start(bf16[4,8,2048]{2,1,0:T(8,128)(2,1)S(1)} %get-tuple-element.51), channel_id=1, source_target_pairs={{0,6},{2,4},{4,2},{6,0},{8,14},{10,12},{12,10},{14,8},{16,22},{18,... | collective-permute-start | bytes 393224 | tf_op jit(solution)/shard_map/ppermute | solution.py:332
  76.8 5.9 %collective-permute-start.24 = (bf16[8,2048]{1,0:T(8,128)(2,1)S(1)}, bf16[8,2048]{1,0:T(8,128)(2,1)S(1)}, u32[]{:S(2)}, u32[]{:S(2)}) collective-permute-start(bf16[8,2048]{1,0:T(8,128)(2,1)S(1)} %get-tuple-element.53), channel_id=1, source_target_pairs={{0,24},{2,26},{4,28},{6,30},{8,16},{10,18},{12,20},{14,22},{16,8},... | collective-permute-start | bytes 98312 | tf_op jit(solution)/shard_map/ppermute | solution.py:332
  79.3 4.1 %collective-permute-start.25 = (bf16[8,2048]{1,0:T(8,128)(2,1)S(1)}, bf16[8,2048]{1,0:T(8,128)(2,1)S(1)}, u32[]{:S(2)}, u32[]{:S(2)}) collective-permute-start(bf16[8,2048]{1,0:T(8,128)(2,1)S(1)} %get-tuple-element.54), channel_id=1, source_target_pairs={{0,8},{2,10},{4,12},{6,14},{8,0},{10,2},{12,4},{14,6},{16,24},{18,... | collective-permute-start | bytes 98312 | tf_op jit(solution)/shard_map/ppermute | solution.py:332
  80.4 4.8 %collective-permute-start.26 = (bf16[8,2048]{1,0:T(8,128)(2,1)S(1)}, bf16[8,2048]{1,0:T(8,128)(2,1)S(1)}, u32[]{:S(2)}, u32[]{:S(2)}) collective-permute-start(bf16[8,2048]{1,0:T(8,128)(2,1)S(1)} %get-tuple-element.55), channel_id=1, source_target_pairs={{0,16},{2,18},{4,20},{6,22},{8,24},{10,26},{12,28},{14,30},{16,0},... | collective-permute-start | bytes 98312 | tf_op jit(solution)/shard_map/ppermute | solution.py:332
  98.7 5.8 %collective-permute-start.27 = (bf16[8,2048]{1,0:T(8,128)(2,1)S(1)}, bf16[8,2048]{1,0:T(8,128)(2,1)S(1)}, u32[]{:S(2)}, u32[]{:S(2)}) collective-permute-start(bf16[8,2048]{1,0:T(8,128)(2,1)S(1)} %get-tuple-element.61), channel_id=1, source_target_pairs={{0,24},{2,26},{4,28},{6,30},{8,16},{10,18},{12,20},{14,22},{16,8},... | collective-permute-start | bytes 98312 | tf_op jit(solution)/shard_map/ppermute | solution.py:332
  100.0 4.6 %collective-permute-start.28 = (bf16[8,2048]{1,0:T(8,128)(2,1)S(1)}, bf16[8,2048]{1,0:T(8,128)(2,1)S(1)}, u32[]{:S(2)}, u32[]{:S(2)}) collective-permute-start(bf16[8,2048]{1,0:T(8,128)(2,1)S(1)} %get-tuple-element.61), channel_id=1, source_target_pairs={{0,8},{2,10},{4,12},{6,14},{8,0},{10,2},{12,4},{14,6},{16,24},{18,... | collective-permute-start | bytes 98312 | tf_op jit(solution)/shard_map/ppermute | solution.py:332
  100.3 4.8 %collective-permute-start.29 = (bf16[8,2048]{1,0:T(8,128)(2,1)S(1)}, bf16[8,2048]{1,0:T(8,128)(2,1)S(1)}, u32[]{:S(2)}, u32[]{:S(2)}) collective-permute-start(bf16[8,2048]{1,0:T(8,128)(2,1)S(1)} %get-tuple-element.61), channel_id=1, source_target_pairs={{0,16},{2,18},{4,20},{6,22},{8,24},{10,26},{12,28},{14,30},{16,0},... | collective-permute-start | bytes 98312 | tf_op jit(solution)/shard_map/ppermute | solution.py:332
  105.1 6.1 %collective-permute-start.32 = (bf16[4,8,2048]{2,1,0:T(8,128)(2,1)S(1)}, bf16[4,8,2048]{2,1,0:T(8,128)(2,1)S(1)}, u32[]{:S(2)}, u32[]{:S(2)}) collective-permute-start(bf16[4,8,2048]{2,1,0:T(8,128)(2,1)S(1)} %pad_maximum_fusion.2.refs_0_), channel_id=1, source_target_pairs={{0,6},{2,4},{4,2},{6,0},{8,14},{10,12},{12,10},{14,8},{16,22},{18,... | collective-permute-start | bytes 393224 | tf_op jit(solution)/shard_map/ppermute | solution.py:332
  106.0 6.5 %collective-permute-start.31 = (bf16[4,8,2048]{2,1,0:T(8,128)(2,1)S(1)}, bf16[4,8,2048]{2,1,0:T(8,128)(2,1)S(1)}, u32[]{:S(2)}, u32[]{:S(2)}) collective-permute-start(bf16[4,8,2048]{2,1,0:T(8,128)(2,1)S(1)} %pad_maximum_fusion.2.refs_0_), channel_id=1, source_target_pairs={{0,4},{2,6},{4,0},{6,2},{8,12},{10,14},{12,8},{14,10},{16,20},{18,... | collective-permute-start | bytes 393224 | tf_op jit(solution)/shard_map/ppermute | solution.py:332
  107.6 5.5 %collective-permute-start.30 = (bf16[4,8,2048]{2,1,0:T(8,128)(2,1)S(1)}, bf16[4,8,2048]{2,1,0:T(8,128)(2,1)S(1)}, u32[]{:S(2)}, u32[]{:S(2)}) collective-permute-start(bf16[4,8,2048]{2,1,0:T(8,128)(2,1)S(1)} %pad_maximum_fusion.2.refs_0_), channel_id=1, source_target_pairs={{0,2},{2,0},{4,6},{6,4},{8,10},{10,8},{12,14},{14,12},{16,18},{18,... | collective-permute-start | bytes 393224 | tf_op jit(solution)/shard_map/ppermute | solution.py:332
  126.4 1.3 collective-permute-start.33
